TPU v7x, 32 devices: a whole 2x2x4 slice. The times are simulated.
32 devices in a mesh: fsdp: 8 (over z, y), tp: 4 (over x, core).
Axes of the slice: x: 2, y: 2, z: 4, core: 2. Of those that a mesh axis runs over, the one named last changes fastest.
Arguments:
- tokens: bfloat16 [16, 1024, 768], P('fsdp', 'tp'), may hold values from -12 to 12
- segment_ids: int32 [16, 1024], P('fsdp'), may hold values from 0 to 5, never falling along the last dimension, each value on 1 to 800 neighbouring positions
- query_key_value_weight: bfloat16 [3, 768, 768], P(None, 'fsdp', 'tp'), may hold values from -0.21875 to 0.21875
- w_out: bfloat16 [768, 768], P('tp', 'fsdp'), may hold values from -0.875 to 0.875
- input_weight: bfloat16 [768, 2, 3072], P('fsdp', None, 'tp'), may hold values from -0.21875 to 0.21875
- w_down: bfloat16 [3072, 768], P('tp', 'fsdp'), may hold values from -0.109375 to 0.109375
- norm_gains: bfloat16 [2, 768], P(None, 'fsdp'), may hold values from 0.25 to 1.75
- norm_biases: bfloat16 [2, 768], P(None, 'fsdp'), may hold values from -3 to 3
- cotangent: bfloat16 [16, 1024, 768], P('fsdp', 'tp'), may hold values from -6 to 6
Outputs:
- layer_out: bfloat16 [16, 1024, 768], P('fsdp', 'tp')
- grad_tokens: bfloat16 [16, 1024, 768], P('fsdp', 'tp')
- grad_qkv: float32 [3, 768, 768], P(None, 'fsdp', 'tp')
- output_weight_gradient: float32 [768, 768], P('tp', 'fsdp')
- input_weight_gradient: float32 [768, 2, 3072], P('fsdp', None, 'tp')
- down_weight_gradient: float32 [3072, 768], P('tp', 'fsdp')
- grad_gains: float32 [2, 768], P(None, 'fsdp')
- grad_biases: float32 [2, 768], P(None, 'fsdp')
- stream_rms: float32 [4], replicated
All inputs are finite; a program needn't handle non-finite values.
Results may differ from a plain program's by a relative error of at most 0.023.
Values may be sent and summed in bfloat16 or wider, within the bound.
A program may use at most 128 MiB of HBM per device.

v0:
```python
from functools import partial

import jax
import jax.numpy as jnp
from jax import lax
from jax.sharding import PartitionSpec as P

HEADS = 12
HEAD_DIM = 64


norm_eps = 1e-05


def norm_forward(value, gain_row, bias_row):
    average = jnp.mean(value, axis=-1, keepdims=True)
    centered = value - average
    inv_std = lax.rsqrt(jnp.mean(centered * centered, axis=-1, keepdims=True) + norm_eps)
    normed = centered * inv_std
    return (normed * gain_row + bias_row, normed, inv_std)


def norm_backward(grad_val, normed, inv_std, gain_row):
    grad_norm = grad_val * gain_row
    return inv_std * (
        grad_norm
        - jnp.mean(grad_norm, axis=-1, keepdims=True)
        - normed * jnp.mean(grad_norm * normed, axis=-1, keepdims=True)
    )


def block_scores(query_blk, keys, seg_query, seg_keys, offset, slopes, head_scale):
    rows_here = query_blk.shape[0]
    raw_score = (
        jnp.einsum("qhe,khe->hqk", query_blk, keys, preferred_element_type=jnp.float32) * head_scale
    )
    query_pos = (offset + lax.iota(jnp.int32, rows_here)).astype(jnp.float32)
    key_pos = lax.iota(jnp.int32, keys.shape[0]).astype(jnp.float32)
    distance = jnp.abs(query_pos[:, None] - key_pos[None, :])
    same_doc = seg_query[:, None] == seg_keys[None, :]
    return jnp.where(same_doc[None], raw_score - slopes[:, None, None] * distance[None], -1e30)


def attend_forward(queries, keys, values, segment, slopes, head_scale, block_rows):
    context_list = []
    norm_list = []
    for offset in range(0, queries.shape[0], block_rows):
        scores = block_scores(
            queries[offset : offset + block_rows],
            keys,
            segment[offset : offset + block_rows],
            segment,
            offset,
            slopes,
            head_scale,
        )
        peak_score = jnp.max(scores, axis=-1, keepdims=True)
        expo_vals = jnp.exp(scores - peak_score)
        row_totals = jnp.sum(expo_vals, axis=-1, keepdims=True)
        probs = (expo_vals / row_totals).astype(jnp.bfloat16)
        context_list.append(
            jnp.einsum("hqk,khe->qhe", probs, values, preferred_element_type=jnp.float32).astype(
                jnp.bfloat16
            )
        )
        norm_list.append((peak_score + jnp.log(row_totals))[..., 0])
    return (jnp.concatenate(context_list, axis=0), jnp.concatenate(norm_list, axis=1))


def attend_backward(
    queries, keys, values, segment, log_norm, grad_context, slopes, head_scale, block_rows
):
    grad_keys = jnp.zeros(keys.shape, jnp.float32)
    grad_values = jnp.zeros(values.shape, jnp.float32)
    query_grads = []
    for offset in range(0, queries.shape[0], block_rows):
        query_blk = queries[offset : offset + block_rows]
        grad_blk = grad_context[offset : offset + block_rows]
        scores = block_scores(
            query_blk,
            keys,
            segment[offset : offset + block_rows],
            segment,
            offset,
            slopes,
            head_scale,
        )
        probs = jnp.exp(scores - log_norm[:, offset : offset + block_rows][..., None])
        grad_values = grad_values + jnp.einsum(
            "hqk,qhe->khe", probs.astype(jnp.bfloat16), grad_blk, preferred_element_type=jnp.float32
        )
        grad_probs = jnp.einsum(
            "qhe,khe->hqk", grad_blk, values, preferred_element_type=jnp.float32
        )
        grad_scores = (
            probs * (grad_probs - jnp.sum(probs * grad_probs, axis=-1, keepdims=True))
        ).astype(jnp.bfloat16)
        query_grads.append(
            jnp.einsum("hqk,khe->qhe", grad_scores, keys, preferred_element_type=jnp.float32)
            * head_scale
        )
        grad_keys = (
            grad_keys
            + jnp.einsum("hqk,qhe->khe", grad_scores, query_blk, preferred_element_type=jnp.float32)
            * head_scale
        )
    grad_queries = jnp.concatenate(query_grads, axis=0)
    return (
        grad_queries.astype(jnp.bfloat16),
        grad_keys.astype(jnp.bfloat16),
        grad_values.astype(jnp.bfloat16),
    )


def local(
    tokens,
    segment_ids,
    query_key_value_weight,
    w_out,
    input_weight,
    w_down,
    norm_gains,
    norm_biases,
    cotangent,
):
    gathered = (
        lax.all_gather(query_key_value_weight, "fsdp", axis=1, tiled=True),
        lax.all_gather(w_out, "fsdp", axis=1, tiled=True),
        lax.all_gather(input_weight, "fsdp", axis=0, tiled=True),
        lax.all_gather(w_down, "fsdp", axis=1, tiled=True),
        lax.all_gather(norm_gains, "fsdp", axis=1, tiled=True),
        lax.all_gather(norm_biases, "fsdp", axis=1, tiled=True),
    )
    (
        query_key_value_whole,
        output_weight_whole,
        input_weight_whole,
        down_weight_whole,
        gains_half,
        biases_half,
    ) = gathered
    gains = gains_half.astype(jnp.float32)
    biases = biases_half.astype(jnp.float32)
    seq_count, quarter, width_d = tokens.shape
    heads_here = query_key_value_whole.shape[2] // HEAD_DIM
    head_scale = HEAD_DIM ** (-0.5)
    head_ids = lax.axis_index("tp") * heads_here + lax.iota(jnp.int32, heads_here)
    slopes = jnp.exp2(-8.0 * (head_ids.astype(jnp.float32) + 1.0) / HEADS)
    input_rows_stack = lax.all_gather(tokens, "tp", axis=1, tiled=True)
    length = input_rows_stack.shape[1]
    block_rows = min(512, length)
    mixed_rows = jnp.einsum(
        "ynk,okq->oynq", input_rows_stack, query_key_value_whole, preferred_element_type=jnp.float32
    ).astype(jnp.bfloat16)
    mixed_rows = mixed_rows.reshape(3, seq_count, length, heads_here, HEAD_DIM)

    def forward_one(bundle):
        return attend_forward(
            bundle[0], bundle[1], bundle[2], bundle[3], slopes, head_scale, block_rows
        )

    attended_rows, log_norm = lax.map(
        forward_one, (mixed_rows[0], mixed_rows[1], mixed_rows[2], segment_ids)
    )
    attended_rows = attended_rows.reshape(seq_count, length, heads_here * HEAD_DIM)
    attention_partials = jnp.einsum(
        "ucf,fo->uco", attended_rows, output_weight_whole, preferred_element_type=jnp.float32
    )
    attn = lax.psum_scatter(
        attention_partials.astype(jnp.bfloat16), "tp", scatter_dimension=1, tiled=True
    ).astype(jnp.float32)
    resid_one = tokens.astype(jnp.float32) + attn
    hidden_state_first, normed_one, inv_one = norm_forward(resid_one, gains[0], biases[0])
    hidden_state_stack = lax.all_gather(
        hidden_state_first.astype(jnp.bfloat16), "tp", axis=1, tiled=True
    )
    projected_rows = jnp.einsum(
        "hki,iet->hket", hidden_state_stack, input_weight_whole, preferred_element_type=jnp.float32
    )
    gate_part = projected_rows[:, :, 0]
    up_part = projected_rows[:, :, 1]
    activated, gelu_pull = jax.vjp(partial(jax.nn.gelu, approximate=False), gate_part)
    hidden_state = (activated * up_part).astype(jnp.bfloat16)
    feedforward_partials = jnp.einsum(
        "xtu,ur->xtr", hidden_state, down_weight_whole, preferred_element_type=jnp.float32
    )
    ffn = lax.psum_scatter(
        feedforward_partials.astype(jnp.bfloat16), "tp", scatter_dimension=1, tiled=True
    ).astype(jnp.float32)
    resid_two = hidden_state_first + ffn
    layer_out, normed_two, inv_two = norm_forward(resid_two, gains[1], biases[1])
    regathered = (
        lax.all_gather(query_key_value_weight, "fsdp", axis=1, tiled=True),
        lax.all_gather(w_out, "fsdp", axis=1, tiled=True),
        lax.all_gather(input_weight, "fsdp", axis=0, tiled=True),
        lax.all_gather(w_down, "fsdp", axis=1, tiled=True),
        lax.all_gather(norm_gains, "fsdp", axis=1, tiled=True),
        lax.all_gather(norm_biases, "fsdp", axis=1, tiled=True),
    )
    (
        query_key_value_whole,
        output_weight_whole,
        input_weight_whole,
        down_weight_whole,
        gains_half,
        biases_half,
    ) = regathered
    gains = gains_half.astype(jnp.float32)
    grad_layer = cotangent.astype(jnp.float32)
    grad_two = norm_backward(grad_layer, normed_two, inv_two, gains[1])
    feedforward_gradient = lax.all_gather(grad_two.astype(jnp.bfloat16), "tp", axis=1, tiled=True)
    hidden_state_gradient = jnp.einsum(
        "oen,pn->oep", feedforward_gradient, down_weight_whole, preferred_element_type=jnp.float32
    )
    down_weight_gradient = jnp.einsum(
        "vxn,vxb->nb", hidden_state, feedforward_gradient, preferred_element_type=jnp.float32
    )
    grad_gate = gelu_pull(hidden_state_gradient * up_part)[0]
    grad_up = hidden_state_gradient * activated
    projected_gradient = jnp.stack([grad_gate, grad_up], axis=2).astype(jnp.bfloat16)
    input_weight_gradient = jnp.einsum(
        "pvr,pvaq->raq", hidden_state_stack, projected_gradient, preferred_element_type=jnp.float32
    )
    feedforward_reverse = jnp.einsum(
        "tvhw,zhw->tvz", projected_gradient, input_weight_whole, preferred_element_type=jnp.float32
    )
    grad_hidden_one = grad_two + lax.psum_scatter(
        feedforward_reverse.astype(jnp.bfloat16), "tp", scatter_dimension=1, tiled=True
    ).astype(jnp.float32)
    grad_one = norm_backward(grad_hidden_one, normed_one, inv_one, gains[0])
    attention_gradient = lax.all_gather(grad_one.astype(jnp.bfloat16), "tp", axis=1, tiled=True)
    grad_context = jnp.einsum(
        "axr,jr->axj", attention_gradient, output_weight_whole, preferred_element_type=jnp.float32
    ).astype(jnp.bfloat16)
    output_weight_gradient = jnp.einsum(
        "etr,etk->rk", attended_rows, attention_gradient, preferred_element_type=jnp.float32
    )
    grad_context = grad_context.reshape(seq_count, length, heads_here, HEAD_DIM)

    def backward_one(bundle):
        return attend_backward(
            bundle[0],
            bundle[1],
            bundle[2],
            bundle[3],
            bundle[4],
            bundle[5],
            slopes,
            head_scale,
            block_rows,
        )

    grad_queries, grad_keys, grad_values = lax.map(
        backward_one,
        (mixed_rows[0], mixed_rows[1], mixed_rows[2], segment_ids, log_norm, grad_context),
    )
    mixed_rows_gradient = jnp.stack([grad_queries, grad_keys, grad_values]).reshape(
        3, seq_count, length, heads_here * HEAD_DIM
    )
    grad_qkv = jnp.einsum(
        "mkz,ymkt->yzt", input_rows_stack, mixed_rows_gradient, preferred_element_type=jnp.float32
    )
    projection_reverse = jnp.einsum(
        "btge,bpe->tgp",
        mixed_rows_gradient,
        query_key_value_whole,
        preferred_element_type=jnp.float32,
    )
    grad_tokens = grad_one + lax.psum_scatter(
        projection_reverse.astype(jnp.bfloat16), "tp", scatter_dimension=1, tiled=True
    ).astype(jnp.float32)
    summed = (
        lax.psum_scatter(
            grad_qkv.astype(jnp.bfloat16), "fsdp", scatter_dimension=1, tiled=True
        ).astype(jnp.float32),
        lax.psum_scatter(
            output_weight_gradient.astype(jnp.bfloat16), "fsdp", scatter_dimension=1, tiled=True
        ).astype(jnp.float32),
        lax.psum_scatter(
            input_weight_gradient.astype(jnp.bfloat16), "fsdp", scatter_dimension=0, tiled=True
        ).astype(jnp.float32),
        lax.psum_scatter(
            down_weight_gradient.astype(jnp.bfloat16), "fsdp", scatter_dimension=1, tiled=True
        ).astype(jnp.float32),
    )
    gain_terms = jnp.stack(
        [
            jnp.sum(grad_hidden_one * normed_one, axis=(0, 1)),
            jnp.sum(grad_layer * normed_two, axis=(0, 1)),
        ]
    )
    bias_terms = jnp.stack(
        [jnp.sum(grad_hidden_one, axis=(0, 1)), jnp.sum(grad_layer, axis=(0, 1))]
    )
    square_terms = jnp.stack(
        [
            jnp.sum(attn * attn),
            jnp.sum(resid_one * resid_one),
            jnp.sum(ffn * ffn),
            jnp.sum(resid_two * resid_two),
        ]
    )
    gain_sum, bias_sum, square_sum = lax.psum(
        (gain_terms, bias_terms, square_terms), ("fsdp", "tp")
    )
    shard_width = width_d // lax.axis_size("fsdp")
    shard_start = lax.axis_index("fsdp") * shard_width
    grad_gains = lax.dynamic_slice_in_dim(gain_sum, shard_start, shard_width, 1)
    grad_biases = lax.dynamic_slice_in_dim(bias_sum, shard_start, shard_width, 1)
    cell_count = float(lax.axis_size("fsdp") * lax.axis_size("tp") * seq_count * quarter * width_d)
    stream_rms = jnp.sqrt(square_sum / cell_count)
    return (
        layer_out.astype(jnp.bfloat16),
        grad_tokens.astype(jnp.bfloat16),
        summed[0],
        summed[1],
        summed[2],
        summed[3],
        grad_gains,
        grad_biases,
        stream_rms,
    )


def solution(mesh):
    placed = (
        P("fsdp", "tp", None),
        P("fsdp", None),
        P(None, "fsdp", "tp"),
        P("tp", "fsdp"),
        P("fsdp", None, "tp"),
        P("tp", "fsdp"),
        P(None, "fsdp"),
        P(None, "fsdp"),
        P("fsdp", "tp", None),
    )
    return jax.shard_map(
        local,
        mesh=mesh,
        in_specs=placed,
        out_specs=(
            P("fsdp", "tp", None),
            P("fsdp", "tp", None),
            P(None, "fsdp", "tp"),
            P("tp", "fsdp"),
            P("fsdp", None, "tp"),
            P("tp", "fsdp"),
            P(None, "fsdp"),
            P(None, "fsdp"),
            P(),
        ),
        check_vma=False,
    )
```

profile of v0, /device:TPU:0, one launch (start us, length us, event | category | flops | bytes accessed | tf_op | source)
XLA Modules:
  0.0 752.7 jit_solution(8099475908191777633)
XLA Ops:
  10.7 35.1 %all_gather.37 = bf16[192,768]{0,1:T(8,128)(2,1)} all-gather(bf16[192,96]{0,1:T(8,128)(2,1)S(1)} %copy.56), channel_id=1, replica_groups=mesh['fsdp'=8,'tp'=4] {'fsdp'}, dimensions={1}, use_global_device_ids=true | all-gather | bytes 331776 | tf_op jit(solution)/shard_map/all_gather | solution.py:128
  45.9 38.8 %all_gather.35 = bf16[3,768,192]{2,0,1:T(4,128)(2,1)S(1)} all-gather(bf16[3,96,192]{2,0,1:T(4,128)(2,1)S(1)} %copy.54), channel_id=1, replica_groups=mesh['fsdp'=8,'tp'=4] {'fsdp'}, dimensions={1}, use_global_device_ids=true | all-gather | bytes 995328 | tf_op jit(solution)/shard_map/all_gather | solution.py:127
  85.9 4.6 convert_bitcast_fusion
  91.8 34.8 %while.28 = (s32[]{:T(128)}, bf16[2,1024,3,64]{1,3,2,0:T(8,128)(2,1)S(1)}, f32[2,3,1024]{2,1,0:T(4,128)S(1)}, bf16[2,1024,3,64]{1,3,2,0:T(8,128)(2,1)S(1)}, s32[...) while((s32[]{:T(128)}, ...), condition=%wide.region_5.6_spmd.clone, body=%wide.region_0.5_spmd.clone.sunk | while | flops 866060800 | bytes 62052532 | solution.py:162
  93.2 3.1 fusion.205
  96.3 5.1 fusion.206
  103.7 2.8 fusion.209
  106.5 2.8 fusion.208
  110.5 3.1 fusion.205
  113.5 5.1 fusion.206
  121.0 2.8 fusion.209
  123.7 2.8 fusion.208
  131.1 20.7 %all-gather = bf16[8,96,2]{1,2,0:T(2,128)(2,1)S(1)} all-gather(bf16[1,96,2]{1,2,0:T(2,128)(2,1)S(1)} %bitcast.430), channel_id=1, replica_groups=mesh['fsdp'=8,'tp'=4] {'fsdp'}, dimensions={0}, use_global_device_ids=true | all-gather | bytes 3456 | tf_op jit(solution)/shard_map/all_gather | solution.py:131
  151.9 16.8 %all-gather.1 = bf16[8,96,2]{1,2,0:T(2,128)(2,1)S(1)} all-gather(bf16[1,96,2]{1,2,0:T(2,128)(2,1)S(1)} %bitcast.431), channel_id=1, replica_groups=mesh['fsdp'=8,'tp'=4] {'fsdp'}, dimensions={0}, use_global_device_ids=true | all-gather | bytes 3456 | tf_op jit(solution)/shard_map/all_gather | solution.py:132
  175.0 11.6 %all-gather.13.cloned.1.call-done = bf16[768,2,768]{2,0,1:T(8,128)(2,1)} async-done(((bf16[96,2,768]{2,0,1:T(8,128)(2,1)}), bf16[768,2,768]{2,0,1:T(8,128)(2,1)}) %all-gather.13.cloned.1.call-update) | async-done | bytes 2359312 | tf_op jit(solution)/shard_map/all_gather | solution.py:129
  186.6 29.0 %all-gather.11.cloned.1.call-done = bf16[2,1024,768]{2,1,0:T(8,128)(2,1)} async-done(((bf16[2,256,768]{2,1,0:T(8,128)(2,1)}), bf16[2,1024,768]{2,1,0:T(8,128)(2,1)}) %all-gather.11.cloned.1.call-update) | async-done | bytes 3145744 | tf_op jit(solution)/shard_map/all_gather | solution.py:174
  215.6 7.8 %fusion.109 = f32[2,1024,2,768]{3,1,2,0:T(8,128)S(1)} fusion(bf16[2,1024,768]{2,1,0:T(8,128)(2,1)} %all-gather.11.cloned.1.call-done, bf16[768,2,768]{2,0,1:T(8,128)(2,1)} %all-gather.13.cloned.1.call-done), kind=kOutput, calls=%fused_computation.162 | convolution fusion | flops 4831838208 | bytes 18087936 | tf_op jit(solution)/shard_map/hki,iet->hket/dot_general | solution.py:177
  223.5 4.5 copy-done.17
  228.0 14.7 %multiply_convert_fusion.3 = (bf16[2,1024,768]{2,1,0:T(8,128)(2,1)}, f32[2,1024,768]{2,1,0:T(8,128)}) fusion(f32[2,1024,2,768]{3,1,2,0:T(8,128)S(1)} %fusion.109), kind=kLoop, calls=%fused_computation.141 | loop fusion | flops 103809024 | bytes 22020096 | tf_op jit(solution)/shard_map/convert_element_type | solution.py:183
  242.7 16.8 %all-gather.15.cloned.1.call-done = bf16[768,768]{0,1:T(8,128)(2,1)} async-done(((bf16[768,96]{0,1:T(8,128)(2,1)}), bf16[768,768]{0,1:T(8,128)(2,1)}) %all-gather.15.cloned.1.call-update) | async-done | bytes 1179664 | tf_op jit(solution)/shard_map/all_gather | solution.py:130
  259.5 6.6 convolution_convert_fusion.1
  266.3 36.2 %reduce-scatter.15.cloned.1.call-done = bf16[2,256,768]{2,1,0:T(8,128)(2,1)} async-done(((bf16[2,1024,768]{2,1,0:T(8,128)(2,1)}), bf16[2,256,768]{2,1,0:T(8,128)(2,1)}) %reduce-scatter.15.cloned.1.call-update) | async-done | bytes 786448 | tf_op jit(solution)/shard_map/reduce_scatter | solution.py:187
  302.5 2.9 fusion.154
  305.7 2.7 fusion.131
  311.5 28.6 %all-gather.17.cloned.1.call-done = bf16[2,1024,768]{2,1,0:T(8,128)(2,1)} async-done(((bf16[2,256,768]{2,1,0:T(8,128)(2,1)}), bf16[2,1024,768]{2,1,0:T(8,128)(2,1)}) %all-gather.17.cloned.1.call-update) | async-done | bytes 3145744 | tf_op jit(solution)/shard_map/all_gather | solution.py:211
  340.2 10.1 %fusion.114 = (bf16[2,1024,1,768]{3,1,0,2:T(8,128)(2,1)S(1)}, bf16[2,1024,1,768]{3,1,0,2:T(8,128)(2,1)S(1)}) fusion(f32[2,1024,768]{2,1,0:T(8,128)} %get-tuple-element.258, f32[2,1024,2,768]{3,1,2,0:T(8,128)} %copy-done.17, bf16[2,1024,768]{2,1,0:T(8,128)(2,1)} %all-gather.17.cloned.1.call-done, bf16[768,768]{0,1:T(8,128)(2,1)} %all-gather.15.cloned.1.call-done), kind=kOutput, calls=%fused_computation.167 | convolution fusion | flops 2444230656 | bytes 29491200 | tf_op jit(solution)/shard_map/oen,pn->oep/dot_general | solution.py:212
  352.9 6.5 bitcast_convert_fusion.1
  359.5 38.1 %reduce-scatter.17.cloned.1.call-done = bf16[2,256,768]{2,1,0:T(8,128)(2,1)} async-done(((bf16[2,1024,768]{2,1,0:T(8,128)(2,1)}), bf16[2,256,768]{2,1,0:T(8,128)(2,1)}) %reduce-scatter.17.cloned.1.call-update) | async-done | bytes 786448 | tf_op jit(solution)/shard_map/reduce_scatter | solution.py:227
  397.5 4.6 multiply_reduce_fusion.4
  404.9 6.6 bitcast_convert_fusion.3
  411.6 10.0 %bitcast_convert_fusion.2 = bf16[768,2,768]{2,0,1:T(8,128)(2,1)} fusion(bf16[2,1024,1,768]{3,1,0,2:T(8,128)(2,1)} %copy-done.59, bf16[2,1024,1,768]{3,1,0,2:T(8,128)(2,1)} %copy-done.58, bf16[2,1024,768]{2,1,0:T(8,128)(2,1)} %all-gather.11.cloned.1.call-done), kind=kOutput, calls=%fused_computation.156 | convolution fusion | flops 4845600768 | bytes 11796480 | tf_op jit(solution)/shard_map/pvr,pvaq->raq/dot_general | solution.py:221
  421.7 11.7 %all-gather.19.cloned.1.call-done = bf16[2,1024,768]{2,1,0:T(8,128)(2,1)} async-done(((bf16[2,256,768]{2,1,0:T(8,128)(2,1)}), bf16[2,1024,768]{2,1,0:T(8,128)(2,1)}) %all-gather.19.cloned.1.call-update) | async-done | bytes 3145744 | tf_op jit(solution)/shard_map/all_gather | solution.py:231
  437.0 3.1 convolution_convert_fusion.2
  443.1 64.6 %while.29 = (s32[]{:T(128)}, bf16[2,1024,3,64]{1,3,2,0:T(8,128)(2,1)}, bf16[2,1024,3,64]{1,3,2,0:T(8,128)(2,1)}, bf16[2,1024,3,64]{1,3,2,0:T(8,128)(2,1)}, bf16[...) while((s32[]{:T(128)}, ...), condition=%wide.region_20.21_spmd.clone, body=%wide.region_17.20_spmd.clone.sunk | while | flops 2053176832 | bytes 210595136 | solution.py:253
  448.7 4.1 multiply_reduce_fusion.12
  460.1 4.1 multiply_reduce_fusion.11
  466.6 2.9 fusion.228
  480.8 4.1 multiply_reduce_fusion.12
  492.2 4.1 multiply_reduce_fusion.11
  498.7 2.8 fusion.228
  507.7 5.5 fusion.135
  518.2 6.0 bitcast_convert_fusion
  526.9 46.2 %reduce-scatter.21.cloned.1.call-done = bf16[96,2,768]{2,0,1:T(8,128)(2,1)} async-done(((bf16[768,2,768]{2,0,1:T(8,128)(2,1)}), bf16[96,2,768]{2,0,1:T(8,128)(2,1)}) %reduce-scatter.21.cloned.1.call-update) | async-done | bytes 294928 | tf_op jit(solution)/shard_map/reduce_scatter | solution.py:279
  577.8 40.0 %all-reduce = (f32[2,768]{1,0:T(2,128)S(1)}, f32[2,768]{1,0:T(2,128)S(1)}, f32[4]{0:T(128)S(1)}) all-reduce(f32[2,768]{1,0:T(2,128)S(1)} %pad_maximum_fusion.10, f32[2,768]{1,0:T(2,128)S(1)} %pad_maximum_fusion.11, f32[4]{0:T(128)S(1)} %pad_maximum_fusion.12), channel_id=1, replica_groups=mesh['fsdp'=8,'tp'=4] {'fsdp','tp'}, use_global_device_ids=true, to_apply=%region_28.29 | all-reduce | flops 3076 | bytes 24608 | tf_op jit(solution)/shard_map/psum | solution.py:303
  619.5 17.7 %reduce-scatter.27.cloned.1.call-done = bf16[96,192]{1,0:T(8,128)(2,1)} async-done(((bf16[768,192]{1,0:T(8,128)(2,1)}), bf16[96,192]{1,0:T(8,128)(2,1)}) %reduce-scatter.27.cloned.1.call-update) | async-done | bytes 36880
  638.8 64.4 %reduce-scatter.25.cloned.1.call-done = bf16[96,576]{1,0:T(8,128)(2,1)} async-done(((bf16[768,576]{1,0:T(8,128)(2,1)}), bf16[96,576]{1,0:T(8,128)(2,1)}) %reduce-scatter.25.cloned.1.call-update) | async-done | bytes 110608
  705.3 37.3 %reduce-scatter.19.cloned.1.call-done = bf16[2,256,768]{2,1,0:T(8,128)(2,1)} async-done(((bf16[2,1024,768]{2,1,0:T(8,128)(2,1)}), bf16[2,256,768]{2,1,0:T(8,128)(2,1)}) %reduce-scatter.19.cloned.1.call-update) | async-done | bytes 786448 | tf_op jit(solution)/shard_map/reduce_scatter | solution.py:269
  742.7 2.7 add_convert_fusion.2
  (308 shorter events, 97.7 us)
Async XLA Ops:
  8.0 76.7 %all-gather.9.cloned.1.call-start = ((), (), s32[]{:S(2)}) async-start(), calls=%async_computation.8 | async-start | bytes 3932160 | tf_op jit(solution)/shard_map/all_gather | solution.py:149
  8.7 161.2 %reduce-scatter.13.cloned.1.call-start = ((), (), s32[]{:S(2)}) async-start(), calls=%async_computation.9 | async-start | bytes 3932160 | tf_op jit(solution)/shard_map/reduce_scatter | solution.py:169
  91.8 35.7 %copy-start.18 = (bf16[192,768]{0,1:T(8,128)(2,1)S(1)}, bf16[192,768]{0,1:T(8,128)(2,1)}, u32[]{:S(2)}) copy-start(bf16[192,768]{0,1:T(8,128)(2,1)} %all_gather.37) | copy-start | bytes 884740
  126.6 3.6 copy-start.19
  127.4 3.6 copy-start.55
  127.4 24.4 %copy-start.56 = (bf16[2,96]{1,0:T(2,128)(2,1)S(1)}, bf16[2,96]{1,0:T(2,128)(2,1)}, u32[]{:S(2)}) copy-start(bf16[2,96]{1,0:T(2,128)(2,1)} %param.20) | copy-start | bytes 1156
  130.1 39.8 %copy-start.6 = (bf16[2,256,768]{2,1,0:T(8,128)(2,1)S(1)}, bf16[2,256,768]{2,1,0:T(8,128)(2,1)}, u32[]{:S(2)}) copy-start(bf16[2,256,768]{2,1,0:T(8,128)(2,1)} %param.13) | copy-start | bytes 2359300
  130.2 56.4 %all-gather.13.cloned.1.call-start = ((), (), s32[]{:S(2)}) async-start(), calls=%async_computation.11 | async-start | bytes 2654208 | tf_op jit(solution)/shard_map/all_gather | solution.py:129
  131.0 84.6 %all-gather.11.cloned.1.call-start = ((), (), s32[]{:S(2)}) async-start(), calls=%async_computation.10 | async-start | bytes 3932160 | tf_op jit(solution)/shard_map/all_gather | solution.py:174
  169.3 232.8 %copy-start.35 = (f32[768]{0:T(1024)}, f32[768]{0:T(1024)S(1)}, u32[]{:S(2)}) copy-start(f32[768]{0:T(1024)S(1)} %get-tuple-element.210) | copy-start | bytes 9220
  169.9 4.4 copy-start.43
  171.5 230.7 %copy-start.37 = (f32[2,256]{1,0:T(2,128)}, f32[2,256]{1,0:T(2,128)S(1)}, u32[]{:S(2)}) copy-start(f32[2,256]{1,0:T(2,128)S(1)} %broadcast_multiply_fusion.5) | copy-start | bytes 6148
  173.0 50.4 %copy-start.39 = (f32[2,256]{1,0:T(2,128)}, f32[2,256]{1,0:T(2,128)S(1)}, u32[]{:S(2)}) copy-start(f32[2,256]{1,0:T(2,128)S(1)} %add_rsqrt_fusion.1) | copy-start | bytes 6148
  174.4 85.1 %all-gather.15.cloned.1.call-start = ((), (), s32[]{:S(2)}) async-start(), calls=%async_computation.12 | async-start | bytes 1327104 | tf_op jit(solution)/shard_map/all_gather | solution.py:130
  175.0 127.5 %reduce-scatter.15.cloned.1.call-start = ((), (), s32[]{:S(2)}) async-start(), calls=%async_computation.13 | async-start | bytes 3932160 | tf_op jit(solution)/shard_map/reduce_scatter | solution.py:187
  223.5 4.5 copy-start.17
  266.1 74.1 %all-gather.17.cloned.1.call-start = ((), (), s32[]{:S(2)}) async-start(), calls=%async_computation.14 | async-start | bytes 3932160 | tf_op jit(solution)/shard_map/all_gather | solution.py:211
  311.5 86.0 %reduce-scatter.17.cloned.1.call-start = ((), (), s32[]{:S(2)}) async-start(), calls=%async_computation.15 | async-start | bytes 3932160 | tf_op jit(solution)/shard_map/reduce_scatter | solution.py:227
  340.2 12.7 %copy-start.57 = (bf16[768,2,768]{2,0,1:T(8,128)(2,1)S(1)}, bf16[768,2,768]{2,0,1:T(8,128)(2,1)}, u32[]{:S(2)}) copy-start(bf16[768,2,768]{2,0,1:T(8,128)(2,1)} %all-gather.13.cloned.1.call-done) | copy-start | bytes 7077892
  359.4 74.0 %all-gather.19.cloned.1.call-start = ((), (), s32[]{:S(2)}) async-start(), calls=%async_computation.16 | async-start | bytes 3932160 | tf_op jit(solution)/shard_map/all_gather | solution.py:231
  397.5 5.8 copy-start.9
  397.5 5.8 copy-start.40
  402.2 9.4 %copy-start.45 = (f32[2,256]{1,0:T(2,128)}, f32[2,256]{1,0:T(2,128)S(1)}, u32[]{:S(2)}) copy-start(f32[2,256]{1,0:T(2,128)S(1)} %broadcast_multiply_fusion) | copy-start | bytes 6148
  402.2 9.3 %copy-start.47 = (f32[2,256]{1,0:T(2,128)}, f32[2,256]{1,0:T(2,128)S(1)}, u32[]{:S(2)}) copy-start(f32[2,256]{1,0:T(2,128)S(1)} %broadcast_multiply_fusion.1) | copy-start | bytes 6148
  404.9 120.0 %reduce-scatter.23.cloned.1.call-start = ((), (), s32[]{:S(2)}) async-start(), calls=%async_computation.19 | async-start | bytes 1327104 | tf_op jit(solution)/shard_map/reduce_scatter | solution.py:282
  411.5 21.8 %copy-start.20 = (bf16[2,1024,3,64]{1,3,2,0:T(8,128)(2,1)S(1)}, bf16[2,1024,3,64]{1,3,2,0:T(8,128)(2,1)}, u32[]{:S(2)}) copy-start(bf16[2,1024,3,64]{1,3,2,0:T(8,128)(2,1)} %copy-done.19) | copy-start | bytes 2359300
  411.6 161.5 %reduce-scatter.21.cloned.1.call-start = ((), (), s32[]{:S(2)}) async-start(), calls=%async_computation.18 | async-start | bytes 2654208 | tf_op jit(solution)/shard_map/reduce_scatter | solution.py:279
  421.6 215.6 %reduce-scatter.27.cloned.1.call-start = ((), (), s32[]{:S(2)}) async-start(), calls=%async_computation.21 | async-start | bytes 442368
  437.0 266.2 %reduce-scatter.25.cloned.1.call-start = ((), (), s32[]{:S(2)}) async-start(), calls=%async_computation.20 | async-start | bytes 1105920
  443.5 3.5 copy-start.3
  443.5 3.5 copy-start.13
  466.6 4.0 copy-start.1
  469.5 3.7 slice-start
  498.7 4.0 copy-start.1
  501.5 3.7 slice-start
  513.2 5.0 copy-start.22
  518.1 224.5 %reduce-scatter.19.cloned.1.call-start = ((), (), s32[]{:S(2)}) async-start(), calls=%async_computation.17 | async-start | bytes 3932160 | tf_op jit(solution)/shard_map/reduce_scatter | solution.py:269
  518.2 6.1 copy-start.54
  524.2 51.0 %copy-start.52 = (f32[768]{0:T(1024)S(1)}, f32[768]{0:T(1024)}, u32[]{:S(2)}) copy-start(f32[768]{0:T(1024)} %get-tuple-element.204) | copy-start | bytes 9220
  524.2 51.0 %copy-start.51 = (f32[768]{0:T(1024)S(1)}, f32[768]{0:T(1024)}, u32[]{:S(2)}) copy-start(f32[768]{0:T(1024)} %get-tuple-element.198) | copy-start | bytes 9220
  524.2 218.4 %copy-start.7 = (bf16[2,256,768]{2,1,0:T(8,128)(2,1)S(1)}, bf16[2,256,768]{2,1,0:T(8,128)(2,1)}, u32[]{:S(2)}) copy-start(bf16[2,256,768]{2,1,0:T(8,128)(2,1)} %param.13) | copy-start | bytes 2359300
  524.2 218.4 %copy-start.10 = (bf16[2,256,768]{2,1,0:T(8,128)(2,1)S(1)}, bf16[2,256,768]{2,1,0:T(8,128)(2,1)}, u32[]{:S(2)}) copy-start(bf16[2,256,768]{2,1,0:T(8,128)(2,1)} %reduce-scatter.13.cloned.1.call-done) | copy-start | bytes 2359300
  524.2 218.4 %copy-start.16 = (f32[2,256,768]{2,1,0:T(8,128)S(1)}, f32[2,256,768]{2,1,0:T(8,128)}, u32[]{:S(2)}) copy-start(f32[2,256,768]{2,1,0:T(8,128)} %copy-done.15) | copy-start | bytes 4718596
  524.2 218.4 %copy-start.36 = (f32[768]{0:T(1024)S(1)}, f32[768]{0:T(1024)}, u32[]{:S(2)}) copy-start(f32[768]{0:T(1024)} %copy-done.35) | copy-start | bytes 9220
  524.2 218.4 %copy-start.38 = (f32[2,256]{1,0:T(2,128)S(1)}, f32[2,256]{1,0:T(2,128)}, u32[]{:S(2)}) copy-start(f32[2,256]{1,0:T(2,128)} %copy-done.37) | copy-start | bytes 6148
  524.2 218.4 %copy-start.41 = (f32[2,256]{1,0:T(2,128)S(1)}, f32[2,256]{1,0:T(2,128)}, u32[]{:S(2)}) copy-start(f32[2,256]{1,0:T(2,128)} %copy-done.39) | copy-start | bytes 6148
  524.2 218.4 %copy-start.46 = (f32[2,256]{1,0:T(2,128)S(1)}, f32[2,256]{1,0:T(2,128)}, u32[]{:S(2)}) copy-start(f32[2,256]{1,0:T(2,128)} %copy-done.45) | copy-start | bytes 6148
  524.3 218.4 %copy-start.48 = (f32[2,256]{1,0:T(2,128)S(1)}, f32[2,256]{1,0:T(2,128)}, u32[]{:S(2)}) copy-start(f32[2,256]{1,0:T(2,128)} %copy-done.47) | copy-start | bytes 6148
  (48 other events, 96.2 us)
Sparse Core Ops, SparseCore 0:
  10.4 31.2 all-gather.8
  130.3 39.1 reduce-scatter.12
  311.6 28.5 all-gather.16
  359.5 37.9 reduce-scatter.16
Sparse Core Ops, SparseCore 1:
  133.6 52.9 all-gather.12
  188.7 26.9 all-gather.10
  217.9 41.5 all-gather.14
  266.2 36.3 reduce-scatter.14
  405.0 28.3 all-gather.18
  437.1 64.2 reduce-scatter.22
  505.2 67.9 reduce-scatter.20
  576.6 60.6 reduce-scatter.26
  640.8 62.4 reduce-scatter.24
  705.8 36.8 reduce-scatter.18
where the time goes:
time: 757 us; the launch traced here: 753 us
  waiting for transfers between devices  339 us (45%)
  blocking collectives  151 us (20%)
  matrix products  142 us (19%)
  other arithmetic  58.3 us (8%)
  local copies, waits for them, and re-layouts  43.7 us (6%)
  between operations  16 us (2%)
    unnamed x16, waiting for transfers between devices  83.5 us
    reduce_scatter x1, waiting for transfers between devices, local(): lax.psum_scatter(input_weight_gradient.astype(jnp.bfloat16), 'fsdp', scat...  46.2 us
    psum x1, blocking collectives, local(): lax.psum((gain_terms, bias_terms, square_terms), ('fsdp', 'tp'))  40 us
    all_gather x1, blocking collectives, local(): lax.all_gather(query_key_value_weight, 'fsdp', axis=1, tiled=True)  38.8 us
    reduce_scatter x1, waiting for transfers between devices, local(): lax.psum_scatter(feedforward_reverse.astype(jnp.bfloat16), 'tp', scatter_...  38.1 us
    reduce_scatter x1, waiting for transfers between devices, local(): lax.psum_scatter(projection_reverse.astype(jnp.bfloat16), 'tp', scatter_d...  37.3 us
    reduce_scatter x1, waiting for transfers between devices, local(): lax.psum_scatter(feedforward_partials.astype(jnp.bfloat16), 'tp', scatter...  36.2 us
    all_gather x1, blocking collectives, local(): lax.all_gather(w_out, 'fsdp', axis=1, tiled=True)  35.1 us
  transfers between devices with their start and end apart: 14, of which 11 were waited for; matrix products, arithmetic and copies ran while one was open for 19% of the time, Pallas kernels for 0%

commit v1 on v0

v1 whole, which is shorter than its diff:
```python
from functools import partial

import jax
import jax.numpy as jnp
from jax import lax
from jax.experimental import pallas as pl
from jax.experimental.pallas import tpu as pltpu
from jax.sharding import PartitionSpec as P

HEADS = 12
HEAD_DIM = 64
MESH = pl.DeviceIdType.MESH
VMEM_LIMIT = 63 << 20
norm_eps = 1e-05
SIZE = {"x": 2, "y": 2, "z": 4}
PORTIONS = ((0, 16, "yzx"), (16, 16, "xzy"), (32, 32, "zxy"), (64, 32, "zyx"))


class Place:
    def __init__(self, span):
        index = lax.axis_index("fsdp")
        shard = lax.axis_index("tp")
        self.span = span
        self.j = index % span
        block = index // span
        self.z = block // 2
        self.y = block % 2
        self.x = shard // 2
        self.k = shard % 2

    def shifted(self, dx=0, dy=0, dz=0, dk=0):
        x = 1 - self.x if dx else self.x
        y = 1 - self.y if dy else self.y
        z = (self.z + dz) % 4 if dz else self.z
        k = 1 - self.k if dk else self.k
        return x, y, z, k

    def device(self, dx=0, dy=0, dz=0, dk=0):
        x, y, z, k = self.shifted(dx, dy, dz, dk)
        return ((z * 2 + y) * self.span + self.j, x * 2 + k)

    def greet(self, offsets):
        barrier = pltpu.get_barrier_semaphore()
        for offset in offsets:
            pl.semaphore_signal(
                barrier, inc=1, device_id=self.device(**offset), device_id_type=MESH
            )
        pl.semaphore_wait(barrier, len(offsets))


ALL_PEERS = ({"dx": 1}, {"dy": 1}, {"dz": 1}, {"dz": 2}, {"dz": 3}, {"dk": 1})
PARTNER = ({"dk": 1},)


def offsets_of(order):
    found = []
    for dx in range(2):
        for dy in range(2):
            for dz in range(4):
                off = {"x": dx, "y": dy, "z": dz}
                stage = max([i + 1 for i, axis in enumerate(order) if off[axis]] or [0])
                found.append((stage, dz, dy, dx))
    return sorted(found)


def remote(src, dst, send, recv, device):
    return pltpu.make_async_remote_copy(
        src_ref=src, dst_ref=dst, send_sem=send, recv_sem=recv, device_id=device, device_id_type=MESH
    )


class Gather:
    def __init__(self, place, own, out, portions, sems):
        self.place, self.own, self.out, self.portions, self.sems = place, own, out, portions, sems

    def slot(self, dx, dy, dz, start, rows, dk=0):
        x, y, z, k = self.place.shifted(dx, dy, dz, dk)
        return self.out.at[x, k, z, y, pl.ds(start, rows), :]

    def index(self, dx, dy, dz):
        return (dx * 2 + dy) * 4 + dz

    def forward(self, number, stage, dx, dy, dz):
        start, rows, order = self.portions[number]
        send, recv = self.sems[2 * number], self.sems[2 * number + 1]
        place = self.place
        own = dx == 0 and dy == 0 and dz == 0
        src = self.own.at[pl.ds(start, rows), :] if own else self.slot(dx, dy, dz, start, rows)
        dst = self.slot(dx, dy, dz, start, rows)
        copies = []
        for later in range(stage, 3):
            axis = order[later]
            for step in range(1, SIZE[axis]):
                seen = {"x": dx, "y": dy, "z": dz}
                seen[axis] = step if axis != "z" else (4 - step)
                where = self.index(seen["x"], seen["y"], seen["z"])
                to = place.device(**{"d" + axis: step})
                copies.append(remote(src, dst, send.at[where], recv.at[where], to))
        where = 16 + self.index(dx, dy, dz)
        copies.append(remote(src, dst, send.at[where], recv.at[where], place.device(dk=1)))
        for copy in copies:
            copy.start()
        return copies

    def arrive(self, number, dx, dy, dz, dk=0):
        start, rows, order = self.portions[number]
        send, recv = self.sems[2 * number], self.sems[2 * number + 1]
        where = self.index(dx, dy, dz) + (16 if dk else 0)
        ref = self.slot(dx, dy, dz, start, rows, dk)
        remote(ref, ref, send.at[where], recv.at[where], self.place.device(dk=1)).wait_recv()

    def begin(self):
        self.started = []
        for number in range(len(self.portions)):
            self.started += self.forward(number, 0, 0, 0, 0)

    def relay(self, stage):
        for number, (start, rows, order) in enumerate(self.portions):
            for at, dz, dy, dx in offsets_of(order):
                if at == stage:
                    self.arrive(number, dx, dy, dz)
                    self.started += self.forward(number, stage, dx, dy, dz)

    def finish(self):
        for number, (start, rows, order) in enumerate(self.portions):
            for at, dz, dy, dx in offsets_of(order):
                self.arrive(number, dx, dy, dz, 1)
        for copy in self.started:
            copy.wait_send()


def gather_sems(portions):
    return [pltpu.SemaphoreType.DMA((32,)) for _ in portions for _ in range(2)]


def gather_kernel(span, wa, wf, ws, tok, cot, ga, gf, gs, xs, cs, *scratch):
    place = Place(span)
    sems_a, sems_f, sems_s = scratch[0:8], scratch[8:16], scratch[16:18]
    local_sems, send, recv = scratch[18:21]
    place.greet(ALL_PEERS)
    other = 1 - place.x
    peer = place.device(dx=1)
    swaps = []
    for n, (src, dst) in enumerate(((tok, xs), (cot, cs))):
        swaps.append(remote(src.at[other], dst.at[place.x], send.at[n], recv.at[n], peer))
    gathers = [
        Gather(place, ws, gs, ((0, 16, "zyx"),), sems_s),
        Gather(place, wa, ga, PORTIONS, sems_a),
        Gather(place, wf, gf, PORTIONS, sems_f),
    ]
    swaps[0].start()
    for gather in gathers:
        gather.begin()
    x, y, z, k = place.shifted()
    locals_ = [
        pltpu.make_async_copy(src, dst, local_sems.at[n])
        for n, (src, dst) in enumerate(
            (
                (wa, ga.at[x, k, z, y]),
                (wf, gf.at[x, k, z, y]),
                (ws, gs.at[x, k, z, y]),
                (tok.at[x], xs.at[x]),
                (cot.at[x], cs.at[x]),
            )
        )
    ]
    for copy in locals_:
        copy.start()
    for gather in gathers:
        for stage in (1, 2, 3):
            gather.relay(stage)
    swaps[1].start()
    for gather in gathers:
        gather.finish()
    for copy in locals_:
        copy.wait()
    for n, copy in enumerate(swaps):
        copy.wait()


def gather_all(span, wa, wf, ws, tok, cot):
    any_space = pl.BlockSpec(memory_space=pl.ANY)
    vmem = pl.BlockSpec(memory_space=pltpu.VMEM)
    shape = lambda a: jax.ShapeDtypeStruct((2, 2, 4, 2) + a.shape, a.dtype)
    return pl.pallas_call(
        partial(gather_kernel, span),
        out_shape=(
            shape(wa),
            shape(wf),
            shape(ws),
            jax.ShapeDtypeStruct(tok.shape, tok.dtype),
            jax.ShapeDtypeStruct(cot.shape, cot.dtype),
        ),
        in_specs=[vmem] * 5,
        out_specs=(any_space,) * 5,
        scratch_shapes=gather_sems(PORTIONS)
        + gather_sems(PORTIONS)
        + gather_sems((0,))
        + [
            pltpu.SemaphoreType.DMA((5,)),
            pltpu.SemaphoreType.DMA((2,)),
            pltpu.SemaphoreType.DMA((2,)),
        ],
        compiler_params=pltpu.CompilerParams(
            collective_id=0, has_side_effects=True, vmem_limit_bytes=VMEM_LIMIT
        ),
        name="gather_weights",
    )(wa, wf, ws, tok, cot)


def keys_kernel(span, kv, out, local_sem, send, recv):
    place = Place(span)
    place.greet(PARTNER)
    push = remote(kv, out.at[:, place.k], send, recv, place.device(dk=1))
    push.start()
    keep = pltpu.make_async_copy(kv, out.at[:, place.k], local_sem)
    keep.start()
    keep.wait()
    push.wait()


def share_keys(span, kv):
    return pl.pallas_call(
        partial(keys_kernel, span),
        out_shape=jax.ShapeDtypeStruct((2, 2) + kv.shape[1:], kv.dtype),
        in_specs=[pl.BlockSpec(memory_space=pltpu.VMEM)],
        out_specs=pl.BlockSpec(memory_space=pltpu.VMEM),
        scratch_shapes=[pltpu.SemaphoreType.DMA] * 3,
        compiler_params=pltpu.CompilerParams(
            collective_id=1, has_side_effects=True, vmem_limit_bytes=VMEM_LIMIT
        ),
        name="share_keys",
    )(kv)


def key_grads_kernel(span, part, out, held, send, recv):
    place = Place(span)
    place.greet(PARTNER)
    push = remote(part.at[:, 1 - place.k], held, send, recv, place.device(dk=1))
    push.start()
    push.wait()
    out[...] = (
        part[:, place.k].astype(jnp.float32) + held[...].astype(jnp.float32)
    ).astype(jnp.bfloat16)


def share_key_grads(span, part):
    shape = part.shape[:1] + part.shape[2:]
    return pl.pallas_call(
        partial(key_grads_kernel, span),
        out_shape=jax.ShapeDtypeStruct(shape, part.dtype),
        in_specs=[pl.BlockSpec(memory_space=pltpu.VMEM)],
        out_specs=pl.BlockSpec(memory_space=pltpu.VMEM),
        scratch_shapes=[pltpu.VMEM(shape, part.dtype)] + [pltpu.SemaphoreType.DMA] * 2,
        compiler_params=pltpu.CompilerParams(
            collective_id=2, has_side_effects=True, vmem_limit_bytes=VMEM_LIMIT
        ),
        name="share_key_grads",
    )(part)


class Scatter:
    def __init__(self, place, part, held, twin, landing, portions, sems, pair_sems):
        self.place, self.part, self.held, self.twin = place, part, held, twin
        self.landing, self.portions, self.sems, self.pair_sems = landing, portions, sems, pair_sems
        self.started = []

    def units(self):
        return [(dx, dz, dy) for dz in (2, 1, 3, 0) for dx in (1, 0) for dy in (1, 0)]

    def begin(self):
        self.loads = {}
        for n, (dx, dz, dy) in enumerate(self.units()):
            x, y, z, k = self.place.shifted(dx, dy, dz)
            load = pltpu.make_async_copy(
                self.part.at[x, k, z, y], self.held.at[dx, dz, dy], self.pair_sems[0].at[n]
            )
            push = remote(
                self.part.at[x, 1 - k, z, y],
                self.twin.at[dx, dz, dy],
                self.pair_sems[1].at[n],
                self.pair_sems[2].at[n],
                self.place.device(dk=1),
            )
            load.start()
            push.start()
            self.loads[dx, dz, dy] = (load, push)

    def hops(self, order):
        found = []
        done = []
        for stage, axis in enumerate(reversed(order)):
            rest = [a for a in "xyz" if a != axis and a not in done]
            for step in range(1, SIZE[axis]):
                for first in range(SIZE[rest[0]] if rest else 1):
                    for second in range(SIZE[rest[1]] if len(rest) > 1 else 1):
                        off = {"x": 0, "y": 0, "z": 0}
                        if rest:
                            off[rest[0]] = first
                        if len(rest) > 1:
                            off[rest[1]] = second
                        base = (off["x"], off["z"], off["y"])
                        off[axis] = step
                        sent = (off["x"], off["z"], off["y"])
                        found.append((stage, axis, step, sent, base, len(found)))
            done.append(axis)
        return found

    def send_unit(self, unit, stage):
        for number, (start, rows, order) in enumerate(self.portions):
            for at, axis, step, sent, base, slot in self.hops(order):
                if at == stage and sent == unit:
                    copy = remote(
                        self.held.at[sent + (pl.ds(start, rows), slice(None))],
                        self.landing[number].at[slot],
                        self.sems[2 * number].at[slot],
                        self.sems[2 * number + 1].at[slot],
                        self.place.device(**{"d" + axis: step}),
                    )
                    copy.start()
                    self.started.append(copy)

    def pair_sum(self):
        for unit in self.units():
            load, push = self.loads[unit]
            load.wait()
            push.wait_recv()
            self.held[unit] = (
                self.held[unit].astype(jnp.float32) + self.twin[unit].astype(jnp.float32)
            ).astype(jnp.bfloat16)
            self.send_unit(unit, 0)

    def reduce(self, stage, number, out=None):
        start, rows, order = self.portions[number]
        hops = [hop for hop in self.hops(order) if hop[0] == stage]
        bases = []
        for hop in hops:
            if hop[4] not in bases:
                bases.append(hop[4])
        for base in bases:
            window = base + (pl.ds(start, rows), slice(None))
            total = self.held[window].astype(jnp.float32)
            for at, axis, step, sent, of, slot in hops:
                if of == base:
                    ref = self.landing[number].at[slot]
                    remote(
                        ref,
                        ref,
                        self.sems[2 * number].at[slot],
                        self.sems[2 * number + 1].at[slot],
                        self.place.device(dk=1),
                    ).wait_recv()
                    total = total + self.landing[number][slot].astype(jnp.float32)
            if stage == 2:
                out[pl.ds(start, rows), :] = total
            else:
                self.held[window] = total.astype(jnp.bfloat16)
                for at, axis, step, sent, of, slot in self.hops(order):
                    if at == stage + 1 and sent == base:
                        copy = remote(
                            self.held.at[window],
                            self.landing[number].at[slot],
                            self.sems[2 * number].at[slot],
                            self.sems[2 * number + 1].at[slot],
                            self.place.device(**{"d" + axis: step}),
                        )
                        copy.start()
                        self.started.append(copy)

    def finish(self):
        for copy in self.started:
            copy.wait_send()
        for load, push in self.loads.values():
            push.wait_send()


def scatter_scratch(width, portions):
    buffers = [
        pltpu.VMEM((2, 4, 2, 96, width), jnp.bfloat16),
        pltpu.VMEM((2, 4, 2, 96, width), jnp.bfloat16),
    ]
    buffers += [pltpu.VMEM((15, rows, width), jnp.bfloat16) for start, rows, order in portions]
    buffers += [pltpu.SemaphoreType.DMA((15,)) for _ in portions for _ in range(2)]
    buffers += [pltpu.SemaphoreType.DMA((16,)) for _ in range(3)]
    return buffers


def scatter_kernel(span, part_a, part_f, small, lo, gt, out_a, out_f, out_s, olo, ogt, *scratch):
    place = Place(span)
    per = 2 + len(PORTIONS) * 3 + 3
    groups = scratch[:per], scratch[per : 2 * per]
    s_own, s_land, s_send, s_recv, t_sems = scratch[2 * per :]
    place.greet(ALL_PEERS)
    scatters = []
    for part, group in zip((part_f, part_a), groups):
        n = len(PORTIONS)
        scatters.append(
            Scatter(
                place,
                part,
                group[0],
                group[1],
                group[2 : 2 + n],
                PORTIONS,
                group[2 + n : 2 + 3 * n],
                group[2 + 3 * n :],
            )
        )
    for scatter in scatters:
        scatter.begin()
    x = place.x
    swaps, keeps = [], []
    for n, (src, dst) in enumerate(((lo, olo), (gt, ogt))):
        swaps.append(
            remote(src.at[1 - x], dst.at[x], t_sems.at[3 * n], t_sems.at[3 * n + 1], place.device(dx=1))
        )
        keeps.append(pltpu.make_async_copy(src.at[x], dst.at[x], t_sems.at[3 * n + 2]))
    for copy in swaps + keeps:
        copy.start()
    for scatter in scatters:
        scatter.pair_sum()
    s_own[...] = small[...]
    sends = []
    for n, to in enumerate(({"dk": 1}, {"dx": 1}, {"dy": 1})):
        copy = remote(s_own.at[...], s_land.at[n], s_send.at[n], s_recv.at[n], place.device(**to))
        copy.start()
        copy.wait()
        s_own[...] = s_own[...] + s_land[n]
    for step in (1, 2, 3):
        sends.append(
            remote(s_own, s_land.at[2 + step], s_send.at[2 + step], s_recv.at[2 + step], place.device(dz=step))
        )
        sends[-1].start()
    for scatter, out in zip(scatters, (out_f, out_a)):
        for stage in range(3):
            for number in (2, 3, 0, 1):
                scatter.reduce(stage, number, out)
    for copy in sends:
        copy.wait()
    total = jnp.zeros_like(s_own)
    for at in range(4):
        step = (place.z - at) % 4
        term = jnp.where(
            step == 0,
            s_own[...],
            jnp.where(step == 1, s_land[3], jnp.where(step == 2, s_land[4], s_land[5])),
        )
        total = total + term
    out_s[...] = total
    for scatter in scatters:
        scatter.finish()
    for copy in swaps + keeps:
        copy.wait()


def scatter_all(span, part_a, part_f, small, lo, gt):
    any_space = pl.BlockSpec(memory_space=pl.ANY)
    vmem = pl.BlockSpec(memory_space=pltpu.VMEM)
    return pl.pallas_call(
        partial(scatter_kernel, span),
        out_shape=(
            jax.ShapeDtypeStruct((96, part_a.shape[-1]), jnp.float32),
            jax.ShapeDtypeStruct((96, part_f.shape[-1]), jnp.float32),
            jax.ShapeDtypeStruct(small.shape, jnp.float32),
            jax.ShapeDtypeStruct(lo.shape, lo.dtype),
            jax.ShapeDtypeStruct(gt.shape, gt.dtype),
        ),
        in_specs=[any_space, any_space, vmem, vmem, vmem],
        out_specs=(vmem,) * 5,
        scratch_shapes=scatter_scratch(part_f.shape[-1], PORTIONS)
        + scatter_scratch(part_a.shape[-1], PORTIONS)
        + [
            pltpu.VMEM(small.shape, jnp.float32),
            pltpu.VMEM((6,) + small.shape, jnp.float32),
            pltpu.SemaphoreType.DMA((6,)),
            pltpu.SemaphoreType.DMA((6,)),
            pltpu.SemaphoreType.DMA((6,)),
        ],
        compiler_params=pltpu.CompilerParams(
            collective_id=3, has_side_effects=True, vmem_limit_bytes=VMEM_LIMIT
        ),
        name="scatter_gradients",
    )(part_a, part_f, small, lo, gt)


def lane_half(tile, half):
    lane = lax.broadcasted_iota(jnp.int32, tile.shape, 1)
    keep = (lane < HEAD_DIM) if half == 0 else (lane >= HEAD_DIM)
    return jnp.where(keep, tile, jnp.zeros_like(tile))


def fill_distance(dist, seg_col, seg_row, pos_row):
    keys, queries = dist.shape
    key_pos = lax.broadcasted_iota(jnp.int32, (keys, queries), 0).astype(jnp.float32)
    gap = jnp.abs(key_pos - pos_row)
    dist[...] = jnp.where(seg_col == seg_row, gap, 1e30)


NT = (((1,), (1,)), ((), ()))
NN = (((1,), (0,)), ((), ()))
CHUNK = 256


def dot(a, b, dims=NN):
    return lax.dot_general(a, b, dims, preferred_element_type=jnp.float32)


def attend_kernel(slopes, q, k, v, seg_col, seg_row, pos_row, ctx, lse, dist, out_t):
    step = pl.program_id(0)

    @pl.when(step == 0)
    def _():
        fill_distance(dist, seg_col[...], seg_row[...], pos_row[...])

    v_t = v[...].astype(jnp.float32).T.astype(jnp.bfloat16)
    for half in range(2):
        slope = slopes[2 * step + half]
        for start in range(0, q.shape[0], CHUNK):
            cols = pl.ds(start, CHUNK)
            part = lane_half(q[cols, :], half)
            scores = dot(k[...], part, NT) - slope * dist[:, cols]
            peak = jnp.max(scores, axis=0, keepdims=True)
            expo = jnp.exp(scores - peak)
            total = jnp.sum(expo, axis=0, keepdims=True)
            rows = slice(half * HEAD_DIM, (half + 1) * HEAD_DIM)
            mixed = dot(v_t[rows, :], expo.astype(jnp.bfloat16)) / total
            out_t[rows, cols] = mixed
            lse[0, pl.ds(half, 1), cols] = peak + jnp.log(total)
    ctx[...] = out_t[...].T.astype(jnp.bfloat16)


def attend(slopes, q, kv, seg_col, seg_row, pos_row):
    rows, keys = q.shape[0], kv.shape[0]
    whole = lambda a: pl.BlockSpec(a.shape, lambda i: (0, 0))
    return pl.pallas_call(
        attend_kernel,
        grid=(6,),
        out_shape=(
            jax.ShapeDtypeStruct((rows, 768), jnp.bfloat16),
            jax.ShapeDtypeStruct((6, 8, rows), jnp.float32),
        ),
        in_specs=[
            pl.BlockSpec(memory_space=pltpu.SMEM),
            pl.BlockSpec((rows, 128), lambda i: (0, i)),
            pl.BlockSpec((keys, 128), lambda i: (0, i)),
            pl.BlockSpec((keys, 128), lambda i: (0, 6 + i)),
            whole(seg_col),
            whole(seg_row),
            whole(pos_row),
        ],
        out_specs=(
            pl.BlockSpec((rows, 128), lambda i: (0, i)),
            pl.BlockSpec((1, 8, rows), lambda i: (i, 0, 0)),
        ),
        scratch_shapes=[
            pltpu.VMEM((keys, rows), jnp.float32),
            pltpu.VMEM((128, rows), jnp.float32),
        ],
        compiler_params=pltpu.CompilerParams(vmem_limit_bytes=VMEM_LIMIT),
        name="attend",
    )(slopes, q, kv, kv, seg_col, seg_row, pos_row)


def attend_grad_kernel(
    slopes, q, k, v, ctx, d_ctx, lse, seg_col, seg_row, pos_row, dq, dk, dv, dist, dq_t, dk_acc, dv_acc
):
    step = pl.program_id(0)

    @pl.when(step == 0)
    def _():
        fill_distance(dist, seg_col[...], seg_row[...], pos_row[...])

    k_t = k[...].astype(jnp.float32).T.astype(jnp.bfloat16)
    delta_t = (ctx[...].astype(jnp.float32) * d_ctx[...].astype(jnp.float32)).T
    for half in range(2):
        slope = slopes[2 * step + half]
        rows = slice(half * HEAD_DIM, (half + 1) * HEAD_DIM)
        delta = jnp.sum(delta_t[rows, :], axis=0, keepdims=True)
        for start in range(0, q.shape[0], CHUNK):
            cols = pl.ds(start, CHUNK)
            part = lane_half(q[cols, :], half)
            grad = lane_half(d_ctx[cols, :], half)
            scores = dot(k[...], part, NT) - slope * dist[:, cols]
            probs = jnp.exp(scores - lse[0, pl.ds(half, 1), cols])
            grad_probs = dot(v[...], grad, NT)
            term_v = dot(probs.astype(jnp.bfloat16), grad)
            grad_scores = (probs * (grad_probs - delta[:, start : start + CHUNK])).astype(jnp.bfloat16)
            term_k = dot(grad_scores, part)
            if half == 0 and start == 0:
                dv_acc[...] = term_v
                dk_acc[...] = term_k
            else:
                dv_acc[...] += term_v
                dk_acc[...] += term_k
            dq_t[rows, cols] = dot(k_t[rows, :], grad_scores)
    dq[...] = (dq_t[...].T * HEAD_DIM**-0.5).astype(jnp.bfloat16)
    dk[...] = dk_acc[...].astype(jnp.bfloat16)
    dv[...] = dv_acc[...].astype(jnp.bfloat16)


def attend_grad(slopes, q, kv, ctx, d_ctx, lse, seg_col, seg_row, pos_row):
    rows, keys = q.shape[0], kv.shape[0]
    whole = lambda a: pl.BlockSpec(a.shape, lambda i: (0, 0))
    row_block = pl.BlockSpec((rows, 128), lambda i: (0, i))
    key_block = pl.BlockSpec((keys, 128), lambda i: (0, i))
    return pl.pallas_call(
        attend_grad_kernel,
        grid=(6,),
        out_shape=(
            jax.ShapeDtypeStruct((rows, 768), jnp.bfloat16),
            jax.ShapeDtypeStruct((keys, 768), jnp.bfloat16),
            jax.ShapeDtypeStruct((keys, 768), jnp.bfloat16),
        ),
        in_specs=[
            pl.BlockSpec(memory_space=pltpu.SMEM),
            row_block,
            key_block,
            pl.BlockSpec((keys, 128), lambda i: (0, 6 + i)),
            row_block,
            row_block,
            pl.BlockSpec((1, 8, rows), lambda i: (i, 0, 0)),
            whole(seg_col),
            whole(seg_row),
            whole(pos_row),
        ],
        out_specs=(row_block, key_block, key_block),
        scratch_shapes=[
            pltpu.VMEM((keys, rows), jnp.float32),
            pltpu.VMEM((128, rows), jnp.float32),
            pltpu.VMEM((keys, 128), jnp.float32),
            pltpu.VMEM((keys, 128), jnp.float32),
        ],
        compiler_params=pltpu.CompilerParams(vmem_limit_bytes=VMEM_LIMIT),
        name="attend_grad",
    )(slopes, q, kv, kv, ctx, d_ctx, lse, seg_col, seg_row, pos_row)


def norm_forward(value, gain_row, bias_row):
    average = jnp.mean(value, axis=-1, keepdims=True)
    centered = value - average
    inv_std = lax.rsqrt(jnp.mean(centered * centered, axis=-1, keepdims=True) + norm_eps)
    normed = centered * inv_std
    return (normed * gain_row + bias_row, normed, inv_std)


def norm_backward(grad_val, normed, inv_std, gain_row):
    grad_norm = grad_val * gain_row
    return inv_std * (
        grad_norm
        - jnp.mean(grad_norm, axis=-1, keepdims=True)
        - normed * jnp.mean(grad_norm * normed, axis=-1, keepdims=True)
    )


def local(
    tokens,
    segment_ids,
    query_key_value_weight,
    w_out,
    input_weight,
    w_down,
    norm_gains,
    norm_biases,
    cotangent,
):
    bf16, f32 = jnp.bfloat16, jnp.float32
    shard_rows = query_key_value_weight.shape[1]
    span = 96 // shard_rows
    groups = None
    if span > 1:
        count = lax.axis_size("fsdp")
        groups = [list(range(i, i + span)) for i in range(0, count, span)]
    place_x = lax.axis_index("tp") // 2
    place_k = lax.axis_index("tp") % 2

    heads = query_key_value_weight.transpose(1, 0, 2).reshape(shard_rows, 3, 3, HEAD_DIM)
    w_out_t = w_out.T.reshape(shard_rows, 3, 1, HEAD_DIM)
    wa = jnp.concatenate([heads, w_out_t], axis=2).reshape(shard_rows, 768)
    wf = jnp.concatenate([input_weight.reshape(shard_rows, 1536), w_down.T], axis=1)
    norms = jnp.concatenate([norm_gains, norm_biases], axis=0)
    if span > 1:
        wa = lax.all_gather(wa, "fsdp", axis=0, tiled=True, axis_index_groups=groups)
        wf = lax.all_gather(wf, "fsdp", axis=0, tiled=True, axis_index_groups=groups)
        norms = lax.all_gather(norms, "fsdp", axis=1, tiled=True, axis_index_groups=groups)
    ws = jnp.pad(norms, ((0, 12), (0, 32)))
    ga, gf, gs, xs, cs = gather_all(span, wa, wf, ws, tokens, cotangent)

    norms = gs[0, 0, :, :, :4, :96].reshape(8, 4, 96).transpose(1, 0, 2).reshape(4, 768).astype(f32)
    gains, biases = norms[:2], norms[2:]
    ga = ga.reshape(4, 768, 3, 4, HEAD_DIM)
    w_qkv = ga[:, :, :, :3].transpose(1, 2, 0, 3, 4).reshape(768, 3 * 768)
    w_out_full_t = ga[:, :, :, 3].transpose(1, 0, 2, 3).reshape(768, 768)
    gf = gf.reshape(4, 768, 2304)

    x_rows = xs.reshape(512, 768)
    qkv = jnp.dot(x_rows, w_qkv, preferred_element_type=f32).astype(bf16)
    q = qkv[:, :768] * jnp.bfloat16(HEAD_DIM**-0.5)
    kv = share_keys(span, qkv[:, 768:].reshape(2, 256, 1536)).reshape(1024, 1536)

    segment = lax.dynamic_index_in_dim(segment_ids, place_x, 0, keepdims=False)
    seg_col = segment.reshape(1024, 1)
    seg_row = lax.dynamic_index_in_dim(segment.reshape(2, 2, 256), place_k, 1, keepdims=False)
    seg_row = seg_row.reshape(1, 512)
    pos_row = (
        lax.broadcasted_iota(jnp.int32, (2, 256), 0) * 512
        + place_k * 256
        + lax.broadcasted_iota(jnp.int32, (2, 256), 1)
    )
    pos_row = pos_row.reshape(1, 512).astype(f32)
    slopes = jnp.exp2(-8.0 * (jnp.arange(HEADS).astype(f32) + 1.0) / HEADS)
    ctx, lse = attend(slopes, q, kv, seg_col, seg_row, pos_row)

    attn = lax.dot_general(ctx, w_out_full_t, NT, preferred_element_type=f32)
    resid_one = x_rows.astype(f32) + attn
    h1, normed_one, inv_one = norm_forward(resid_one, gains[0], biases[0])
    h1b = h1.astype(bf16)
    ffn = jnp.zeros_like(h1)
    kept = []
    for t in range(4):
        projected = jnp.dot(h1b, gf[t, :, :1536], preferred_element_type=f32)
        gate, up = projected[:, :768], projected[:, 768:]
        cdf = 0.5 * (1.0 + lax.erf(gate * (0.5**0.5)))
        pdf = jnp.exp(-0.5 * gate * gate) * 0.3989422804014327
        act = gate * cdf
        hidden = (act * up).astype(bf16)
        slope = ((cdf + gate * pdf) * up).astype(bf16)
        kept.append((hidden, act.astype(bf16), slope))
        ffn = ffn + lax.dot_general(hidden, gf[t, :, 1536:], NT, preferred_element_type=f32)
    resid_two = h1 + ffn
    layer_out, normed_two, inv_two = norm_forward(resid_two, gains[1], biases[1])
    grad_layer = cs.reshape(512, 768).astype(f32)
    grad_two = norm_backward(grad_layer, normed_two, inv_two, gains[1])
    d_ffn = grad_two.astype(bf16)
    d_ffn_t = d_ffn.T
    h1b_t = h1b.T
    d_h1 = grad_two
    grads_f = []
    for t in range(4):
        hidden, act, slope = kept[t]
        d_hidden = jnp.dot(d_ffn, gf[t, :, 1536:], preferred_element_type=f32)
        d_gate = (d_hidden * slope.astype(f32)).astype(bf16)
        d_up = (d_hidden * act.astype(f32)).astype(bf16)
        d_proj = jnp.concatenate([d_gate, d_up], axis=1)
        d_win = jnp.dot(h1b_t, d_proj, preferred_element_type=f32).astype(bf16)
        d_down = jnp.dot(d_ffn_t, hidden, preferred_element_type=f32).astype(bf16)
        grads_f.append(jnp.concatenate([d_win, d_down], axis=1))
        d_h1 = d_h1 + lax.dot_general(d_proj, gf[t, :, :1536], NT, preferred_element_type=f32)
    part_f = jnp.stack(grads_f).reshape(2, 2, 4, 2, 96, 2304)
    grad_one = norm_backward(d_h1, normed_one, inv_one, gains[0])
    d_attn = grad_one.astype(bf16)
    d_ctx = jnp.dot(d_attn, w_out_full_t, preferred_element_type=f32).astype(bf16)
    d_wout_t = jnp.dot(d_attn.T, ctx, preferred_element_type=f32).astype(bf16)
    dq, dk, dv = attend_grad(slopes, q, kv, ctx, d_ctx, lse, seg_col, seg_row, pos_row)
    d_kv = share_key_grads(span, jnp.concatenate([dk, dv], axis=1).reshape(2, 2, 256, 1536))
    d_qkv = jnp.concatenate([dq, d_kv.reshape(512, 1536)], axis=1)
    d_wqkv = jnp.dot(x_rows.T, d_qkv, preferred_element_type=f32).astype(bf16)
    d_x = lax.dot_general(d_qkv, w_qkv, NT, preferred_element_type=f32)
    part_a = jnp.concatenate(
        [
            d_wqkv.reshape(768, 3, 4, 3, HEAD_DIM).transpose(2, 0, 1, 3, 4),
            d_wout_t.reshape(768, 4, 3, 1, HEAD_DIM).transpose(1, 0, 2, 3, 4),
        ],
        axis=3,
    ).reshape(2, 2, 4, 2, 96, 768)
    grad_tokens = (grad_one + d_x).astype(bf16).reshape(2, 256, 768)

    sums = jnp.stack(
        [
            jnp.sum(d_h1 * normed_one, axis=0),
            jnp.sum(grad_layer * normed_two, axis=0),
            jnp.sum(d_h1, axis=0),
            jnp.sum(grad_layer, axis=0),
        ]
    )
    squares = jnp.stack([jnp.sum(v * v) for v in (attn, resid_one, ffn, resid_two)])
    small = jnp.concatenate(
        [sums, jnp.pad(squares[None], ((0, 0), (0, 764))), jnp.zeros((3, 768), f32)], axis=0
    )
    out_a, out_f, out_s, lo, gt = scatter_all(
        span, part_a, part_f, small, layer_out.astype(bf16).reshape(2, 256, 768), grad_tokens
    )
    if span > 1:
        out_a = lax.psum_scatter(
            out_a, "fsdp", scatter_dimension=0, tiled=True, axis_index_groups=groups
        )
        out_f = lax.psum_scatter(
            out_f, "fsdp", scatter_dimension=0, tiled=True, axis_index_groups=groups
        )
        out_s = lax.psum(out_s, "fsdp", axis_index_groups=groups)
    out_a = out_a.reshape(shard_rows, 3, 4, HEAD_DIM)
    shard_start = lax.axis_index("fsdp") * shard_rows
    mine = lax.dynamic_slice_in_dim(out_s[:4], shard_start, shard_rows, 1)
    cells = float(lax.axis_size("fsdp") * 2 * 1024 * 768)
    return (
        lo,
        gt,
        out_a[:, :, :3].transpose(1, 0, 2, 3).reshape(3, shard_rows, 192),
        out_a[:, :, 3].reshape(shard_rows, 192).T,
        out_f[:, :1536].reshape(shard_rows, 2, 768),
        out_f[:, 1536:].T,
        mine[:2],
        mine[2:],
        jnp.sqrt(out_s[4, :4] / cells),
    )


def solution(mesh):
    placed = (
        P("fsdp", "tp", None),
        P("fsdp", None),
        P(None, "fsdp", "tp"),
        P("tp", "fsdp"),
        P("fsdp", None, "tp"),
        P("tp", "fsdp"),
        P(None, "fsdp"),
        P(None, "fsdp"),
        P("fsdp", "tp", None),
    )
    return jax.shard_map(
        local,
        mesh=mesh,
        in_specs=placed,
        out_specs=(
            P("fsdp", "tp", None),
            P("fsdp", "tp", None),
            P(None, "fsdp", "tp"),
            P("tp", "fsdp"),
            P("fsdp", None, "tp"),
            P("tp", "fsdp"),
            P(None, "fsdp"),
            P(None, "fsdp"),
            P(),
        ),
        check_vma=False,
    )
```

time: 757 us -> 536 us (0.71)
  waiting for transfers between devices: 339 us -> 0 us
  Pallas kernels: 0 us -> 335 us
  blocking collectives: 151 us -> 0 us
  matrix products: 142 us -> 60 us
  local copies, waits for them, and re-layouts: 43.7 us -> 98.2 us
  other arithmetic: 58.3 us -> 31.4 us
  between operations: 16 us -> 2.11 us
    pallas_call x0 -> x6, Pallas kernels: none -> 335 us  [the longest x1 151 us: scatter_all(): pl.pallas_call(partial(scatter_kernel, span), out_shape=(jax.ShapeDtypeSt...]
    reduce_scatter x6 -> x0, waiting for transfers between devices: 158 us -> none  [the longest x1 46.2 us: local(): lax.psum_scatter(input_weight_gradient.astype(jnp.bfloat16), 'fsdp', scat...]
    all_gather x4 -> x0, blocking collectives: 111 us -> none  [the longest x1 38.8 us: local(): lax.all_gather(query_key_value_weight, 'fsdp', axis=1, tiled=True)]
    all_gather x6 -> x0, waiting for transfers between devices: 97.7 us -> none  [the longest x1 29 us: local(): lax.all_gather(hidden_state_first.astype(jnp.bfloat16), 'tp', axis=1, til...]
    unnamed x16 -> x0, waiting for transfers between devices: 83.5 us -> none
    dot_general x40 -> x30, matrix products: 142 us -> 60 us  [the longest x4 9.32 us: local(): projected = jnp.dot(h1b, gf[t, :, :1536], preferred_element_type=f32)]
    reshape x0 -> x8, local copies, waits for them, and re-layouts: none -> 49 us  [the longest x2 28.2 us: local(): part_a = jnp.concatenate([d_wqkv.reshape(768, 3, 4, 3, HEAD_DIM).transpos...]
    psum x1 -> x0, blocking collectives: 40 us -> none  [local(): lax.psum((gain_terms, bias_terms, square_terms), ('fsdp', 'tp'))]
  transfers between devices with their start and end apart: 14 -> 0, of which waited for: 11 -> 0; matrix products, arithmetic and copies ran while one was open for 19% -> 0% of each run, Pallas kernels for 0% -> 0%
where the time goes in v1:
time: 536 us; the launch traced here: 526 us
  Pallas kernels  335 us (62%)
  local copies, waits for them, and re-layouts  98.2 us (18%)
  matrix products  60 us (11%)
  other arithmetic  31.4 us (6%)
    pallas_call x1, Pallas kernels, scatter_all(): pl.pallas_call(partial(scatter_kernel, span), out_shape=(jax.ShapeDtypeSt...  151 us
    pallas_call x1, Pallas kernels, gather_all(): pl.pallas_call(partial(gather_kernel, span), out_shape=(shape(wa), shape(...  129 us
    reshape x2, local copies, waits for them, and re-layouts, local(): part_a = jnp.concatenate([d_wqkv.reshape(768, 3, 4, 3, HEAD_DIM).transpos...  28.2 us
    pallas_call x1, Pallas kernels, attend(): pl.pallas_call(attend_kernel, grid=(6,), out_shape=(jax.ShapeDtypeStruct(...  21.6 us
    pallas_call x1, Pallas kernels, attend_grad(): pl.pallas_call(attend_grad_kernel, grid=(6,), out_shape=(jax.ShapeDtypeSt...  20 us
    reshape x1, local copies, waits for them, and re-layouts, local(): ga = ga.reshape(4, 768, 3, 4, HEAD_DIM)  17.7 us
    pallas_call x1, local copies, waits for them, and re-layouts, gather_all(): pl.pallas_call(partial(gather_kernel, span), out_shape=(shape(wa), shape(...  15.9 us
    unnamed x133, local copies, waits for them, and re-layouts  15.8 us

profile of v1, /device:TPU:0, one launch (start us, length us, event | category | flops | bytes accessed | tf_op | source)
XLA Modules:
  0.0 526.4 jit_solution(6479873170465821564)
XLA Ops:
  4.7 1.7 pad_maximum_fusion.20.wf
  8.1 129.0 %gather_weights.1 = (bf16[2,2,4,2,96,768]{5,4,3,2,1,0:T(8,128)(2,1)}, bf16[2,2,4,2,96,2304]{5,4,3,2,1,0:T(8,128)(2,1)}, bf16[2,2,4,2,16,128]{5,4,3,2,1,0:T(8,128...) custom-call(bf16[96,768]{1,0:T(8,128)(2,1)} %copy.29.wa, bf16[96,2304]{1,0:T(8,128)(2,1)} %pad_maximum_fusion.20.wf, ...), custom_call_target="tpu_custom_call" | custom-call | tf_op jit(solution)/shard_map/gather_weights/pallas_call | solution.py:185
  137.1 15.9 %copy.30 = bf16[2,2,4,2,96,768]{4,3,2,5,1,0:T(2,128)(2,1)} copy(bf16[2,2,4,2,96,768]{5,4,3,2,1,0:T(8,128)(2,1)} %get-tuple-element.25) | data formatting | bytes 9437184 | tf_op jit(solution)/shard_map/gather_weights/pallas_call | solution.py:185
  153.0 17.7 %reshape.202 = bf16[4,768,3,4,64]{1,4,3,2,0:T(8,128)(2,1)} reshape(bf16[2,2,4,2,96,768]{4,3,2,5,1,0:T(2,128)(2,1)} %copy.30) | data formatting | bytes 9437184 | tf_op jit(solution)/shard_map/reshape | solution.py:690
  170.7 2.2 slice_bitcast_fusion
  174.0 2.0 convolution_convert_fusion.1
  176.1 1.5 slice.154
  178.0 6.5 %share_keys.1 = bf16[2,2,256,1536]{3,2,1,0:T(8,128)(2,1)} custom-call(bf16[2,256,1536]{2,1,0:T(8,128)(2,1)} %bitcast.179), custom_call_target="tpu_custom_call" | custom-call | tf_op jit(solution)/shard_map/share_keys/pallas_call | solution.py:223
  184.5 2.1 slice_multiply_fusion.4.q
  187.1 21.6 %attend.1 = (bf16[512,768]{1,0:T(8,128)(2,1)}, f32[6,8,512]{2,1,0:T(8,128)}) custom-call(f32[12]{0:T(128)} %multiply_exponential_fusion.slopes, bf16[512,768]{1,0:T(8,128)(2,1)} %slice_multiply_fusion.4.q, bf16[1024,1536]{1,0:T(8,128)(2,1)} %bitcast.172, bf16[1024,1536]{1,0:T(8,128)(2,1)} %bitcast.173, s32[1024,1]{1,0:T(8,128)} %copy.32.seg_col, ...), custom_call_target="tpu_custom_call" | custom-call | tf_op jit(solution)/shard_map/attend/pallas_call | solution.py:535
  208.8 1.4 slice.155
  210.2 1.5 fusion.71
  213.4 3.4 fusion.3
  218.5 2.4 fusion.45
  220.9 3.2 fusion.1
  226.6 1.4 fusion.5
  230.6 1.4 fusion.7
  232.0 1.6 copy-done.4
  234.1 1.9 fusion.69
  236.4 2.6 fusion.38
  239.5 2.8 fusion.67
  242.3 3.0 multiply_convert_fusion.7
  245.4 3.7 fusion
  249.1 2.6 multiply_convert_fusion.5
  251.8 1.4 fusion.2
  254.2 1.6 multiply_convert_fusion.3
  255.9 1.4 fusion.4
  258.3 1.6 multiply_convert_fusion.1
  260.0 2.8 multiply_reduce_fusion.4
  264.0 1.7 convolution_convert_fusion.11.d_ctx
  265.7 20.0 %attend_grad.1 = (bf16[512,768]{1,0:T(8,128)(2,1)}, bf16[1024,768]{1,0:T(8,128)(2,1)}, bf16[1024,768]{1,0:T(8,128)(2,1)}) custom-call(f32[12]{0:T(128)} %multiply_exponential_fusion.slopes, bf16[512,768]{1,0:T(8,128)(2,1)} %slice_multiply_fusion.4.q, bf16[1024,1536]{1,0:T(8,128)(2,1)} %bitcast.174, bf16[1024,1536]{1,0:T(8,128)(2,1)} %bitcast.175, ...), custom_call_target="tpu_custom_call" | custom-call | tf_op jit(solution)/shard_map/attend_grad/pallas_call | solution.py:606
  285.8 3.7 pad_maximum_fusion.2
  289.5 6.8 %share_key_grads.1 = bf16[2,256,1536]{2,1,0:T(8,128)(2,1)} custom-call(bf16[2,2,256,1536]{3,2,1,0:T(8,128)(2,1)} %bitcast.178), custom_call_target="tpu_custom_call" | custom-call | tf_op jit(solution)/shard_map/share_key_grads/pallas_call | solution.py:249
  296.4 6.2 %add_convert_fusion = bf16[512,768]{1,0:T(8,128)(2,1)} fusion(f32[512,768]{1,0:T(8,128)} %copy-done.1, bf16[768,2304]{0,1:T(8,128)(2,1)} %bitcast.183, bf16[512,1536]{1,0:T(8,128)(2,1)} %bitcast.187, bf16[512,768]{1,0:T(8,128)(2,1)} %get-tuple-element.31), kind=kOutput, calls=%fused_computation.70 | convolution fusion | flops 1817444352 | bytes 8257536 | tf_op jit(solution)/shard_map/dot_general | solution.py:757
  302.6 2.6 maximum_bitcast_fusion.4
  305.9 1.4 convolution_convert_fusion.4
  308.7 1.4 convolution_convert_fusion.5
  312.3 1.4 convolution_convert_fusion.2
  315.1 1.4 convolution_convert_fusion.3
  317.9 6.9 %pad_maximum_fusion = bf16[4,768,2304]{2,1,0:T(8,128)(2,1)} fusion(bf16[1,768,2304]{2,1,0:T(8,128)(2,1)S(1)} %get-tuple-element.89, bf16[1,768,2304]{2,1,0:T(8,128)(2,1)S(1)} %get-tuple-element.88, bf16[1,768,2304]{2,1,0:T(8,128)(2,1)S(1)} %get-tuple-element.87, bf16[1,768,2304]{2,1,0:T(8,128)(2,1)S(1)} %get-tuple-element.86), kind=kLoop, calls=%fused_computation | loop fusion | flops 21233664 | bytes 28311552 | tf_op jit(solution)/shard_map/stack | solution.py:748
  324.8 3.8 convolution_convert_fusion
  328.6 4.5 copy.34
  333.1 2.4 convolution_convert_fusion.10
  335.7 2.6 pad_maximum_fusion.1
  338.3 14.1 %copy.48 = bf16[4,768,3,4,64]{4,3,2,1,0:T(4,128)(2,1)} copy(bf16[4,768,3,4,64]{1,4,3,0,2:T(8,128)(2,1)} %pad_maximum_fusion.1) | data formatting | bytes 9437184 | tf_op jit(solution)/shard_map/reshape | solution.py:764
  352.4 14.1 %reshape.224.part_a = bf16[2,2,4,2,96,768]{5,4,3,2,1,0:T(8,128)(2,1)} reshape(bf16[4,768,3,4,64]{4,3,2,1,0:T(4,128)(2,1)} %copy.48) | data formatting | bytes 9437184 | tf_op jit(solution)/shard_map/reshape | solution.py:764
  366.5 150.7 %scatter_gradients.1 = (f32[96,768]{1,0:T(8,128)}, f32[96,2304]{1,0:T(8,128)}, f32[8,768]{1,0:T(8,128)}, bf16[2,256,768]{2,1,0:T(8,128)(2,1)}, bf16[2,256,768]{2,1,0:T(8,128)(2,1)}) custom-call(bf16[2,2,4,2,96,768]{5,4,3,2,1,0:T(8,128)(2,1)} %reshape.224.part_a, bf16[2,2,4,2,96,2304]{5,4,3,2,1,0:T(8,128)(2,1)} %bitcast.176, f32[8,768]{1,0:T(8,128)} %concatenate.59.small, ...), custom_call_target="tpu_custom_call" | custom-call | tf_op jit(solution)/shard_map/scatter_gradients/pallas_call | solution.py:459
  521.3 1.7 slice_bitcast_fusion.27
  (193 shorter events, 34.6 us)
Async XLA Ops:
  0.6 5.8 %copy-start.31 = (bf16[3,96,192]{2,1,0:T(8,128)(2,1)S(1)}, bf16[3,96,192]{2,1,0:T(8,128)(2,1)}, u32[]{:S(2)}) copy-start(bf16[3,96,192]{2,1,0:T(8,128)(2,1)} %param.11) | copy-start | bytes 331780
  0.7 5.9 %copy-start.32 = (bf16[192,96]{1,0:T(8,128)(2,1)S(1)}, bf16[192,96]{1,0:T(8,128)(2,1)}, u32[]{:S(2)}) copy-start(bf16[192,96]{1,0:T(8,128)(2,1)} %param.12) | copy-start | bytes 110596
  0.7 6.8 %copy-start.35 = (bf16[2,96]{1,0:T(2,128)(2,1)S(1)}, bf16[2,96]{1,0:T(2,128)(2,1)}, u32[]{:S(2)}) copy-start(bf16[2,96]{1,0:T(2,128)(2,1)} %param.15) | copy-start | bytes 1156
  0.7 6.8 %copy-start.34 = (bf16[2,96]{1,0:T(2,128)(2,1)S(1)}, bf16[2,96]{1,0:T(2,128)(2,1)}, u32[]{:S(2)}) copy-start(bf16[2,96]{1,0:T(2,128)(2,1)} %param.16) | copy-start | bytes 1156
  173.3 2.8 copy-start.2
  176.1 1.9 copy-start.14
  208.8 1.5 copy-start.3
  210.2 1.6 copy-start.16
  213.4 17.2 %copy-start.20 = (bf16[512,768]{1,0:T(8,128)(2,1)}, bf16[512,768]{1,0:T(8,128)(2,1)S(1)}, u32[]{:S(2)}) copy-start(bf16[512,768]{1,0:T(8,128)(2,1)S(1)} %fusion.41) | copy-start | bytes 2359300
  213.4 12.3 %slice-start = ((s8[14155776]{0:T(1024)(128)(4,1)}), s8[4194304]{0:T(1024)(128)(4,1)S(1)}, s32[]{:S(2)}) async-start(s8[14155776]{0:T(1024)(128)(4,1)} %bitcast.204), calls=%async_computation | async-start | bytes 8388608
  213.4 12.3 %slice-start.1 = ((s8[14155776]{0:T(1024)(128)(4,1)}), s8[4194304]{0:T(1024)(128)(4,1)S(1)}, s32[]{:S(2)}) async-start(s8[14155776]{0:T(1024)(128)(4,1)} %bitcast.204), calls=%async_computation.1 | async-start | bytes 8388608
  216.8 1.7 copy-start.6
  218.5 2.4 copy-start.26
  218.5 7.2 %slice-start.2 = ((s8[14155776]{0:T(1024)(128)(4,1)}), s8[4194304]{0:T(1024)(128)(4,1)S(1)}, s32[]{:S(2)}) async-start(s8[14155776]{0:T(1024)(128)(4,1)} %bitcast.204), calls=%async_computation.2 | async-start | bytes 8388608
  220.9 4.8 slice-start.3
  224.1 1.6 copy-start.10
  228.0 1.7 copy-start.8
  232.0 1.6 copy-start.4
  234.1 1.9 copy-start.12
  236.4 2.6 copy-start
  239.5 2.8 copy-start.11
  242.3 15.0 %copy-start.28 = (bf16[512,768]{1,0:T(8,128)(2,1)}, bf16[512,768]{1,0:T(8,128)(2,1)S(1)}, u32[]{:S(2)}) copy-start(bf16[512,768]{1,0:T(8,128)(2,1)S(1)} %get-tuple-element.62) | copy-start | bytes 2359300
  242.3 9.5 %slice-start.4 = ((s8[14155776]{0:T(1024)(128)(4,1)}), s8[4194304]{0:T(1024)(128)(4,1)S(1)}, s32[]{:S(2)}) async-start(s8[14155776]{0:T(1024)(128)(4,1)} %bitcast.211), calls=%async_computation.4 | async-start | bytes 8388608
  242.3 9.5 %slice-start.5 = ((s8[14155776]{0:T(1024)(128)(4,1)}), s8[4194304]{0:T(1024)(128)(4,1)S(1)}, s32[]{:S(2)}) async-start(s8[14155776]{0:T(1024)(128)(4,1)} %bitcast.211), calls=%async_computation.5 | async-start | bytes 8388608
  245.3 3.7 copy-start.47
  245.4 3.7 copy-start.49
  245.4 3.7 copy-start.7
  245.4 6.4 %slice-start.6 = ((s8[14155776]{0:T(1024)(128)(4,1)}), s8[4194304]{0:T(1024)(128)(4,1)S(1)}, s32[]{:S(2)}) async-start(s8[14155776]{0:T(1024)(128)(4,1)} %bitcast.211), calls=%async_computation.6 | async-start | bytes 8388608
  249.1 2.7 slice-start.7
  251.8 1.5 copy-start.51
  251.8 1.5 copy-start.53
  251.8 2.4 copy-start.9
  255.9 1.5 copy-start.43
  255.9 1.5 copy-start.45
  255.9 2.5 copy-start.5
  260.0 2.8 copy-start.39
  260.0 2.8 copy-start.41
  264.0 1.7 copy-start.1
  296.3 9.5 %copy-start.21 = (bf16[512,768]{1,0:T(8,128)(2,1)S(1)}, bf16[512,768]{1,0:T(8,128)(2,1)}, u32[]{:S(2)}) copy-start(bf16[512,768]{1,0:T(8,128)(2,1)} %copy-done.20) | copy-start | bytes 2359300
  296.4 9.5 %copy-start.52 = (bf16[512,768]{1,0:T(8,128)(2,1)S(1)}, bf16[512,768]{1,0:T(8,128)(2,1)}, u32[]{:S(2)}) copy-start(bf16[512,768]{1,0:T(8,128)(2,1)} %copy-done.51) | copy-start | bytes 2359300
  296.4 9.5 %copy-start.54 = (bf16[512,768]{1,0:T(8,128)(2,1)S(1)}, bf16[512,768]{1,0:T(8,128)(2,1)}, u32[]{:S(2)}) copy-start(bf16[512,768]{1,0:T(8,128)(2,1)} %copy-done.53) | copy-start | bytes 2359300
  317.9 6.9 %copy-start.15 = (bf16[2,256,1536]{2,1,0:T(8,128)(2,1)S(1)}, bf16[2,256,1536]{2,1,0:T(8,128)(2,1)}, u32[]{:S(2)}) copy-start(bf16[2,256,1536]{2,1,0:T(8,128)(2,1)} %share_key_grads.1) | copy-start | bytes 4718596
  317.9 6.9 %copy-start.37 = (bf16[2,256,768]{2,1,0:T(8,128)(2,1)S(1)}, bf16[2,256,768]{2,1,0:T(8,128)(2,1)}, u32[]{:S(2)}) copy-start(bf16[2,256,768]{2,1,0:T(8,128)(2,1)} %get-tuple-element.24) | copy-start | bytes 2359300
  317.9 6.9 %copy-start.38 = (bf16[512,768]{1,0:T(8,128)(2,1)S(1)}, bf16[512,768]{1,0:T(8,128)(2,1)}, u32[]{:S(2)}) copy-start(bf16[512,768]{1,0:T(8,128)(2,1)} %get-tuple-element.31) | copy-start | bytes 2359300
  517.2 2.4 copy-start.30
  519.6 3.4 copy-start.33
  519.6 4.6 copy-start.19
  519.8 5.3 %copy-start.18 = (bf16[2,256,768]{2,1,0:T(8,128)(2,1)S(1)}, bf16[2,256,768]{2,1,0:T(8,128)(2,1)}, u32[]{:S(2)}) copy-start(bf16[2,256,768]{2,1,0:T(8,128)(2,1)} %get-tuple-element.100) | copy-start | bytes 2359300
  (15 other events, 18.9 us)

commit v2 on v0

v2 whole, which is shorter than its diff:
```python
from functools import partial

import jax
import jax.numpy as jnp
from jax import lax
from jax.experimental import pallas as pl
from jax.experimental.pallas import tpu as pltpu
from jax.sharding import PartitionSpec as P

HEADS = 12
HEAD_DIM = 64
MESH = pl.DeviceIdType.MESH
VMEM_LIMIT = 63 << 20
norm_eps = 1e-05
ROUNDS = 4
CUT = 48
NT = (((1,), (1,)), ((), ()))
NN = (((1,), (0,)), ((), ()))
CHUNK = 256


class Place:
    def __init__(self, span):
        index = lax.axis_index("fsdp")
        shard = lax.axis_index("tp")
        self.span = span
        self.j = index % span
        block = index // span
        self.z = block // 2
        self.y = block % 2
        self.x = shard // 2
        self.k = shard % 2

    def shifted(self, dx=0, dy=0, dz=0, dk=0):
        x = 1 - self.x if dx else self.x
        y = 1 - self.y if dy else self.y
        z = (self.z + dz) % 4 if dz else self.z
        k = 1 - self.k if dk else self.k
        return x, y, z, k

    def device(self, dx=0, dy=0, dz=0, dk=0):
        x, y, z, k = self.shifted(dx, dy, dz, dk)
        return ((z * 2 + y) * self.span + self.j, x * 2 + k)

    def greet(self, offsets):
        barrier = pltpu.get_barrier_semaphore()
        for offset in offsets:
            pl.semaphore_signal(
                barrier, inc=1, device_id=self.device(**offset), device_id_type=MESH
            )
        pl.semaphore_wait(barrier, len(offsets))


ALL_PEERS = ({"dx": 1}, {"dy": 1}, {"dz": 1}, {"dz": 2}, {"dz": 3}, {"dk": 1})


def remote(src, dst, send, recv, device):
    return pltpu.make_async_remote_copy(
        src_ref=src, dst_ref=dst, send_sem=send, recv_sem=recv, device_id=device, device_id_type=MESH
    )


def dot(a, b, dims=NN):
    return lax.dot_general(a, b, dims, preferred_element_type=jnp.float32)


class Copies:
    names = ()

    def start(self, *names):
        for name in names:
            self.copy(name).start()

    def wait(self, *names):
        for name in names:
            self.copy(name).wait_recv()

    def finish(self):
        for name in self.names:
            self.copy(name).wait_send()


class GatherRound(Copies):
    names = ("z1", "z2", "z3", "ax", "by", "ay0", "bx0", "ay1", "bx1") + tuple(
        "d%d" % i for i in range(7)
    )
    lines = {
        "ax": ((0, 0, "a"), {"dx": 1}),
        "by": ((0, 0, "b"), {"dy": 1}),
        "ay0": ((0, 0, "a"), {"dy": 1}),
        "bx0": ((0, 0, "b"), {"dx": 1}),
        "ay1": ((1, 0, "a"), {"dy": 1}),
        "bx1": ((0, 1, "b"), {"dx": 1}),
        "d0": ((0, 0, ""), {"dk": 1}),
        "d1": ((1, 0, "a"), {"dk": 1}),
        "d2": ((0, 1, "b"), {"dk": 1}),
        "d3": ((0, 1, "a"), {"dk": 1}),
        "d4": ((1, 0, "b"), {"dk": 1}),
        "d5": ((1, 1, "a"), {"dk": 1}),
        "d6": ((1, 1, "b"), {"dk": 1}),
    }
    steps = {
        2: ("ax", "ay1", "d1"),
        3: ("by", "bx1", "d2"),
        4: ("ay0", "d3"),
        5: ("bx0", "d4"),
        6: ("ay1", "d5"),
        7: ("bx1", "d6"),
    }

    def __init__(self, place, own, out, send, recv, keep):
        self.place, self.own, self.out = place, own, out
        self.send, self.recv, self.keep = send, recv, keep

    def line(self, dx, dy, part):
        x, y, z, k = self.place.shifted(dx, dy)
        rows = {"a": pl.ds(0, CUT), "b": pl.ds(CUT, 96 - CUT), "": pl.ds(0, 96)}[part]
        return self.out.at[x, k, :, y, rows, :]

    def copy(self, name):
        place = self.place
        at = self.names.index(name)
        send, recv = self.send.at[at], self.recv.at[at]
        if name[0] == "z":
            x, y, z, k = place.shifted()
            return remote(
                self.own, self.out.at[x, k, z, y], send, recv, place.device(dz=int(name[1]))
            )
        where, to = self.lines[name]
        ref = self.line(*where)
        return remote(ref, ref, send, recv, place.device(**to))

    def kept(self):
        x, y, z, k = self.place.shifted()
        return pltpu.make_async_copy(self.own, self.out.at[x, k, z, y], self.keep)

    def event(self, n):
        if n == 0:
            self.kept().start()
            self.start("z1", "z2", "z3")
        elif n == 1:
            self.kept().wait()
            self.wait("z1", "z2", "z3")
            self.start("ax", "by", "ay0", "bx0", "d0")
        elif n == 8:
            self.wait(*self.names[9:])
        else:
            self.wait(self.steps[n][0])
            self.start(*self.steps[n][1:])


class NormGather(Copies):
    names = ("z1", "z2", "z3", "y")

    def __init__(self, place, own, out, send, recv, keep):
        self.place, self.own, self.out = place, own, out
        self.send, self.recv, self.keep = send, recv, keep

    def copy(self, name):
        place = self.place
        at = self.names.index(name)
        send, recv = self.send.at[at], self.recv.at[at]
        if name == "y":
            ref = self.out.at[:, place.y]
            return remote(ref, ref, send, recv, place.device(dy=1))
        return remote(
            self.own, self.out.at[place.z, place.y], send, recv, place.device(dz=int(name[1]))
        )

    def kept(self):
        return pltpu.make_async_copy(self.own, self.out.at[self.place.z, self.place.y], self.keep)


class Events:
    def __init__(self, steps):
        self.steps = list(steps)

    def run(self, count):
        for step in self.steps[:count]:
            step()
        del self.steps[:count]

    def spread(self, trips, points, count):
        total = trips * points
        return self.place(trips, points, {n * total // max(count, 1): 1 for n in range(count)})

    def place(self, trips, points, counts):
        total = trips * points
        slots = [[] for _ in range(total)]
        for number in sorted(counts):
            slots[number] += self.steps[: counts[number]]
            del self.steps[: counts[number]]

        def stop(i, point):
            for trip in range(trips):
                todo = slots[trip * points + point]
                if todo:

                    @pl.when(i == trip)
                    def _():
                        for step in todo:
                            step()

        return stop


def lane_half(tile, half):
    lane = lax.broadcasted_iota(jnp.int32, tile.shape, 1)
    keep = (lane < HEAD_DIM) if half == 0 else (lane >= HEAD_DIM)
    return jnp.where(keep, tile, jnp.zeros_like(tile))


def swap_halves(tile):
    return pltpu.roll(tile.astype(jnp.float32), HEAD_DIM, 1)


def fill_distance(dist, seg_col, seg_row, pos_row):
    keys, queries = dist.shape
    key_pos = lax.broadcasted_iota(jnp.int32, (keys, queries), 0).astype(jnp.float32)
    gap = jnp.abs(key_pos - pos_row[...])
    dist[...] = jnp.where(seg_col[...] == seg_row[...], gap, 1e30)


def out_weights(w):
    first = lax.broadcasted_iota(jnp.int32, (768, 128), 1) < HEAD_DIM
    left = jnp.where(first, swap_halves(w[:, 128:256]), w[:, 384:512].astype(jnp.float32))
    right = jnp.where(first, swap_halves(w[:, 640:768]), 0.0)
    return left.astype(jnp.bfloat16), right.astype(jnp.bfloat16)


def whole(ref):
    value = ref[...]
    return value.reshape(768, value.shape[-1])


HEAD_SPOTS = ((0, 0), (0, 1), (1, 0))


def norm_stats(value):
    average = jnp.mean(value, axis=-1, keepdims=True)
    centered = value - average
    inv_std = lax.rsqrt(jnp.mean(centered * centered, axis=-1, keepdims=True) + norm_eps)
    return centered * inv_std, inv_std


def norm_backward(grad_val, normed, inv_std, gain_row):
    grad_norm = grad_val * gain_row
    return inv_std * (
        grad_norm
        - jnp.mean(grad_norm, axis=-1, keepdims=True)
        - normed * jnp.mean(grad_norm * normed, axis=-1, keepdims=True)
    )


ROWS = 128


def row_blocks(body):
    def step(i, carry):
        body(pl.ds(pl.multiple_of(i * ROWS, ROWS), ROWS), i)
        return carry

    lax.fori_loop(0, 512 // ROWS, step, 0)


def columns(value):
    return jnp.sum(value.reshape(value.shape[0] // 8, 8, value.shape[1]), axis=0)


def forward_kernel(
    span,
    slopes,
    shard,
    norm_rows,
    tok,
    cot,
    seg_col,
    seg_row,
    pos_row,
    o_weights,
    o_norms,
    o_x,
    o_cot,
    o_q,
    o_k,
    o_v,
    o_ctx,
    o_lse,
    o_kept,
    o_h1b,
    o_n1,
    o_i1,
    o_n2,
    o_i2,
    o_out,
    o_squares,
    weights,
    norms,
    xs,
    keys,
    values,
    dist,
    out_t,
    acc,
    h1,
    kept,
    g_send,
    g_recv,
    g_keep,
    n_send,
    n_recv,
    n_keep,
    t_sems,
    kv_send,
    kv_recv,
    store_sems,
    kept_sems,
):
    f32, bf16 = jnp.float32, jnp.bfloat16
    place = Place(span)
    x, y, z, k = place.shifted()
    rounds = [
        GatherRound(place, shard.at[r], weights.at[r], g_send.at[r], g_recv.at[r], g_keep.at[r])
        for r in range(ROUNDS)
    ]
    norm_gather = NormGather(place, norm_rows, norms, n_send, n_recv, n_keep)

    def swap(n):
        src, dst = ((tok, xs), (cot, o_cot))[n]
        return remote(
            src.at[1 - place.x],
            dst.at[place.x],
            t_sems.at[3 * n],
            t_sems.at[3 * n + 1],
            place.device(dx=1),
        )

    def stay(n):
        src, dst = ((tok, xs), (cot, o_cot))[n]
        return pltpu.make_async_copy(src.at[place.x], dst.at[place.x], t_sems.at[3 * n + 2])

    def store(n):
        src, dst = (
            (weights.at[0], o_weights.at[0]),
            (weights.at[1], o_weights.at[1]),
            (weights.at[2], o_weights.at[2]),
            (weights.at[3], o_weights.at[3]),
            (xs, o_x),
            (keys, o_k),
            (values, o_v),
        )[n]
        return pltpu.make_async_copy(src, dst, store_sems.at[n])

    place.greet(ALL_PEERS)
    swap(0).start()
    stay(0).start()
    stay(1).start()
    norm_gather.kept().start()
    norm_gather.start("z1", "z2", "z3")

    def step(r, n):
        def go():
            rounds[r].event(n)
            if n == 8:
                store(r).start()

        return go

    order = [(0, 0), (0, 1), (1, 0), (0, 2), (0, 3), (1, 1), (2, 0), (0, 4), (0, 5), (0, 6), (0, 7), (0, 8)]
    order += [(1, 2), (1, 3), (2, 1), (3, 0), (1, 4), (1, 5), (1, 6), (1, 7), (2, 2), (2, 3), (3, 1), (1, 8)]
    order += [(2, 4), (2, 5), (2, 6), (2, 7), (3, 2), (3, 3), (2, 8)]
    order += [(3, 4), (3, 5), (3, 6), (3, 7), (3, 8)]
    events = Events(step(*at) for at in order)
    events.steps.insert(-5, lambda: swap(1).start())

    events.run(2)
    fill_distance(dist, seg_col, seg_row, pos_row)
    norm_gather.kept().wait()
    norm_gather.wait("z1", "z2", "z3")
    norm_gather.start("y")
    events.run(10)
    swap(0).wait_recv()
    stay(0).wait()
    store(4).start()

    def share(t, n):
        ref = (keys, values)[n].at[pl.ds(2 * t, 2), :, place.k]
        return remote(ref, ref, kv_send.at[t, n], kv_recv.at[t, n], place.device(dk=1))

    def project(t, carry):
        w = whole(weights.at[0, t // 2, t % 2])
        for s in range(2):
            out = dot(xs[s], w).astype(bf16)
            for i in range(2):
                cols = slice(i * 128, i * 128 + 128)
                o_q[2 * t + i, pl.ds(s * 256, 256), :] = out[:, cols] * bf16(HEAD_DIM**-0.5)
                keys[2 * t + i, s, k] = out[:, 256 + i * 128 : 384 + i * 128]
                values[2 * t + i, s, k] = out[:, 512 + i * 128 : 640 + i * 128]
        share(t, 0).start()
        share(t, 1).start()
        return carry

    lax.fori_loop(0, 4, project, 0)
    out_t[1, pl.ds(HEAD_DIM, HEAD_DIM), :] = jnp.zeros((HEAD_DIM, 512), f32)
    stop = events.spread(4, 7, 12)

    def attend(t, carry):
        share(t, 0).wait_recv()
        share(t, 1).wait_recv()
        point = 0
        for spot, (tile, half) in enumerate(HEAD_SPOTS):
            slope = slopes[3 * t + spot]
            key = keys[2 * t + tile].reshape(1024, 128)
            rows = slice(half * HEAD_DIM, (half + 1) * HEAD_DIM)
            value_t = values[2 * t + tile].reshape(1024, 128).astype(f32).T.astype(bf16)[rows]
            for start in range(0, 512, CHUNK):
                cols = pl.ds(start, CHUNK)
                part = lane_half(o_q[2 * t + tile, cols, :], half)
                scores = dot(key, part, NT) - slope * dist[:, cols]
                peak = jnp.max(scores, axis=0, keepdims=True)
                expo = jnp.exp(scores - peak)
                total = jnp.sum(expo, axis=0, keepdims=True)
                out_t[tile, rows, cols] = dot(value_t, expo.astype(bf16)) / total
                o_lse[t, pl.ds(spot, 1), cols] = peak + jnp.log(total)
                stop(t, point)
                point += 1
        for tile in range(2):
            o_ctx[2 * t + tile] = out_t[tile].T.astype(bf16)
        left, right = out_weights(whole(weights.at[0, t // 2, t % 2]))
        mixed = dot(o_ctx[2 * t], left, NT) + dot(o_ctx[2 * t + 1], right, NT)

        @pl.when(t == 0)
        def _():
            acc[...] = mixed

        @pl.when(t > 0)
        def _():
            acc[...] += mixed

        stop(t, point)
        return carry

    lax.fori_loop(0, 4, attend, 0)
    store(5).start()
    store(6).start()
    norm_gather.wait("y")
    norm_sum = jnp.sum(norms[...].reshape(8, 8, 768), axis=0)
    o_norms[...] = norm_sum

    def first_norm(rows, i):
        attn = acc[rows, :]
        half = i // 2
        resid = xs[half, pl.ds(pl.multiple_of((i % 2) * ROWS, ROWS), ROWS), :].astype(f32) + attn
        normed, inv = norm_stats(resid)
        value = normed * norm_sum[0:1] + norm_sum[2:3]
        h1[rows, :] = value
        o_h1b[rows, :] = value.astype(bf16)
        o_n1[rows, :] = normed
        o_i1[rows, :] = inv
        acc[rows, :] = jnp.zeros_like(attn)
        if_first = jnp.where(i == 0, 0.0, 1.0)
        o_squares[0] = o_squares[0] * if_first + columns(attn * attn)
        o_squares[1] = o_squares[1] * if_first + columns(resid * resid)

    o_squares[...] = jnp.zeros_like(o_squares)
    row_blocks(first_norm)

    stop_f = events.place(
        12, 2, {1: 1, 2: 1, 3: 1, 4: 1, 5: 1, 6: 1, 8: 1, 9: 1, 11: 1, 12: 1, 13: 1, 14: 1, 16: 1}
    )
    assert not events.steps

    def keep_copy(n):
        return pltpu.make_async_copy(kept.at[n % 2], o_kept.at[n], kept_sems.at[n % 2])

    def feed(n, carry):
        r, t = 1 + n // 4, n % 4
        stop_f(n, 0)

        @pl.when(n >= 2)
        def _():
            keep_copy(n - 2).wait()

        ref = weights.at[r, t // 2, t % 2]
        for start in range(0, 512, CHUNK):
            rows = pl.ds(start, CHUNK)
            w = whole(ref)
            projected = dot(o_h1b[rows, :], w[:, :512])
            gate, up = projected[:, :256], projected[:, 256:]
            cdf = 0.5 + 0.5 * lax.erf(gate * (0.5**0.5))
            pdf = jnp.exp(-0.5 * gate * gate) * 0.3989422804014327
            act = gate * cdf
            hidden = (act * up).astype(bf16)
            kept[n % 2, 0, rows, :] = hidden
            kept[n % 2, 1, rows, :] = act.astype(bf16)
            kept[n % 2, 2, rows, :] = ((cdf + gate * pdf) * up).astype(bf16)
            acc[rows, :] += dot(hidden, w[:, 512:], NT)
        keep_copy(n).start()
        stop_f(n, 1)
        return carry

    lax.fori_loop(0, 12, feed, 0)

    def second_norm(rows, i):
        ffn = acc[rows, :]
        resid = h1[rows, :] + ffn
        normed, inv = norm_stats(resid)
        o_out[rows, :] = (normed * norm_sum[1:2] + norm_sum[3:4]).astype(bf16)
        o_n2[rows, :] = normed
        o_i2[rows, :] = inv
        o_squares[2] += columns(ffn * ffn)
        o_squares[3] += columns(resid * resid)

    row_blocks(second_norm)
    for n in (10, 11):
        keep_copy(n).wait()
    for r in rounds:
        r.finish()
    norm_gather.finish()
    for n in range(2):
        swap(n).wait_send()
    swap(1).wait_recv()
    stay(1).wait()
    for t in range(4):
        for n in range(2):
            share(t, n).wait_send()
    for n in range(7):
        store(n).wait()


def forward(span, slopes, shard, norm_rows, tok, cot, seg_col, seg_row, pos_row):
    f32, bf16 = jnp.float32, jnp.bfloat16
    any_space = pl.BlockSpec(memory_space=pl.ANY)
    vmem = pl.BlockSpec(memory_space=pltpu.VMEM)
    outs = (
        ((ROUNDS, 2, 2, 4, 2, 96, 768), bf16, any_space),
        ((8, 768), f32, vmem),
        ((2, 256, 768), bf16, any_space),
        ((2, 256, 768), bf16, any_space),
        ((8, 512, 128), bf16, vmem),
        ((8, 2, 2, 256, 128), bf16, any_space),
        ((8, 2, 2, 256, 128), bf16, any_space),
        ((8, 512, 128), bf16, vmem),
        ((4, 8, 512), f32, vmem),
        ((12, 3, 512, 256), bf16, any_space),
        ((512, 768), bf16, vmem),
        ((512, 768), f32, vmem),
        ((512, 1), f32, vmem),
        ((512, 768), f32, vmem),
        ((512, 1), f32, vmem),
        ((512, 768), bf16, vmem),
        ((4, 8, 768), f32, vmem),
    )
    dma = pltpu.SemaphoreType.DMA
    return pl.pallas_call(
        partial(forward_kernel, span),
        out_shape=tuple(jax.ShapeDtypeStruct(s, d) for s, d, _ in outs),
        in_specs=[pl.BlockSpec(memory_space=pltpu.SMEM)] + [vmem] * 7,
        out_specs=tuple(spec for _, _, spec in outs),
        scratch_shapes=[
            pltpu.VMEM((ROUNDS, 2, 2, 4, 2, 96, 768), bf16),
            pltpu.VMEM((4, 2, 8, 768), f32),
            pltpu.VMEM((2, 256, 768), bf16),
            pltpu.VMEM((8, 2, 2, 256, 128), bf16),
            pltpu.VMEM((8, 2, 2, 256, 128), bf16),
            pltpu.VMEM((1024, 512), f32),
            pltpu.VMEM((2, 128, 512), f32),
            pltpu.VMEM((512, 768), f32),
            pltpu.VMEM((512, 768), f32),
            pltpu.VMEM((2, 3, 512, 256), bf16),
            dma((ROUNDS, 16)),
            dma((ROUNDS, 16)),
            dma((ROUNDS,)),
            dma((4,)),
            dma((4,)),
            dma,
            dma((6,)),
            dma((4, 2)),
            dma((4, 2)),
            dma((7,)),
            dma((2,)),
        ],
        compiler_params=pltpu.CompilerParams(
            collective_id=0, has_side_effects=True, vmem_limit_bytes=VMEM_LIMIT
        ),
        name="forward",
    )(slopes, shard, norm_rows, tok, cot, seg_col, seg_row, pos_row)


class ScatterRound(Copies):
    names = ("ay1", "bx", "ay0", "ax", "by", "az1", "az2", "az3", "bz1", "bz2", "bz3")

    def __init__(self, place, held, twin, stage, land_ay, land_bx, land_ax, land_by, land_z, send, recv, pair):
        self.place, self.held, self.twin, self.stage = place, held, twin, stage
        self.land_ay, self.land_bx, self.land_ax = land_ay, land_bx, land_ax
        self.land_by, self.land_z = land_by, land_z
        self.send, self.recv, self.pair = send, recv, pair

    def copy(self, name):
        p = self.place
        at = self.names.index(name)
        send, recv = self.send.at[at], self.recv.at[at]
        a, b = pl.ds(0, CUT), pl.ds(CUT, 96 - CUT)
        if name in ("ay1", "ay0"):
            dx = int(name[2])
            return remote(
                self.held.at[dx, :, 1 - p.y, a, :], self.land_ay.at[dx], send, recv, p.device(dy=1)
            )
        if name == "bx":
            return remote(self.held.at[1, :, :, b, :], self.land_bx, send, recv, p.device(dx=1))
        if name == "ax":
            return remote(self.held.at[1, :, p.y, a, :], self.land_ax, send, recv, p.device(dx=1))
        if name == "by":
            return remote(self.held.at[0, :, 1 - p.y, b, :], self.land_by, send, recv, p.device(dy=1))
        step = int(name[2])
        rows = a if name[0] == "a" else b
        return remote(
            self.held.at[0, (p.z + step) % 4, p.y, rows, :],
            self.land_z.at[step - 1, rows, :],
            send,
            recv,
            p.device(dz=step),
        )

    def push(self, dx):
        return remote(
            self.stage.at[dx], self.twin.at[dx], self.pair.at[0, dx], self.pair.at[1, dx], self.place.device(dk=1)
        )

    def add(self, ref, other):
        ref[...] = (ref[...].astype(jnp.float32) + other[...].astype(jnp.float32)).astype(jnp.bfloat16)

    def pair_sum(self, dx):
        self.push(dx).wait_recv()

        def body(i, carry):
            self.add(self.held.at[dx, i], self.twin.at[dx, i])
            return carry

        lax.fori_loop(0, 4, body, 0)
        if dx:
            self.start("bx", "ay1")
        else:
            self.start("ay0")

    def event(self, n, out=None):
        p = self.place
        a, b = pl.ds(0, CUT), pl.ds(CUT, 96 - CUT)
        if n == 0:
            self.wait("ay1")
            self.add(self.held.at[1, :, p.y, a, :], self.land_ay.at[1])
            self.start("ax")
        elif n == 1:
            self.wait("bx")
            self.add(self.held.at[0, :, 1 - p.y, b, :], self.land_bx.at[:, 1 - p.y])
            self.start("by")
            self.add(self.held.at[0, :, p.y, b, :], self.land_bx.at[:, p.y])
        elif n == 2:
            self.wait("ay0")
            self.add(self.held.at[0, :, p.y, a, :], self.land_ay.at[0])
        elif n == 3:
            self.wait("ax")
            self.add(self.held.at[0, :, p.y, a, :], self.land_ax)
            self.start("az1", "az2", "az3")
        elif n == 4:
            self.wait("by")
            self.add(self.held.at[0, :, p.y, b, :], self.land_by)
            self.start("bz1", "bz2", "bz3")
        else:
            self.wait("az1", "az2", "az3", "bz1", "bz2", "bz3")
            total = self.held[0, p.z, p.y].astype(jnp.float32)
            for step in range(3):
                total = total + self.land_z[step].astype(jnp.float32)
            out[...] = total


def backward_kernel(
    span,
    slopes,
    i_weights,
    norms,
    i_x,
    i_cot,
    i_q,
    i_k,
    i_v,
    i_ctx,
    i_lse,
    i_kept,
    i_h1b,
    i_n1,
    i_i1,
    i_n2,
    i_i2,
    i_out,
    squares,
    seg_col,
    seg_row,
    pos_row,
    o_out,
    o_tokens,
    o_grads,
    o_small,
    w_buf,
    kept,
    h1_t,
    f_t,
    d_rows,
    n_buf,
    d_h1,
    q,
    keys,
    values,
    ctx,
    lse,
    dist,
    d_ctx,
    d_kv,
    d_kv_in,
    dq_t,
    acc_k,
    acc_v,
    held,
    twin,
    stage,
    land_ay,
    land_bx,
    land_ax,
    land_by,
    land_z,
    small,
    small_in,
    load_sems,
    step_sems,
    r_send,
    r_recv,
    r_pair,
    t_sems,
    kv_send,
    kv_recv,
    s_send,
    s_recv,
):
    f32, bf16 = jnp.float32, jnp.bfloat16
    place = Place(span)
    x, y, z, k = place.shifted()
    rounds = [
        ScatterRound(
            place,
            held.at[n],
            twin.at[n % 3],
            stage,
            land_ay.at[n],
            land_bx.at[n],
            land_ax.at[n],
            land_by.at[n],
            land_z.at[n],
            r_send.at[n],
            r_recv.at[n],
            r_pair.at[n],
        )
        for n in range(ROUNDS)
    ]

    def load(n):
        src, dst = (
            (i_cot, d_rows.at[2]),
            (i_n2, n_buf),
            (i_h1b, d_rows.at[1]),
            (i_x, d_rows.at[2]),
            (i_q, q),
            (i_k, keys),
            (i_v, values),
            (i_ctx, ctx),
            (i_lse, lse),
            (i_n1, n_buf),
        )[n]
        return pltpu.make_async_copy(src, dst, load_sems.at[n])

    def where(n):
        return x ^ (1 - n % 2), jnp.where(n < 2, 1 - k, k)

    def fetch(n, part):
        r = 3 - n // 4
        wx, wk = where(n % 4)
        if part == 0:
            return pltpu.make_async_copy(i_weights.at[r, wx, wk], w_buf.at[n % 2], step_sems.at[n % 2, 0])
        return pltpu.make_async_copy(
            i_kept.at[(r - 1) * 4 + wx * 2 + wk], kept.at[n % 2], step_sems.at[n % 2, 1]
        )

    for n in (0, 1, 2, 4, 5, 6, 7, 8):
        load(n).start()
    fetch(0, 0).start()
    fetch(0, 1).start()
    place.greet(ALL_PEERS)

    def swap(n):
        src, dst = ((i_out, o_out), (d_rows.at[0], o_tokens))[n]
        return remote(
            src.at[1 - place.x],
            dst.at[place.x],
            t_sems.at[3 * n],
            t_sems.at[3 * n + 1],
            place.device(dx=1),
        )

    def stay(n):
        src, dst = ((i_out, o_out), (d_rows.at[0], o_tokens))[n]
        return pltpu.make_async_copy(src.at[place.x], dst.at[place.x], t_sems.at[3 * n + 2])

    swap(0).start()
    stay(0).start()
    load(0).wait()
    load(1).wait()
    small[...] = jnp.zeros_like(small)

    def halves(ref, i):
        return ref.at[i // 2, pl.ds(pl.multiple_of((i % 2) * ROWS, ROWS), ROWS), :]

    sums = [jnp.zeros((8, 768), f32)] * 2
    for i in range(512 // ROWS):
        rows = pl.ds(i * ROWS, ROWS)
        grad = halves(d_rows.at[2], i)[...].astype(f32)
        normed = n_buf[rows, :]
        out = norm_backward(grad, normed, i_i2[rows, :], norms[1:2])
        d_h1[rows, :] = out
        halves(d_rows.at[0], i)[...] = out.astype(bf16)
        f_t[:, rows] = out.T.astype(bf16)
        sums[0] = sums[0] + columns(grad * normed)
        sums[1] = sums[1] + columns(grad)
    small[1] = sums[0]
    small[3] = sums[1]
    load(9).start()
    load(3).start()
    load(2).wait()
    for i in range(512 // ROWS):
        rows = pl.ds(i * ROWS, ROWS)
        h1_t[:, rows] = halves(d_rows.at[1], i)[...].astype(f32).T.astype(bf16)
    fill_distance(dist, seg_col, seg_row, pos_row)

    def pair(n, dx):
        return lambda: rounds[n].pair_sum(dx)

    def step(n, at):
        return lambda: rounds[n].event(at, o_grads.at[3 - n])

    def put(n, dx, value, cols):
        block = value.astype(bf16).reshape(4, 2, 96, value.shape[-1])

        @pl.when(n % 4 < 2)
        def _():
            stage[dx, :, :, :, cols] = block

        @pl.when(n % 4 >= 2)
        def _():
            held[n // 4, dx, :, :, :, cols] = block

    def push(n, dx):
        return remote(
            stage.at[dx], twin.at[n % 3, dx], r_pair.at[n, 0, dx], r_pair.at[n, 1, dx], place.device(dk=1)
        )

    plan = {
        2: [pair(0, 1)],
        3: [pair(0, 0)],
        5: [step(0, 0), step(0, 1)],
        6: [step(0, 2), pair(1, 1)],
        7: [pair(1, 0), step(0, 3), step(0, 4)],
        9: [step(1, 0), step(1, 1), step(0, 5)],
        10: [step(1, 2), pair(2, 1)],
        11: [pair(2, 0), step(1, 3), step(1, 4)],
    }

    def feed(n, carry):
        dx = 1 - n % 2

        @pl.when(n < 11)
        def _():
            fetch(n + 1, 0).start()
            fetch(n + 1, 1).start()

        @pl.when(n % 4 < 2)
        def _():
            @pl.when(n >= 4)
            def _():
                push(n // 4 - 1, dx).wait_send()

        fetch(n, 0).wait()
        fetch(n, 1).wait()
        w = whole(w_buf.at[n % 2])
        hold = kept.at[n % 2]
        d_ffn = d_rows[0].reshape(512, 768)
        put(n, dx, dot(f_t[...], hold[0]), slice(512, 768))
        d_hidden = dot(d_ffn, w[:, 512:])
        d_gate = (d_hidden * hold[2].astype(f32)).astype(bf16)
        d_up = (d_hidden * hold[1].astype(f32)).astype(bf16)
        put(n, dx, dot(h1_t[...], d_gate), slice(0, 256))
        put(n, dx, dot(h1_t[...], d_up), slice(256, 512))

        @pl.when(n % 4 < 2)
        def _():
            push(n // 4, dx).start()

        d_h1[...] += dot(d_gate, w[:, :256], NT) + dot(d_up, w[:, 256:512], NT)
        for at, todo in plan.items():

            @pl.when(n == at)
            def _():
                for item in todo:
                    item()

        return carry

    lax.fori_loop(0, 12, feed, 0)
    load(9).wait()
    load(3).wait()
    for i in range(512 // ROWS):
        rows = pl.ds(i * ROWS, ROWS)
        h1_t[:, rows] = halves(d_rows.at[2], i)[...].astype(f32).T.astype(bf16)
    sums = [jnp.zeros((8, 768), f32)] * 2
    for i in range(512 // ROWS):
        rows = pl.ds(i * ROWS, ROWS)
        grad = d_h1[rows, :]
        normed = n_buf[rows, :]
        out = norm_backward(grad, normed, i_i1[rows, :], norms[0:1])
        d_h1[rows, :] = out
        halves(d_rows.at[1], i)[...] = out.astype(bf16)
        f_t[:, rows] = out.T.astype(bf16)
        sums[0] = sums[0] + columns(grad * normed)
        sums[1] = sums[1] + columns(grad)
    small[0] = sums[0]
    small[2] = sums[1]
    for n in range(4, 9):
        load(n).wait()

    def fetch_a(n):
        wx, wk = where(n)
        return pltpu.make_async_copy(i_weights.at[0, wx, wk], w_buf.at[n % 2], step_sems.at[n % 2, 0])

    def fetch_b(t):
        return pltpu.make_async_copy(
            i_weights.at[0, t // 2, t % 2], w_buf.at[t % 2], step_sems.at[t % 2, 0]
        )

    fetch_b(0).start()
    dq_t[1, pl.ds(HEAD_DIM, HEAD_DIM), :] = jnp.zeros((HEAD_DIM, 512), f32)

    def share(t):
        return remote(
            d_kv.at[t, :, :, :, 1 - place.k], d_kv_in.at[t], kv_send.at[t], kv_recv.at[t], place.device(dk=1)
        )

    events = Events(
        [
            step(1, 5),
            step(2, 0),
            step(2, 1),
            step(2, 2),
            step(2, 3),
            step(2, 4),
        ]
    )
    stop = events.spread(4, 6, 6)

    def attend(t, carry):
        @pl.when(t < 3)
        def _():
            fetch_b(t + 1).start()

        fetch_b(t).wait()
        left, right = out_weights(whole(w_buf.at[t % 2]))
        d_attn = d_rows[1].reshape(512, 768)
        d_ctx[0] = dot(d_attn, left).astype(bf16)
        d_ctx[1] = dot(d_attn, right).astype(bf16)
        point = 0
        for spot, (tile, half) in enumerate(HEAD_SPOTS):
            slope = slopes[3 * t + spot]
            key = keys[2 * t + tile].reshape(1024, 128)
            value = values[2 * t + tile].reshape(1024, 128)
            rows = slice(half * HEAD_DIM, (half + 1) * HEAD_DIM)
            key_t = key.astype(f32).T.astype(bf16)[rows]
            product = ctx[2 * t + tile].astype(f32) * d_ctx[tile].astype(f32)
            delta = jnp.sum(product.T[rows], axis=0, keepdims=True)
            for start in range(0, 512, CHUNK):
                cols = pl.ds(start, CHUNK)
                part = lane_half(q[2 * t + tile, cols, :], half)
                grad = lane_half(d_ctx[tile, cols, :], half)
                scores = dot(key, part, NT) - slope * dist[:, cols]
                probs = jnp.exp(scores - lse[t, pl.ds(spot, 1), cols])
                grad_probs = dot(value, grad, NT)
                term_v = dot(probs.astype(bf16), grad)
                grad_scores = (probs * (grad_probs - delta[:, start : start + CHUNK])).astype(bf16)
                term_k = dot(grad_scores, part)
                if half == 0 and start == 0:
                    acc_v[...] = term_v
                    acc_k[...] = term_k
                else:
                    acc_v[...] += term_v
                    acc_k[...] += term_k
                dq_t[tile, rows, cols] = dot(key_t, grad_scores)
                stop(t, point)
                point += 1
            if half == 1 or tile == 1:
                d_kv[t, 0, tile] = acc_k[...].astype(bf16).reshape(2, 2, 256, 128)
                d_kv[t, 1, tile] = acc_v[...].astype(bf16).reshape(2, 2, 256, 128)
        share(t).start()
        for tile in range(2):
            q[2 * t + tile] = (dq_t[tile].T * HEAD_DIM**-0.5).astype(bf16)
        return carry

    lax.fori_loop(0, 4, attend, 0)
    fetch_a(0).start()
    first = lax.broadcasted_iota(jnp.int32, (768, 128), 1) < HEAD_DIM

    def project(n, carry):
        dx = 1 - n % 2
        wx, wk = where(n)
        t = wx * 2 + wk

        @pl.when(n < 3)
        def _():
            fetch_a(n + 1).start()

        @pl.when(n < 2)
        def _():
            push(2, dx).wait_send()

        share(t).wait_recv()
        parts = [q[2 * t], q[2 * t + 1]]
        for kind in range(2):
            for tile in range(2):
                mine = d_kv[t, kind, tile, :, k].reshape(512, 128).astype(f32)
                mine = mine + d_kv_in[t, kind, tile].reshape(512, 128).astype(f32)
                parts.append(mine.astype(bf16))
        d_qkv = jnp.concatenate(parts, axis=1)
        d_w = dot(h1_t[...], d_qkv)
        left = dot(f_t[...], ctx[2 * t])
        right = swap_halves(dot(f_t[...], ctx[2 * t + 1]))
        tiles = [
            d_w[:, 0:128],
            jnp.where(first, d_w[:, 128:256], pltpu.roll(left, HEAD_DIM, 1)),
            d_w[:, 256:384],
            jnp.where(first, d_w[:, 384:512], left),
            d_w[:, 512:640],
            jnp.where(first, d_w[:, 640:768], right),
        ]
        put(12 + n, dx, jnp.concatenate(tiles, axis=1), slice(0, 768))

        @pl.when(n < 2)
        def _():
            push(3, dx).start()

        fetch_a(n).wait()
        d_h1[...] += dot(d_qkv, whole(w_buf.at[n % 2]), NT)
        for at in (2, 3):

            @pl.when(n == at)
            def _():
                rounds[3].pair_sum(3 - at)

        return carry

    lax.fori_loop(0, 4, project, 0)
    for i in range(512 // ROWS):
        rows = pl.ds(i * ROWS, ROWS)
        halves(d_rows.at[0], i)[...] = d_h1[rows, :].astype(bf16)
    swap(1).start()
    stay(1).start()
    total = jnp.concatenate(
        [jnp.sum(small[i], axis=0, keepdims=True) for i in range(4)]
        + [jnp.sum(squares[i], axis=0, keepdims=True) for i in range(4)],
        axis=0,
    )

    def spread(n):
        to = ({"dk": 1}, {"dx": 1}, {"dy": 1}, {"dz": 1}, {"dz": 2}, {"dz": 3})[n]
        src = small.at[min(n, 3)]
        return remote(src, small_in.at[n], s_send.at[n], s_recv.at[n], place.device(**to))

    small[0] = total
    for n in range(3):
        spread(n).start()
        spread(n).wait_recv()
        total = total + small_in[n]
        small[n + 1] = total
    for n in range(3, 6):
        spread(n).start()
    rounds[3].event(0)
    rounds[3].event(1)
    rounds[2].event(5, o_grads.at[1])
    for at in range(2, 6):
        rounds[3].event(at, o_grads.at[0])
    for n in range(3, 6):
        spread(n).wait_recv()
    result = jnp.zeros_like(total)
    for at in range(4):
        step_of = (place.z - at) % 4
        term = jnp.where(
            step_of == 0,
            total,
            jnp.where(step_of == 1, small_in[3], jnp.where(step_of == 2, small_in[4], small_in[5])),
        )
        result = result + term
    o_small[...] = result
    for n in range(6):
        spread(n).wait_send()
    for r in rounds:
        r.finish()
    for dx in range(2):
        push(3, dx).wait_send()
    for t in range(4):
        share(t).wait_send()
    for n in range(2):
        swap(n).wait()
        stay(n).wait()


def backward(span, slopes, saved, seg_col, seg_row, pos_row):
    f32, bf16 = jnp.float32, jnp.bfloat16
    any_space = pl.BlockSpec(memory_space=pl.ANY)
    vmem = pl.BlockSpec(memory_space=pltpu.VMEM)
    dma = pltpu.SemaphoreType.DMA
    (weights, norms, xs, cot, q, keys, values, ctx, lse, kept, h1b, n1, i1, n2, i2, out, squares) = saved
    h1b = h1b.reshape(2, 256, 768)
    out = out.reshape(2, 256, 768)
    in_specs = [pl.BlockSpec(memory_space=pltpu.SMEM), any_space, vmem] + [any_space] * 10
    in_specs += [vmem, any_space, vmem, any_space, vmem, vmem, vmem, vmem]
    rest = 96 - CUT
    return pl.pallas_call(
        partial(backward_kernel, span),
        out_shape=(
            jax.ShapeDtypeStruct((2, 256, 768), bf16),
            jax.ShapeDtypeStruct((2, 256, 768), bf16),
            jax.ShapeDtypeStruct((ROUNDS, 96, 768), f32),
            jax.ShapeDtypeStruct((8, 768), f32),
        ),
        in_specs=in_specs,
        out_specs=(any_space, any_space, vmem, vmem),
        scratch_shapes=[
            pltpu.VMEM((2, 4, 2, 96, 768), bf16),
            pltpu.VMEM((2, 3, 512, 256), bf16),
            pltpu.VMEM((768, 512), bf16),
            pltpu.VMEM((768, 512), bf16),
            pltpu.VMEM((3, 2, 256, 768), bf16),
            pltpu.VMEM((512, 768), f32),
            pltpu.VMEM((512, 768), f32),
            pltpu.VMEM((8, 512, 128), bf16),
            pltpu.VMEM((8, 2, 2, 256, 128), bf16),
            pltpu.VMEM((8, 2, 2, 256, 128), bf16),
            pltpu.VMEM((8, 512, 128), bf16),
            pltpu.VMEM((4, 8, 512), f32),
            pltpu.VMEM((1024, 512), f32),
            pltpu.VMEM((2, 512, 128), bf16),
            pltpu.VMEM((4, 2, 2, 2, 2, 256, 128), bf16),
            pltpu.VMEM((4, 2, 2, 2, 256, 128), bf16),
            pltpu.VMEM((2, 128, 512), f32),
            pltpu.VMEM((1024, 128), f32),
            pltpu.VMEM((1024, 128), f32),
            pltpu.VMEM((ROUNDS, 2, 4, 2, 96, 768), bf16),
            pltpu.VMEM((3, 2, 4, 2, 96, 768), bf16),
            pltpu.VMEM((2, 4, 2, 96, 768), bf16),
            pltpu.VMEM((ROUNDS, 2, 4, CUT, 768), bf16),
            pltpu.VMEM((ROUNDS, 4, 2, rest, 768), bf16),
            pltpu.VMEM((ROUNDS, 4, CUT, 768), bf16),
            pltpu.VMEM((ROUNDS, 4, rest, 768), bf16),
            pltpu.VMEM((ROUNDS, 3, 96, 768), bf16),
            pltpu.VMEM((4, 8, 768), f32),
            pltpu.VMEM((6, 8, 768), f32),
            dma((10,)),
            dma((2, 2)),
            dma((ROUNDS, 11)),
            dma((ROUNDS, 11)),
            dma((ROUNDS, 2, 2)),
            dma((6,)),
            dma((4,)),
            dma((4,)),
            dma((6,)),
            dma((6,)),
        ],
        compiler_params=pltpu.CompilerParams(
            collective_id=1, has_side_effects=True, vmem_limit_bytes=VMEM_LIMIT
        ),
        name="backward",
    )(
        slopes,
        weights,
        norms,
        xs,
        cot,
        q,
        keys,
        values,
        ctx,
        lse,
        kept,
        h1b,
        n1,
        i1,
        n2,
        i2,
        out,
        squares,
        seg_col,
        seg_row,
        pos_row,
    )


def local(
    tokens,
    segment_ids,
    query_key_value_weight,
    w_out,
    input_weight,
    w_down,
    norm_gains,
    norm_biases,
    cotangent,
):
    f32 = jnp.float32
    shard_rows = query_key_value_weight.shape[1]
    span = 96 // shard_rows
    groups = None
    if span > 1:
        count = lax.axis_size("fsdp")
        groups = [list(range(i, i + span)) for i in range(0, count, span)]
    place_x = lax.axis_index("tp") // 2
    place_k = lax.axis_index("tp") % 2
    block = lax.axis_index("fsdp") // span

    heads = query_key_value_weight.transpose(1, 0, 2).reshape(shard_rows, 3, 3, HEAD_DIM)
    w_out_t = w_out.T.reshape(shard_rows, 3, 1, HEAD_DIM)
    wa = jnp.concatenate([heads, w_out_t], axis=2).reshape(shard_rows, 1, 768)
    gate_up = input_weight.reshape(shard_rows, 2, 3, 256).transpose(0, 2, 1, 3)
    down = w_down.T.reshape(shard_rows, 3, 1, 256)
    wf = jnp.concatenate([gate_up, down], axis=2).reshape(shard_rows, 3, 768)
    shard = jnp.concatenate([wa, wf], axis=1).transpose(1, 0, 2)
    norms = jnp.concatenate([norm_gains, norm_biases], axis=0).astype(f32)
    if span > 1:
        shard = lax.all_gather(shard, "fsdp", axis=1, tiled=True, axis_index_groups=groups)
        norms = lax.all_gather(norms, "fsdp", axis=1, tiled=True, axis_index_groups=groups)
    norm_rows = lax.dynamic_update_slice(jnp.zeros((8, 768), f32), norms, (0, block * 96))

    segment = lax.dynamic_index_in_dim(segment_ids, place_x, 0, keepdims=False)
    seg_col = segment.reshape(1024, 1)
    seg_row = lax.dynamic_index_in_dim(segment.reshape(2, 2, 256), place_k, 1, keepdims=False)
    seg_row = seg_row.reshape(1, 512)
    pos_row = (
        lax.broadcasted_iota(jnp.int32, (2, 256), 0) * 512
        + place_k * 256
        + lax.broadcasted_iota(jnp.int32, (2, 256), 1)
    )
    pos_row = pos_row.reshape(1, 512).astype(f32)
    slopes = jnp.exp2(-8.0 * (jnp.arange(HEADS).astype(f32) + 1.0) / HEADS)

    saved = forward(span, slopes, shard, norm_rows, tokens, cotangent, seg_col, seg_row, pos_row)
    layer_out, grad_tokens, grads, small = backward(span, slopes, saved, seg_col, seg_row, pos_row)

    if span > 1:
        grads = lax.psum_scatter(
            grads, "fsdp", scatter_dimension=1, tiled=True, axis_index_groups=groups
        )
        small = lax.psum(small, "fsdp", axis_index_groups=groups)
    grads_a = grads[0].reshape(shard_rows, 3, 4, HEAD_DIM)
    grads_f = grads[1:].reshape(3, shard_rows, 3, 256)
    shard_start = lax.axis_index("fsdp") * shard_rows
    mine = lax.dynamic_slice_in_dim(small[:4], shard_start, shard_rows, 1)
    cells = float(lax.axis_size("fsdp") * 2 * 1024 * 768)
    return (
        layer_out,
        grad_tokens,
        grads_a[:, :, :3].transpose(1, 0, 2, 3).reshape(3, shard_rows, 192),
        grads_a[:, :, 3].reshape(shard_rows, 192).T,
        grads_f[:, :, :2].transpose(1, 2, 0, 3).reshape(shard_rows, 2, 768),
        grads_f[:, :, 2].transpose(0, 2, 1).reshape(768, shard_rows),
        mine[:2],
        mine[2:],
        jnp.sqrt(jnp.sum(small[4:], axis=1) / cells),
    )


def solution(mesh):
    placed = (
        P("fsdp", "tp", None),
        P("fsdp", None),
        P(None, "fsdp", "tp"),
        P("tp", "fsdp"),
        P("fsdp", None, "tp"),
        P("tp", "fsdp"),
        P(None, "fsdp"),
        P(None, "fsdp"),
        P("fsdp", "tp", None),
    )
    return jax.shard_map(
        local,
        mesh=mesh,
        in_specs=placed,
        out_specs=(
            P("fsdp", "tp", None),
            P("fsdp", "tp", None),
            P(None, "fsdp", "tp"),
            P("tp", "fsdp"),
            P("fsdp", None, "tp"),
            P("tp", "fsdp"),
            P(None, "fsdp"),
            P(None, "fsdp"),
            P(),
        ),
        check_vma=False,
    )
```

time: 757 us -> 278 us (0.37)
  waiting for transfers between devices: 339 us -> 0 us
  Pallas kernels: 0 us -> 257 us
  blocking collectives: 151 us -> 0 us
  matrix products: 142 us -> 0 us
  other arithmetic: 58.3 us -> 4.86 us
  local copies, waits for them, and re-layouts: 43.7 us -> 15.6 us
  between operations: 16 us -> 0.84 us
    pallas_call x0 -> x2, Pallas kernels: none -> 257 us  [the longest x1 145 us: backward(): pl.pallas_call(partial(backward_kernel, span), out_shape=(jax.ShapeDtypeS...]
    reduce_scatter x6 -> x0, waiting for transfers between devices: 158 us -> none  [the longest x1 46.2 us: local(): lax.psum_scatter(input_weight_gradient.astype(jnp.bfloat16), 'fsdp', scat...]
    dot_general x40 -> x0, matrix products: 142 us -> none  [the longest x8 32.8 us: block_scores(): jnp.einsum('qhe,khe->hqk', query_blk, keys, preferred_element_type=jnp.fl...]
    all_gather x4 -> x0, blocking collectives: 111 us -> none  [the longest x1 38.8 us: local(): lax.all_gather(query_key_value_weight, 'fsdp', axis=1, tiled=True)]
    all_gather x6 -> x0, waiting for transfers between devices: 97.7 us -> none  [the longest x1 29 us: local(): lax.all_gather(hidden_state_first.astype(jnp.bfloat16), 'tp', axis=1, til...]
    unnamed x16 -> x0, waiting for transfers between devices: 83.5 us -> none
    psum x1 -> x0, blocking collectives: 40 us -> none  [local(): lax.psum((gain_terms, bias_terms, square_terms), ('fsdp', 'tp'))]
    convert_element_type x21 -> x1, other arithmetic: 31.4 us -> 0.68 us  [local(): norms = jnp.concatenate([norm_gains, norm_biases], axis=0).astype(f32)]
  transfers between devices with their start and end apart: 14 -> 0, of which waited for: 11 -> 0; matrix products, arithmetic and copies ran while one was open for 19% -> 0% of each run, Pallas kernels for 0% -> 0%
where the time goes in v2:
time: 278 us
  Pallas kernels  257 us (92%)
  local copies, waits for them, and re-layouts  15.6 us (6%)
  other arithmetic  4.86 us (2%)
    pallas_call x1, Pallas kernels, backward(): pl.pallas_call(partial(backward_kernel, span), out_shape=(jax.ShapeDtypeS...  145 us
    pallas_call x1, Pallas kernels, forward(): pl.pallas_call(partial(forward_kernel, span), out_shape=tuple((jax.ShapeD...  111 us
    unnamed x17, local copies, waits for them, and re-layouts  5.58 us

profile of v2, /device:TPU:0, one launch (start us, length us, event | category | flops | bytes accessed | tf_op | source)
XLA Modules:
  0.0 277.9 jit_solution(9498640481293507125)
XLA Ops:
  0.6 0.0 copy-start.2
  0.7 0.5 multiply_exponential_fusion.slopes
  1.2 0.1 convert_bitcast_fusion
  1.3 0.6 copy.42
  1.9 0.7 maximum_convert_fusion
  2.6 0.7 dynamic-slice_reduce_fusion
  3.3 0.6 constant_dynamic-slice_fusion.1
  3.9 0.2 dynamic_update_slice.3.norm_rows
  4.1 0.0 copy-start.3
  4.1 1.1 copy.26
  5.2 0.8 pad_maximum_fusion.1
  6.1 0.1 copy.29
  6.2 1.0 reshape.102
  7.2 0.0 copy-done.2
  7.2 0.1 reshape.101
  7.4 0.4 pad_maximum_fusion
  7.8 0.0 copy-done.3
  7.8 0.5 copy.28
  8.3 0.5 reshape.103
  8.8 0.9 maximum_bitcast_fusion.shard
  9.6 1.0 copy.30.seg_col
  10.7 111.3 %forward.1 = (bf16[4,2,2,4,2,96,768]{6,5,4,3,2,1,0:T(8,128)(2,1)}, f32[8,768]{1,0:T(8,128)}, bf16[2,256,768]{2,1,0:T(8,128)(2,1)}, bf16[2,256,768]{2,1,0:T(8,128...) custom-call(f32[12]{0:T(128)} %multiply_exponential_fusion.slopes, ...), custom_call_target="tpu_custom_call" | custom-call | tf_op jit(solution)/shard_map/forward/pallas_call | solution.py:555
  122.0 145.3 %backward.1 = (bf16[2,256,768]{2,1,0:T(8,128)(2,1)}, bf16[2,256,768]{2,1,0:T(8,128)(2,1)}, f32[4,96,768]{2,1,0:T(8,128)}, f32[8,768]{1,0:T(8,128)}) custom-call(f32[12]{0:T(128)} %multiply_exponential_fusion.slopes, bf16[4,2,2,4,2,96,768]{6,5,4,3,2,1,0:T(8,128)(2,1)} %get-tuple-element.30.i_weights, f32[8,768]{1,0:T(8,128)} %get-tuple-element.31.norms, ...), custom_call_target="tpu_custom_call" | custom-call | tf_op jit(solution)/shard_map/backward/pallas_call | solution.py:1130
  267.3 0.9 slice_reduce_fusion
  268.2 0.5 multiply_sqrt_fusion
  268.7 0.1 constant_dynamic-slice_fusion
  268.8 0.6 fusion
  269.4 1.0 slice.30
  270.4 1.2 slice.33
  271.6 0.2 copy.32
  271.8 0.7 slice.41
  272.4 0.9 copy.35
  273.3 0.5 reshape.110
  273.8 0.3 slice.43
  274.1 0.0 copy-start.1
  274.1 0.2 slice_bitcast_fusion
  274.3 1.0 copy.40
  275.3 0.0 copy-start
  275.4 0.7 copy.41
  276.1 0.0 copy-done.1
  276.1 0.9 copy.48
  277.0 0.0 copy-done
  277.0 0.9 copy.49
  (6 shorter events, 0.1 us)
Async XLA Ops:
  0.6 6.5 %copy-start.2 = (bf16[96,2,768]{2,1,0:T(2,128)(2,1)S(1)}, bf16[96,2,768]{2,1,0:T(2,128)(2,1)}, u32[]{:S(2)}) copy-start(bf16[96,2,768]{2,1,0:T(2,128)(2,1)} %param.13) | copy-start | bytes 884740
  4.1 3.7 %copy-start.3 = (f32[8,768]{1,0:T(8,128)}, f32[8,768]{1,0:T(8,128)S(1)}, u32[]{:S(2)}) copy-start(f32[8,768]{1,0:T(8,128)S(1)} %dynamic_update_slice.3.norm_rows) | copy-start | bytes 73732
  274.1 2.0 copy-start.1
  275.3 1.6 copy-start

commit v3 on v2

--- a/solution.py
+++ b/solution.py
@@ -13,7 +13,6 @@
 VMEM_LIMIT = 63 << 20
 norm_eps = 1e-05
 ROUNDS = 4
-CUT = 48
 NT = (((1,), (1,)), ((), ()))
 NN = (((1,), (0,)), ((), ()))
 CHUNK = 256
@@ -60,6 +59,17 @@
     )
 
 
+PARTS = {
+    "a": pl.ds(0, 32),
+    "c": pl.ds(32, 16),
+    "ac": pl.ds(0, 48),
+    "b": pl.ds(48, 32),
+    "d": pl.ds(80, 16),
+    "bd": pl.ds(48, 48),
+    "": pl.ds(0, 96),
+}
+
+
 def dot(a, b, dims=NN):
     return lax.dot_general(a, b, dims, preferred_element_type=jnp.float32)
 
@@ -84,29 +94,31 @@
     names = ("z1", "z2", "z3", "ax", "by", "ay0", "bx0", "ay1", "bx1") + tuple(
         "d%d" % i for i in range(7)
     )
+    names += ("cx", "cz1", "cz2", "cz3", "dy", "dz1", "dz2", "dz3")
     lines = {
         "ax": ((0, 0, "a"), {"dx": 1}),
         "by": ((0, 0, "b"), {"dy": 1}),
-        "ay0": ((0, 0, "a"), {"dy": 1}),
-        "bx0": ((0, 0, "b"), {"dx": 1}),
-        "ay1": ((1, 0, "a"), {"dy": 1}),
-        "bx1": ((0, 1, "b"), {"dx": 1}),
+        "ay0": ((0, 0, "ac"), {"dy": 1}),
+        "bx0": ((0, 0, "bd"), {"dx": 1}),
+        "ay1": ((1, 0, "ac"), {"dy": 1}),
+        "bx1": ((0, 1, "bd"), {"dx": 1}),
         "d0": ((0, 0, ""), {"dk": 1}),
-        "d1": ((1, 0, "a"), {"dk": 1}),
-        "d2": ((0, 1, "b"), {"dk": 1}),
-        "d3": ((0, 1, "a"), {"dk": 1}),
-        "d4": ((1, 0, "b"), {"dk": 1}),
-        "d5": ((1, 1, "a"), {"dk": 1}),
-        "d6": ((1, 1, "b"), {"dk": 1}),
+        "d1": ((1, 0, "ac"), {"dk": 1}),
+        "d2": ((0, 1, "bd"), {"dk": 1}),
+        "d3": ((0, 1, "ac"), {"dk": 1}),
+        "d4": ((1, 0, "bd"), {"dk": 1}),
+        "d5": ((1, 1, "ac"), {"dk": 1}),
+        "d6": ((1, 1, "bd"), {"dk": 1}),
     }
     steps = {
-        2: ("ax", "ay1", "d1"),
-        3: ("by", "bx1", "d2"),
-        4: ("ay0", "d3"),
-        5: ("bx0", "d4"),
-        6: ("ay1", "d5"),
-        7: ("bx1", "d6"),
+        3: (("ax", "cz1", "cz2", "cz3"), ("ay1", "d1")),
+        4: (("by", "dz1", "dz2", "dz3"), ("bx1", "d2")),
+        5: (("ay0",), ("d3",)),
+        6: (("bx0",), ("d4",)),
+        7: (("ay1",), ("d5",)),
+        8: (("bx1",), ("d6",)),
     }
+    last = 9
 
     def __init__(self, place, own, out, send, recv, keep):
         self.place, self.own, self.out = place, own, out
@@ -114,18 +126,30 @@
 
     def line(self, dx, dy, part):
         x, y, z, k = self.place.shifted(dx, dy)
-        rows = {"a": pl.ds(0, CUT), "b": pl.ds(CUT, 96 - CUT), "": pl.ds(0, 96)}[part]
-        return self.out.at[x, k, :, y, rows, :]
+        return self.out.at[x, k, :, y, PARTS[part], :]
 
     def copy(self, name):
         place = self.place
         at = self.names.index(name)
         send, recv = self.send.at[at], self.recv.at[at]
+        x, y, z, k = place.shifted()
         if name[0] == "z":
-            x, y, z, k = place.shifted()
             return remote(
                 self.own, self.out.at[x, k, z, y], send, recv, place.device(dz=int(name[1]))
             )
+        if name in ("cx", "dy"):
+            rows = PARTS[name[0]]
+            return remote(
+                self.own.at[rows, :],
+                self.out.at[x, k, z, y, rows, :],
+                send,
+                recv,
+                place.device(**{"d" + name[1]: 1}),
+            )
+        if name[:2] in ("cz", "dz"):
+            x, y, z, k = place.shifted(dx=1) if name[0] == "c" else place.shifted(dy=1)
+            ref = self.out.at[x, k, z, y, PARTS[name[0]], :]
+            return remote(ref, ref, send, recv, place.device(dz=int(name[2])))
         where, to = self.lines[name]
         ref = self.line(*where)
         return remote(ref, ref, send, recv, place.device(**to))
@@ -137,16 +161,19 @@
     def event(self, n):
         if n == 0:
             self.kept().start()
-            self.start("z1", "z2", "z3")
+            self.start("cx", "dy", "z1", "z2", "z3")
         elif n == 1:
+            self.wait("cx", "dy")
+            self.start("cz1", "cz2", "cz3", "dz1", "dz2", "dz3")
+        elif n == 2:
             self.kept().wait()
             self.wait("z1", "z2", "z3")
             self.start("ax", "by", "ay0", "bx0", "d0")
-        elif n == 8:
-            self.wait(*self.names[9:])
+        elif n == 9:
+            self.wait(*["d%d" % i for i in range(7)])
         else:
-            self.wait(self.steps[n][0])
-            self.start(*self.steps[n][1:])
+            self.wait(*self.steps[n][0])
+            self.start(*self.steps[n][1])
 
 
 class NormGather(Copies):
@@ -214,11 +241,42 @@
     return pltpu.roll(tile.astype(jnp.float32), HEAD_DIM, 1)
 
 
-def fill_distance(dist, seg_col, seg_row, pos_row):
-    keys, queries = dist.shape
-    key_pos = lax.broadcasted_iota(jnp.int32, (keys, queries), 0).astype(jnp.float32)
-    gap = jnp.abs(key_pos - pos_row[...])
-    dist[...] = jnp.where(seg_col[...] == seg_row[...], gap, 1e30)
+def fill_distance(dist, segments, place):
+    row = segments[pl.ds(place.x, 1), :].astype(jnp.float32)
+    column = jnp.broadcast_to(row, (8, 1024)).T[:, 0:1]
+    for s in range(2):
+        first = (2 * s + place.k) * 256
+        mine = segments[pl.ds(place.x, 1), pl.ds(pl.multiple_of(first, 256), 256)].astype(jnp.float32)
+        gap = lax.broadcasted_iota(jnp.int32, (1024, 256), 0) - (
+            lax.broadcasted_iota(jnp.int32, (1024, 256), 1) + first
+        )
+        dist[:, s * 256 : (s + 1) * 256] = jnp.where(
+            column == mine, jnp.abs(gap).astype(jnp.float32), 1e30
+        )
+
+
+def pack_attention(raw, shard):
+    qkv, w_out = raw[0], raw[1]
+    turned = w_out[...].astype(jnp.float32).T
+    for c in range(3):
+        shard[0, :, c * 256 : c * 256 + 128] = qkv[c, :, 0:128]
+        shard[0, :, c * 256 + 128 : c * 256 + 256] = jnp.concatenate(
+            [
+                qkv[c, :, 128:192].astype(jnp.float32),
+                turned[:, c * HEAD_DIM : (c + 1) * HEAD_DIM],
+            ],
+            axis=1,
+        ).astype(jnp.bfloat16)
+
+
+def pack_feed(raw, shard):
+    w_in, w_down = raw[2], raw[3]
+    turned = w_down[...].astype(jnp.float32).T.astype(jnp.bfloat16)
+    for r in range(3):
+        units = slice(r * 256, (r + 1) * 256)
+        shard[1 + r, :, 0:256] = w_in[:, 0, units]
+        shard[1 + r, :, 256:512] = w_in[:, 1, units]
+        shard[1 + r, :, 512:768] = turned[:, units]
 
 
 def out_weights(w):
@@ -270,13 +328,12 @@
 def forward_kernel(
     span,
     slopes,
-    shard,
-    norm_rows,
+    raw,
+    gains,
+    biases,
     tok,
     cot,
-    seg_col,
-    seg_row,
-    pos_row,
+    segments,
     o_weights,
     o_norms,
     o_x,
@@ -294,11 +351,17 @@
     o_i2,
     o_out,
     o_squares,
+    shard,
+    norm_rows,
     weights,
     norms,
     xs,
+    q,
     keys,
     values,
+    ctx,
+    h1b,
+    n1,
     dist,
     out_t,
     acc,
@@ -348,37 +411,54 @@
             (xs, o_x),
             (keys, o_k),
             (values, o_v),
+            (q, o_q),
+            (ctx, o_ctx),
+            (h1b, o_h1b),
+            (n1, o_n1),
         )[n]
         return pltpu.make_async_copy(src, dst, store_sems.at[n])
 
+    if len(raw) > 1:
+        pack_attention(raw, shard)
+    else:
+        shard[...] = raw[0][...]
     place.greet(ALL_PEERS)
-    swap(0).start()
-    stay(0).start()
-    stay(1).start()
+    rounds[0].event(0)
+    for n in range(2):
+        swap(n).start()
+        stay(n).start()
+    norm_rows[...] = jnp.zeros_like(norm_rows)
+    norm_rows[0:2, 0:96] = gains[...].astype(f32)
+    norm_rows[2:4, 0:96] = biases[...].astype(f32)
+    block = place.z * 2 + place.y
+    norm_rows[...] = pltpu.roll(norm_rows[...], block * 96, 1)
     norm_gather.kept().start()
     norm_gather.start("z1", "z2", "z3")
+    if len(raw) > 1:
+        pack_feed(raw, shard)
 
     def step(r, n):
         def go():
             rounds[r].event(n)
-            if n == 8:
+            if n == GatherRound.last:
                 store(r).start()
 
         return go
 
-    order = [(0, 0), (0, 1), (1, 0), (0, 2), (0, 3), (1, 1), (2, 0), (0, 4), (0, 5), (0, 6), (0, 7), (0, 8)]
-    order += [(1, 2), (1, 3), (2, 1), (3, 0), (1, 4), (1, 5), (1, 6), (1, 7), (2, 2), (2, 3), (3, 1), (1, 8)]
-    order += [(2, 4), (2, 5), (2, 6), (2, 7), (3, 2), (3, 3), (2, 8)]
-    order += [(3, 4), (3, 5), (3, 6), (3, 7), (3, 8)]
+    order = [(0, 1), (0, 2), (1, 0), (1, 1), (0, 3), (0, 4), (1, 2), (2, 0), (2, 1)]
+    order += [(0, 5), (0, 6), (0, 7), (0, 8), (0, 9)]
+    begun = len(order)
+    order += [(1, 3), (1, 4), (2, 2), (3, 0), (3, 1), (1, 5), (1, 6), (1, 7), (1, 8), (2, 3), (2, 4), (3, 2), (1, 9)]
+    order += [(2, 5), (2, 6), (2, 7), (2, 8), (3, 3), (3, 4), (2, 9)]
+    order += [(3, 5), (3, 6), (3, 7), (3, 8), (3, 9)]
     events = Events(step(*at) for at in order)
-    events.steps.insert(-5, lambda: swap(1).start())
-
-    events.run(2)
-    fill_distance(dist, seg_col, seg_row, pos_row)
+
+    events.run(1)
+    fill_distance(dist, segments, place)
     norm_gather.kept().wait()
     norm_gather.wait("z1", "z2", "z3")
     norm_gather.start("y")
-    events.run(10)
+    events.run(begun - 1)
     swap(0).wait_recv()
     stay(0).wait()
     store(4).start()
@@ -393,7 +473,7 @@
             out = dot(xs[s], w).astype(bf16)
             for i in range(2):
                 cols = slice(i * 128, i * 128 + 128)
-                o_q[2 * t + i, pl.ds(s * 256, 256), :] = out[:, cols] * bf16(HEAD_DIM**-0.5)
+                q[2 * t + i, pl.ds(s * 256, 256), :] = out[:, cols] * bf16(HEAD_DIM**-0.5)
                 keys[2 * t + i, s, k] = out[:, 256 + i * 128 : 384 + i * 128]
                 values[2 * t + i, s, k] = out[:, 512 + i * 128 : 640 + i * 128]
         share(t, 0).start()
@@ -402,7 +482,7 @@
 
     lax.fori_loop(0, 4, project, 0)
     out_t[1, pl.ds(HEAD_DIM, HEAD_DIM), :] = jnp.zeros((HEAD_DIM, 512), f32)
-    stop = events.spread(4, 7, 12)
+    stop = events.spread(4, 7, 13)
 
     def attend(t, carry):
         share(t, 0).wait_recv()
@@ -415,7 +495,7 @@
             value_t = values[2 * t + tile].reshape(1024, 128).astype(f32).T.astype(bf16)[rows]
             for start in range(0, 512, CHUNK):
                 cols = pl.ds(start, CHUNK)
-                part = lane_half(o_q[2 * t + tile, cols, :], half)
+                part = lane_half(q[2 * t + tile, cols, :], half)
                 scores = dot(key, part, NT) - slope * dist[:, cols]
                 peak = jnp.max(scores, axis=0, keepdims=True)
                 expo = jnp.exp(scores - peak)
@@ -425,9 +505,9 @@
                 stop(t, point)
                 point += 1
         for tile in range(2):
-            o_ctx[2 * t + tile] = out_t[tile].T.astype(bf16)
+            ctx[2 * t + tile] = out_t[tile].T.astype(bf16)
         left, right = out_weights(whole(weights.at[0, t // 2, t % 2]))
-        mixed = dot(o_ctx[2 * t], left, NT) + dot(o_ctx[2 * t + 1], right, NT)
+        mixed = dot(ctx[2 * t], left, NT) + dot(ctx[2 * t + 1], right, NT)
 
         @pl.when(t == 0)
         def _():
@@ -441,8 +521,8 @@
         return carry
 
     lax.fori_loop(0, 4, attend, 0)
-    store(5).start()
-    store(6).start()
+    for n in range(5, 9):
+        store(n).start()
     norm_gather.wait("y")
     norm_sum = jnp.sum(norms[...].reshape(8, 8, 768), axis=0)
     o_norms[...] = norm_sum
@@ -454,8 +534,8 @@
         normed, inv = norm_stats(resid)
         value = normed * norm_sum[0:1] + norm_sum[2:3]
         h1[rows, :] = value
-        o_h1b[rows, :] = value.astype(bf16)
-        o_n1[rows, :] = normed
+        h1b[rows, :] = value.astype(bf16)
+        n1[rows, :] = normed
         o_i1[rows, :] = inv
         acc[rows, :] = jnp.zeros_like(attn)
         if_first = jnp.where(i == 0, 0.0, 1.0)
@@ -464,9 +544,11 @@
 
     o_squares[...] = jnp.zeros_like(o_squares)
     row_blocks(first_norm)
+    store(9).start()
+    store(10).start()
 
     stop_f = events.place(
-        12, 2, {1: 1, 2: 1, 3: 1, 4: 1, 5: 1, 6: 1, 8: 1, 9: 1, 11: 1, 12: 1, 13: 1, 14: 1, 16: 1}
+        12, 2, {1: 1, 2: 1, 3: 1, 4: 1, 5: 1, 6: 1, 8: 1, 9: 1, 11: 1, 13: 1, 14: 1, 16: 1}
     )
     assert not events.steps
 
@@ -485,7 +567,7 @@
         for start in range(0, 512, CHUNK):
             rows = pl.ds(start, CHUNK)
             w = whole(ref)
-            projected = dot(o_h1b[rows, :], w[:, :512])
+            projected = dot(h1b[rows, :], w[:, :512])
             gate, up = projected[:, :256], projected[:, 256:]
             cdf = 0.5 + 0.5 * lax.erf(gate * (0.5**0.5))
             pdf = jnp.exp(-0.5 * gate * gate) * 0.3989422804014327
@@ -524,11 +606,15 @@
     for t in range(4):
         for n in range(2):
             share(t, n).wait_send()
-    for n in range(7):
+    for n in range(11):
         store(n).wait()
 
 
-def forward(span, slopes, shard, norm_rows, tok, cot, seg_col, seg_row, pos_row):
+def forward_refs(span, count, *refs):
+    forward_kernel(span, refs[0], refs[1 : 1 + count], *refs[1 + count :])
+
+
+def forward(span, slopes, raw, gains, biases, tok, cot, segments):
     f32, bf16 = jnp.float32, jnp.bfloat16
     any_space = pl.BlockSpec(memory_space=pl.ANY)
     vmem = pl.BlockSpec(memory_space=pltpu.VMEM)
@@ -537,14 +623,14 @@
         ((8, 768), f32, vmem),
         ((2, 256, 768), bf16, any_space),
         ((2, 256, 768), bf16, any_space),
-        ((8, 512, 128), bf16, vmem),
+        ((8, 512, 128), bf16, any_space),
         ((8, 2, 2, 256, 128), bf16, any_space),
         ((8, 2, 2, 256, 128), bf16, any_space),
-        ((8, 512, 128), bf16, vmem),
+        ((8, 512, 128), bf16, any_space),
         ((4, 8, 512), f32, vmem),
         ((12, 3, 512, 256), bf16, any_space),
-        ((512, 768), bf16, vmem),
-        ((512, 768), f32, vmem),
+        ((512, 768), bf16, any_space),
+        ((512, 768), f32, any_space),
         ((512, 1), f32, vmem),
         ((512, 768), f32, vmem),
         ((512, 1), f32, vmem),
@@ -552,24 +638,31 @@
         ((4, 8, 768), f32, vmem),
     )
     dma = pltpu.SemaphoreType.DMA
+    copies = len(GatherRound.names)
     return pl.pallas_call(
-        partial(forward_kernel, span),
+        partial(forward_refs, span, len(raw)),
         out_shape=tuple(jax.ShapeDtypeStruct(s, d) for s, d, _ in outs),
-        in_specs=[pl.BlockSpec(memory_space=pltpu.SMEM)] + [vmem] * 7,
+        in_specs=[pl.BlockSpec(memory_space=pltpu.SMEM)] + [vmem] * (len(raw) + 5),
         out_specs=tuple(spec for _, _, spec in outs),
         scratch_shapes=[
+            pltpu.VMEM((ROUNDS, 96, 768), bf16),
+            pltpu.VMEM((8, 768), f32),
             pltpu.VMEM((ROUNDS, 2, 2, 4, 2, 96, 768), bf16),
             pltpu.VMEM((4, 2, 8, 768), f32),
             pltpu.VMEM((2, 256, 768), bf16),
+            pltpu.VMEM((8, 512, 128), bf16),
             pltpu.VMEM((8, 2, 2, 256, 128), bf16),
             pltpu.VMEM((8, 2, 2, 256, 128), bf16),
+            pltpu.VMEM((8, 512, 128), bf16),
+            pltpu.VMEM((512, 768), bf16),
+            pltpu.VMEM((512, 768), f32),
             pltpu.VMEM((1024, 512), f32),
             pltpu.VMEM((2, 128, 512), f32),
             pltpu.VMEM((512, 768), f32),
             pltpu.VMEM((512, 768), f32),
             pltpu.VMEM((2, 3, 512, 256), bf16),
-            dma((ROUNDS, 16)),
-            dma((ROUNDS, 16)),
+            dma((ROUNDS, copies)),
+            dma((ROUNDS, copies)),
             dma((ROUNDS,)),
             dma((4,)),
             dma((4,)),
@@ -577,58 +670,66 @@
             dma((6,)),
             dma((4, 2)),
             dma((4, 2)),
-            dma((7,)),
+            dma((11,)),
             dma((2,)),
         ],
         compiler_params=pltpu.CompilerParams(
             collective_id=0, has_side_effects=True, vmem_limit_bytes=VMEM_LIMIT
         ),
         name="forward",
-    )(slopes, shard, norm_rows, tok, cot, seg_col, seg_row, pos_row)
+    )(slopes, *raw, gains, biases, tok, cot, segments)
 
 
 class ScatterRound(Copies):
-    names = ("ay1", "bx", "ay0", "ax", "by", "az1", "az2", "az3", "bz1", "bz2", "bz3")
-
-    def __init__(self, place, held, twin, stage, land_ay, land_bx, land_ax, land_by, land_z, send, recv, pair):
+    names = ("ay1", "bx", "ay0", "ax", "by", "cx", "dy") + tuple(
+        part + "z%d" % step for part in "abcd" for step in (1, 2, 3)
+    )
+
+    def __init__(self, place, held, twin, stage, landing, send, recv, pair):
         self.place, self.held, self.twin, self.stage = place, held, twin, stage
-        self.land_ay, self.land_bx, self.land_ax = land_ay, land_bx, land_ax
-        self.land_by, self.land_z = land_by, land_z
+        self.ay, self.bx, self.ax, self.by, self.z, self.cz, self.dz, self.last = landing
         self.send, self.recv, self.pair = send, recv, pair
 
     def copy(self, name):
-        p = self.place
+        p, held = self.place, self.held
         at = self.names.index(name)
-        send, recv = self.send.at[at], self.recv.at[at]
-        a, b = pl.ds(0, CUT), pl.ds(CUT, 96 - CUT)
+        a, b, c, d = (PARTS[part] for part in "abcd")
+        step = int(name[2]) if name[1] == "z" else 0
+        far = (p.z + step) % 4
+        ac, bd = PARTS["ac"], PARTS["bd"]
         if name in ("ay1", "ay0"):
             dx = int(name[2])
-            return remote(
-                self.held.at[dx, :, 1 - p.y, a, :], self.land_ay.at[dx], send, recv, p.device(dy=1)
-            )
-        if name == "bx":
-            return remote(self.held.at[1, :, :, b, :], self.land_bx, send, recv, p.device(dx=1))
-        if name == "ax":
-            return remote(self.held.at[1, :, p.y, a, :], self.land_ax, send, recv, p.device(dx=1))
-        if name == "by":
-            return remote(self.held.at[0, :, 1 - p.y, b, :], self.land_by, send, recv, p.device(dy=1))
-        step = int(name[2])
-        rows = a if name[0] == "a" else b
-        return remote(
-            self.held.at[0, (p.z + step) % 4, p.y, rows, :],
-            self.land_z.at[step - 1, rows, :],
-            send,
-            recv,
-            p.device(dz=step),
-        )
+            src, dst, to = held.at[dx, :, 1 - p.y, ac, :], self.ay.at[dx], {"dy": 1}
+        elif name == "bx":
+            src, dst, to = held.at[1, :, :, bd, :], self.bx, {"dx": 1}
+        elif name == "ax":
+            src, dst, to = held.at[1, :, p.y, a, :], self.ax, {"dx": 1}
+        elif name == "by":
+            src, dst, to = held.at[0, :, 1 - p.y, b, :], self.by, {"dy": 1}
+        elif name == "cx":
+            src, dst, to = held.at[1, p.z, p.y, c, :], self.last.at[0], {"dx": 1}
+        elif name == "dy":
+            src, dst, to = held.at[0, p.z, 1 - p.y, d, :], self.last.at[1], {"dy": 1}
+        elif name[0] == "c":
+            src, dst, to = held.at[:, far, p.y, c, :], self.cz.at[step - 1], {"dz": step}
+        elif name[0] == "d":
+            src, dst, to = held.at[0, far, :, d, :], self.dz.at[step - 1], {"dz": step}
+        else:
+            rows = PARTS[name[0]]
+            into = pl.ds(0, 32) if name[0] == "a" else pl.ds(32, 32)
+            src, dst, to = held.at[0, far, p.y, rows, :], self.z.at[step - 1, into, :], {"dz": step}
+        return remote(src, dst, self.send.at[at], self.recv.at[at], p.device(**to))
 
     def push(self, dx):
         return remote(
             self.stage.at[dx], self.twin.at[dx], self.pair.at[0, dx], self.pair.at[1, dx], self.place.device(dk=1)
         )
 
-    def add(self, ref, other):
-        ref[...] = (ref[...].astype(jnp.float32) + other[...].astype(jnp.float32)).astype(jnp.bfloat16)
+    def add(self, ref, *others):
+        total = ref[...].astype(jnp.float32)
+        for other in others:
+            total = total + other[...].astype(jnp.float32)
+        ref[...] = total.astype(jnp.bfloat16)
 
     def pair_sum(self, dx):
         self.push(dx).wait_recv()
@@ -644,34 +745,51 @@
             self.start("ay0")
 
     def event(self, n, out=None):
-        p = self.place
-        a, b = pl.ds(0, CUT), pl.ds(CUT, 96 - CUT)
+        p, held = self.place, self.held
+        a, b, c, d = (PARTS[part] for part in "abcd")
+        ac, bd = PARTS["ac"], PARTS["bd"]
         if n == 0:
             self.wait("ay1")
-            self.add(self.held.at[1, :, p.y, a, :], self.land_ay.at[1])
+            self.add(held.at[1, :, p.y, ac, :], self.ay.at[1])
             self.start("ax")
         elif n == 1:
             self.wait("bx")
-            self.add(self.held.at[0, :, 1 - p.y, b, :], self.land_bx.at[:, 1 - p.y])
+            self.add(held.at[0, :, 1 - p.y, bd, :], self.bx.at[:, 1 - p.y])
             self.start("by")
-            self.add(self.held.at[0, :, p.y, b, :], self.land_bx.at[:, p.y])
+            self.add(held.at[0, :, p.y, bd, :], self.bx.at[:, p.y])
+            self.start("dz1", "dz2", "dz3")
         elif n == 2:
             self.wait("ay0")
-            self.add(self.held.at[0, :, p.y, a, :], self.land_ay.at[0])
+            self.add(held.at[0, :, p.y, ac, :], self.ay.at[0])
+            self.start("cz1", "cz2", "cz3")
         elif n == 3:
             self.wait("ax")
-            self.add(self.held.at[0, :, p.y, a, :], self.land_ax)
+            self.add(held.at[0, :, p.y, a, :], self.ax)
             self.start("az1", "az2", "az3")
         elif n == 4:
             self.wait("by")
-            self.add(self.held.at[0, :, p.y, b, :], self.land_by)
+            self.add(held.at[0, :, p.y, b, :], self.by)
             self.start("bz1", "bz2", "bz3")
+        elif n == 5:
+            self.wait("cz1", "cz2", "cz3", "dz1", "dz2", "dz3")
+            self.add(held.at[1, p.z, p.y, c, :], *[self.cz.at[i, 1] for i in range(3)])
+            self.start("cx")
+            self.add(held.at[0, p.z, 1 - p.y, d, :], *[self.dz.at[i, 1 - p.y] for i in range(3)])
+            self.start("dy")
+            self.add(held.at[0, p.z, p.y, c, :], *[self.cz.at[i, 0] for i in range(3)])
+            self.add(held.at[0, p.z, p.y, d, :], *[self.dz.at[i, p.y] for i in range(3)])
         else:
-            self.wait("az1", "az2", "az3", "bz1", "bz2", "bz3")
-            total = self.held[0, p.z, p.y].astype(jnp.float32)
-            for step in range(3):
-                total = total + self.land_z[step].astype(jnp.float32)
-            out[...] = total
+            self.wait("az1", "az2", "az3", "bz1", "bz2", "bz3", "cx", "dy")
+            for rows, others in (
+                (a, [self.z.at[i, pl.ds(0, 32), :] for i in range(3)]),
+                (b, [self.z.at[i, pl.ds(32, 32), :] for i in range(3)]),
+                (c, [self.last.at[0]]),
+                (d, [self.last.at[1]]),
+            ):
+                total = held[0, p.z, p.y, rows, :].astype(jnp.float32)
+                for other in others:
+                    total = total + other[...].astype(jnp.float32)
+                out[rows, :] = total
 
 
 def backward_kernel(
@@ -694,9 +812,7 @@
     i_i2,
     i_out,
     squares,
-    seg_col,
-    seg_row,
-    pos_row,
+    segments,
     o_out,
     o_tokens,
     o_grads,
@@ -728,6 +844,9 @@
     land_ax,
     land_by,
     land_z,
+    land_cz,
+    land_dz,
+    land_last,
     small,
     small_in,
     load_sems,
@@ -750,11 +869,10 @@
             held.at[n],
             twin.at[n % 3],
             stage,
-            land_ay.at[n],
-            land_bx.at[n],
-            land_ax.at[n],
-            land_by.at[n],
-            land_z.at[n],
+            [
+                ref.at[n]
+                for ref in (land_ay, land_bx, land_ax, land_by, land_z, land_cz, land_dz, land_last)
+            ],
             r_send.at[n],
             r_recv.at[n],
             r_pair.at[n],
@@ -778,7 +896,10 @@
         return pltpu.make_async_copy(src, dst, load_sems.at[n])
 
     def where(n):
-        return x ^ (1 - n % 2), jnp.where(n < 2, 1 - k, k)
+        return x ^ (1 - n // 2), k ^ (1 - n % 2)
+
+    def where_heads(n):
+        return x ^ (1 - n // 2), n % 2
 
     def fetch(n, part):
         r = 3 - n // 4
@@ -837,7 +958,7 @@
     for i in range(512 // ROWS):
         rows = pl.ds(i * ROWS, ROWS)
         h1_t[:, rows] = halves(d_rows.at[1], i)[...].astype(f32).T.astype(bf16)
-    fill_distance(dist, seg_col, seg_row, pos_row)
+    fill_distance(dist, segments, place)
 
     def pair(n, dx):
         return lambda: rounds[n].pair_sum(dx)
@@ -845,16 +966,16 @@
     def step(n, at):
         return lambda: rounds[n].event(at, o_grads.at[3 - n])
 
-    def put(n, dx, value, cols):
+    def put(n, dx, theirs, value, cols):
         block = value.astype(bf16).reshape(4, 2, 96, value.shape[-1])
 
-        @pl.when(n % 4 < 2)
+        @pl.when(theirs)
         def _():
             stage[dx, :, :, :, cols] = block
 
-        @pl.when(n % 4 >= 2)
+        @pl.when(jnp.logical_not(theirs))
         def _():
-            held[n // 4, dx, :, :, :, cols] = block
+            held[n, dx, :, :, :, cols] = block
 
     def push(n, dx):
         return remote(
@@ -862,43 +983,42 @@
         )
 
     plan = {
-        2: [pair(0, 1)],
+        1: [pair(0, 1)],
         3: [pair(0, 0)],
-        5: [step(0, 0), step(0, 1)],
-        6: [step(0, 2), pair(1, 1)],
-        7: [pair(1, 0), step(0, 3), step(0, 4)],
-        9: [step(1, 0), step(1, 1), step(0, 5)],
-        10: [step(1, 2), pair(2, 1)],
-        11: [pair(2, 0), step(1, 3), step(1, 4)],
+        5: [step(0, 0), pair(1, 1)],
+        7: [step(0, 2), pair(1, 0)],
+        8: [step(0, 1)],
+        9: [step(1, 0), pair(2, 1)],
+        10: [step(0, 3)],
+        11: [step(0, 4), step(1, 2), pair(2, 0)],
     }
 
     def feed(n, carry):
-        dx = 1 - n % 2
+        dx = 1 - n % 4 // 2
+        theirs = n % 2 == 0
 
         @pl.when(n < 11)
         def _():
             fetch(n + 1, 0).start()
             fetch(n + 1, 1).start()
 
-        @pl.when(n % 4 < 2)
+        @pl.when(jnp.logical_and(theirs, n >= 4))
         def _():
-            @pl.when(n >= 4)
-            def _():
-                push(n // 4 - 1, dx).wait_send()
+            push(n // 4 - 1, dx).wait_send()
 
         fetch(n, 0).wait()
         fetch(n, 1).wait()
         w = whole(w_buf.at[n % 2])
         hold = kept.at[n % 2]
         d_ffn = d_rows[0].reshape(512, 768)
-        put(n, dx, dot(f_t[...], hold[0]), slice(512, 768))
+        put(n // 4, dx, theirs, dot(f_t[...], hold[0]), slice(512, 768))
         d_hidden = dot(d_ffn, w[:, 512:])
         d_gate = (d_hidden * hold[2].astype(f32)).astype(bf16)
         d_up = (d_hidden * hold[1].astype(f32)).astype(bf16)
-        put(n, dx, dot(h1_t[...], d_gate), slice(0, 256))
-        put(n, dx, dot(h1_t[...], d_up), slice(256, 512))
-
-        @pl.when(n % 4 < 2)
+        put(n // 4, dx, theirs, dot(h1_t[...], d_gate), slice(0, 256))
+        put(n // 4, dx, theirs, dot(h1_t[...], d_up), slice(256, 512))
+
+        @pl.when(theirs)
         def _():
             push(n // 4, dx).start()
 
@@ -934,16 +1054,52 @@
     for n in range(4, 9):
         load(n).wait()
 
-    def fetch_a(n):
-        wx, wk = where(n)
+    small[0] = jnp.concatenate(
+        [jnp.sum(small[i], axis=0, keepdims=True) for i in range(4)]
+        + [jnp.sum(squares[i], axis=0, keepdims=True) for i in range(4)],
+        axis=0,
+    )
+
+    def spread(n):
+        to = ({"dk": 1}, {"dx": 1}, {"dy": 1}, {"dz": 1}, {"dz": 2}, {"dz": 3})[n]
+        return remote(
+            small.at[min(n, 3)], small_in.at[n], s_send.at[n], s_recv.at[n], place.device(**to)
+        )
+
+    def small_step(n):
+        def go():
+            if 0 < n < 4:
+                spread(n - 1).wait_recv()
+                small[n] = small[n - 1] + small_in[n - 1]
+            if n < 3:
+                spread(n).start()
+            if n == 3:
+                for at in (3, 4, 5):
+                    spread(at).start()
+            if n == 4:
+                for at in (3, 4, 5):
+                    spread(at).wait_recv()
+                total = small[3]
+                result = jnp.zeros_like(total)
+                for at in range(4):
+                    back = (place.z - at) % 4
+                    term = jnp.where(
+                        back == 0,
+                        total,
+                        jnp.where(
+                            back == 1, small_in[3], jnp.where(back == 2, small_in[4], small_in[5])
+                        ),
+                    )
+                    result = result + term
+                o_small[...] = result
+
+        return go
+
+    def fetch_heads(n):
+        wx, wk = where_heads(n)
         return pltpu.make_async_copy(i_weights.at[0, wx, wk], w_buf.at[n % 2], step_sems.at[n % 2, 0])
 
-    def fetch_b(t):
-        return pltpu.make_async_copy(
-            i_weights.at[0, t // 2, t % 2], w_buf.at[t % 2], step_sems.at[t % 2, 0]
-        )
-
-    fetch_b(0).start()
+    fetch_heads(0).start()
     dq_t[1, pl.ds(HEAD_DIM, HEAD_DIM), :] = jnp.zeros((HEAD_DIM, 512), f32)
 
     def share(t):
@@ -951,25 +1107,37 @@
             d_kv.at[t, :, :, :, 1 - place.k], d_kv_in.at[t], kv_send.at[t], kv_recv.at[t], place.device(dk=1)
         )
 
-    events = Events(
-        [
-            step(1, 5),
-            step(2, 0),
-            step(2, 1),
-            step(2, 2),
-            step(2, 3),
-            step(2, 4),
-        ]
-    )
-    stop = events.spread(4, 6, 6)
-
-    def attend(t, carry):
-        @pl.when(t < 3)
-        def _():
-            fetch_b(t + 1).start()
-
-        fetch_b(t).wait()
-        left, right = out_weights(whole(w_buf.at[t % 2]))
+    beside = {
+        (0, 0): [small_step(0), step(0, 5)],
+        (0, 2): [small_step(1), step(2, 0)],
+        (0, 4): [small_step(2), step(1, 1)],
+        (1, 0): [small_step(3), step(0, 6)],
+        (1, 2): [step(1, 3)],
+        (1, 4): [small_step(4), step(2, 2)],
+        (2, 0): [step(1, 4)],
+        (2, 2): [step(1, 5)],
+        (2, 5): [step(2, 1)],
+        (3, 0): [pair(3, 1)],
+        (3, 1): [step(1, 6)],
+        (3, 3): [step(2, 3)],
+        (3, 5): [step(2, 4)],
+    }
+    first = lax.broadcasted_iota(jnp.int32, (768, 128), 1) < HEAD_DIM
+
+    def stop(i, point):
+        for (trip, at), todo in beside.items():
+            if at == point:
+
+                @pl.when(i == trip)
+                def _():
+                    for item in todo:
+                        item()
+
+    def attend(n):
+        wx, wk = where_heads(n)
+        t = wx * 2 + wk
+        fetch_heads(n).wait()
+        left, right = out_weights(whole(w_buf.at[n % 2]))
         d_attn = d_rows[1].reshape(512, 768)
         d_ctx[0] = dot(d_attn, left).astype(bf16)
         d_ctx[1] = dot(d_attn, right).astype(bf16)
@@ -999,7 +1167,7 @@
                     acc_v[...] += term_v
                     acc_k[...] += term_k
                 dq_t[tile, rows, cols] = dot(key_t, grad_scores)
-                stop(t, point)
+                stop(n, point)
                 point += 1
             if half == 1 or tile == 1:
                 d_kv[t, 0, tile] = acc_k[...].astype(bf16).reshape(2, 2, 256, 128)
@@ -1007,22 +1175,14 @@
         share(t).start()
         for tile in range(2):
             q[2 * t + tile] = (dq_t[tile].T * HEAD_DIM**-0.5).astype(bf16)
-        return carry
-
-    lax.fori_loop(0, 4, attend, 0)
-    fetch_a(0).start()
-    first = lax.broadcasted_iota(jnp.int32, (768, 128), 1) < HEAD_DIM
-
-    def project(n, carry):
-        dx = 1 - n % 2
-        wx, wk = where(n)
+
+    def project(n):
+        wx, wk = where_heads(n)
         t = wx * 2 + wk
-
-        @pl.when(n < 3)
-        def _():
-            fetch_a(n + 1).start()
-
-        @pl.when(n < 2)
+        dx = 1 - n // 2
+        theirs = wk != k
+
+        @pl.when(theirs)
         def _():
             push(2, dx).wait_send()
 
@@ -1045,64 +1205,42 @@
             d_w[:, 512:640],
             jnp.where(first, d_w[:, 640:768], right),
         ]
-        put(12 + n, dx, jnp.concatenate(tiles, axis=1), slice(0, 768))
-
-        @pl.when(n < 2)
+        put(3, dx, theirs, jnp.concatenate(tiles, axis=1), slice(0, 768))
+
+        @pl.when(theirs)
         def _():
             push(3, dx).start()
 
-        fetch_a(n).wait()
         d_h1[...] += dot(d_qkv, whole(w_buf.at[n % 2]), NT)
-        for at in (2, 3):
-
-            @pl.when(n == at)
-            def _():
-                rounds[3].pair_sum(3 - at)
+
+    def heads(n, carry):
+        @pl.when(n < 4)
+        def _():
+            attend(n)
+
+        @pl.when(n > 0)
+        def _():
+            project(n - 1)
+
+        @pl.when(n < 3)
+        def _():
+            fetch_heads(n + 1).start()
 
         return carry
 
-    lax.fori_loop(0, 4, project, 0)
+    lax.fori_loop(0, 5, heads, 0)
     for i in range(512 // ROWS):
         rows = pl.ds(i * ROWS, ROWS)
         halves(d_rows.at[0], i)[...] = d_h1[rows, :].astype(bf16)
+    rounds[3].pair_sum(0)
     swap(1).start()
     stay(1).start()
-    total = jnp.concatenate(
-        [jnp.sum(small[i], axis=0, keepdims=True) for i in range(4)]
-        + [jnp.sum(squares[i], axis=0, keepdims=True) for i in range(4)],
-        axis=0,
-    )
-
-    def spread(n):
-        to = ({"dk": 1}, {"dx": 1}, {"dy": 1}, {"dz": 1}, {"dz": 2}, {"dz": 3})[n]
-        src = small.at[min(n, 3)]
-        return remote(src, small_in.at[n], s_send.at[n], s_recv.at[n], place.device(**to))
-
-    small[0] = total
-    for n in range(3):
-        spread(n).start()
-        spread(n).wait_recv()
-        total = total + small_in[n]
-        small[n + 1] = total
-    for n in range(3, 6):
-        spread(n).start()
-    rounds[3].event(0)
-    rounds[3].event(1)
-    rounds[2].event(5, o_grads.at[1])
-    for at in range(2, 6):
-        rounds[3].event(at, o_grads.at[0])
-    for n in range(3, 6):
-        spread(n).wait_recv()
-    result = jnp.zeros_like(total)
-    for at in range(4):
-        step_of = (place.z - at) % 4
-        term = jnp.where(
-            step_of == 0,
-            total,
-            jnp.where(step_of == 1, small_in[3], jnp.where(step_of == 2, small_in[4], small_in[5])),
-        )
-        result = result + term
-    o_small[...] = result
+    step(2, 5)()
+    for at in (0, 1, 2):
+        step(3, at)()
+    step(2, 6)()
+    for at in (3, 4, 5, 6):
+        step(3, at)()
     for n in range(6):
         spread(n).wait_send()
     for r in rounds:
@@ -1116,7 +1254,7 @@
         stay(n).wait()
 
 
-def backward(span, slopes, saved, seg_col, seg_row, pos_row):
+def backward(span, slopes, saved, segments):
     f32, bf16 = jnp.float32, jnp.bfloat16
     any_space = pl.BlockSpec(memory_space=pl.ANY)
     vmem = pl.BlockSpec(memory_space=pltpu.VMEM)
@@ -1125,8 +1263,8 @@
     h1b = h1b.reshape(2, 256, 768)
     out = out.reshape(2, 256, 768)
     in_specs = [pl.BlockSpec(memory_space=pltpu.SMEM), any_space, vmem] + [any_space] * 10
-    in_specs += [vmem, any_space, vmem, any_space, vmem, vmem, vmem, vmem]
-    rest = 96 - CUT
+    in_specs += [vmem, any_space, vmem, any_space, vmem, vmem]
+    copies = len(ScatterRound.names)
     return pl.pallas_call(
         partial(backward_kernel, span),
         out_shape=(
@@ -1160,17 +1298,20 @@
             pltpu.VMEM((ROUNDS, 2, 4, 2, 96, 768), bf16),
             pltpu.VMEM((3, 2, 4, 2, 96, 768), bf16),
             pltpu.VMEM((2, 4, 2, 96, 768), bf16),
-            pltpu.VMEM((ROUNDS, 2, 4, CUT, 768), bf16),
-            pltpu.VMEM((ROUNDS, 4, 2, rest, 768), bf16),
-            pltpu.VMEM((ROUNDS, 4, CUT, 768), bf16),
-            pltpu.VMEM((ROUNDS, 4, rest, 768), bf16),
-            pltpu.VMEM((ROUNDS, 3, 96, 768), bf16),
+            pltpu.VMEM((ROUNDS, 2, 4, 48, 768), bf16),
+            pltpu.VMEM((ROUNDS, 4, 2, 48, 768), bf16),
+            pltpu.VMEM((ROUNDS, 4, 32, 768), bf16),
+            pltpu.VMEM((ROUNDS, 4, 32, 768), bf16),
+            pltpu.VMEM((ROUNDS, 3, 64, 768), bf16),
+            pltpu.VMEM((ROUNDS, 3, 2, 16, 768), bf16),
+            pltpu.VMEM((ROUNDS, 3, 2, 16, 768), bf16),
+            pltpu.VMEM((ROUNDS, 2, 16, 768), bf16),
             pltpu.VMEM((4, 8, 768), f32),
             pltpu.VMEM((6, 8, 768), f32),
             dma((10,)),
             dma((2, 2)),
-            dma((ROUNDS, 11)),
-            dma((ROUNDS, 11)),
+            dma((ROUNDS, copies)),
+            dma((ROUNDS, copies)),
             dma((ROUNDS, 2, 2)),
             dma((6,)),
             dma((4,)),
@@ -1201,10 +1342,62 @@
         i2,
         out,
         squares,
-        seg_col,
-        seg_row,
-        pos_row,
+        segments,
     )
+
+
+def finish_kernel(
+    block, grads, small, lo, gt, o_lo, o_gt, o_qkv, o_wout, o_win, o_down, o_gains, o_biases, rows, sems
+):
+    def move(n, src, dst):
+        return pltpu.make_async_copy(src, dst, sems.at[n])
+
+    move(0, lo, rows.at[0]).start()
+    move(1, gt, rows.at[1]).start()
+    turned = []
+    for c in range(3):
+        o_qkv[c] = grads[0, :, c * 256 : c * 256 + 192]
+        turned.append(grads[0, :, c * 256 + 128 : c * 256 + 256].T[HEAD_DIM:])
+    o_wout[...] = jnp.concatenate(turned, axis=0)
+    move(0, lo, rows.at[0]).wait()
+    move(2, rows.at[0], o_lo).start()
+    move(1, gt, rows.at[1]).wait()
+    move(3, rows.at[1], o_gt).start()
+    for r in range(3):
+        units = slice(r * 256, (r + 1) * 256)
+        o_win[:, 0, units] = grads[1 + r, :, 0:256]
+        o_win[:, 1, units] = grads[1 + r, :, 256:512]
+        o_down[units, :] = grads[1 + r, :, 512:768].T
+    mine = pltpu.roll(small[...], 768 - block[0] * 96, 1)
+    o_gains[...] = mine[0:2, 0:96]
+    o_biases[...] = mine[2:4, 0:96]
+    move(2, rows.at[0], o_lo).wait()
+    move(3, rows.at[1], o_gt).wait()
+
+
+def finish(block, grads, small, lo, gt):
+    any_space = pl.BlockSpec(memory_space=pl.ANY)
+    vmem = pl.BlockSpec(memory_space=pltpu.VMEM)
+    f32 = jnp.float32
+    shape = jax.ShapeDtypeStruct
+    return pl.pallas_call(
+        finish_kernel,
+        out_shape=(
+            shape(lo.shape, lo.dtype),
+            shape(gt.shape, gt.dtype),
+            shape((3, 96, 192), f32),
+            shape((192, 96), f32),
+            shape((96, 2, 768), f32),
+            shape((768, 96), f32),
+            shape((2, 96), f32),
+            shape((2, 96), f32),
+        ),
+        in_specs=[pl.BlockSpec(memory_space=pltpu.SMEM), vmem, vmem, any_space, any_space],
+        out_specs=(any_space, any_space) + (vmem,) * 6,
+        scratch_shapes=[pltpu.VMEM((2,) + lo.shape, lo.dtype), pltpu.SemaphoreType.DMA((4,))],
+        compiler_params=pltpu.CompilerParams(vmem_limit_bytes=VMEM_LIMIT),
+        name="finish",
+    )(block, grads, small, lo, gt)
 
 
 def local(
@@ -1221,63 +1414,53 @@
     f32 = jnp.float32
     shard_rows = query_key_value_weight.shape[1]
     span = 96 // shard_rows
-    groups = None
-    if span > 1:
+    slopes = jnp.exp2(-8.0 * (jnp.arange(HEADS).astype(f32) + 1.0) / HEADS)
+    cells = float(lax.axis_size("fsdp") * 2 * 1024 * 768)
+    if span == 1:
+        raw = (query_key_value_weight, w_out, input_weight, w_down)
+        gains, biases = norm_gains, norm_biases
+    else:
         count = lax.axis_size("fsdp")
         groups = [list(range(i, i + span)) for i in range(0, count, span)]
-    place_x = lax.axis_index("tp") // 2
-    place_k = lax.axis_index("tp") % 2
-    block = lax.axis_index("fsdp") // span
-
-    heads = query_key_value_weight.transpose(1, 0, 2).reshape(shard_rows, 3, 3, HEAD_DIM)
-    w_out_t = w_out.T.reshape(shard_rows, 3, 1, HEAD_DIM)
-    wa = jnp.concatenate([heads, w_out_t], axis=2).reshape(shard_rows, 1, 768)
-    gate_up = input_weight.reshape(shard_rows, 2, 3, 256).transpose(0, 2, 1, 3)
-    down = w_down.T.reshape(shard_rows, 3, 1, 256)
-    wf = jnp.concatenate([gate_up, down], axis=2).reshape(shard_rows, 3, 768)
-    shard = jnp.concatenate([wa, wf], axis=1).transpose(1, 0, 2)
-    norms = jnp.concatenate([norm_gains, norm_biases], axis=0).astype(f32)
-    if span > 1:
-        shard = lax.all_gather(shard, "fsdp", axis=1, tiled=True, axis_index_groups=groups)
-        norms = lax.all_gather(norms, "fsdp", axis=1, tiled=True, axis_index_groups=groups)
-    norm_rows = lax.dynamic_update_slice(jnp.zeros((8, 768), f32), norms, (0, block * 96))
-
-    segment = lax.dynamic_index_in_dim(segment_ids, place_x, 0, keepdims=False)
-    seg_col = segment.reshape(1024, 1)
-    seg_row = lax.dynamic_index_in_dim(segment.reshape(2, 2, 256), place_k, 1, keepdims=False)
-    seg_row = seg_row.reshape(1, 512)
-    pos_row = (
-        lax.broadcasted_iota(jnp.int32, (2, 256), 0) * 512
-        + place_k * 256
-        + lax.broadcasted_iota(jnp.int32, (2, 256), 1)
-    )
-    pos_row = pos_row.reshape(1, 512).astype(f32)
-    slopes = jnp.exp2(-8.0 * (jnp.arange(HEADS).astype(f32) + 1.0) / HEADS)
-
-    saved = forward(span, slopes, shard, norm_rows, tokens, cotangent, seg_col, seg_row, pos_row)
-    layer_out, grad_tokens, grads, small = backward(span, slopes, saved, seg_col, seg_row, pos_row)
-
-    if span > 1:
+        heads = query_key_value_weight.transpose(1, 0, 2).reshape(shard_rows, 3, 3, HEAD_DIM)
+        w_out_t = w_out.T.reshape(shard_rows, 3, 1, HEAD_DIM)
+        wa = jnp.concatenate([heads, w_out_t], axis=2).reshape(shard_rows, 1, 768)
+        gate_up = input_weight.reshape(shard_rows, 2, 3, 256).transpose(0, 2, 1, 3)
+        down = w_down.T.reshape(shard_rows, 3, 1, 256)
+        wf = jnp.concatenate([gate_up, down], axis=2).reshape(shard_rows, 3, 768)
+        shard = jnp.concatenate([wa, wf], axis=1).transpose(1, 0, 2)
+        raw = (lax.all_gather(shard, "fsdp", axis=1, tiled=True, axis_index_groups=groups),)
+        gains, biases = (
+            lax.all_gather(rows, "fsdp", axis=1, tiled=True, axis_index_groups=groups)
+            for rows in (norm_gains, norm_biases)
+        )
+
+    saved = forward(span, slopes, raw, gains, biases, tokens, cotangent, segment_ids)
+    layer_out, grad_tokens, grads, small = backward(span, slopes, saved, segment_ids)
+
+    if span == 1:
+        block = lax.axis_index("fsdp").astype(jnp.int32).reshape(1)
+        outs = finish(block, grads, small, layer_out, grad_tokens)
+    else:
         grads = lax.psum_scatter(
             grads, "fsdp", scatter_dimension=1, tiled=True, axis_index_groups=groups
         )
         small = lax.psum(small, "fsdp", axis_index_groups=groups)
-    grads_a = grads[0].reshape(shard_rows, 3, 4, HEAD_DIM)
-    grads_f = grads[1:].reshape(3, shard_rows, 3, 256)
-    shard_start = lax.axis_index("fsdp") * shard_rows
-    mine = lax.dynamic_slice_in_dim(small[:4], shard_start, shard_rows, 1)
-    cells = float(lax.axis_size("fsdp") * 2 * 1024 * 768)
-    return (
-        layer_out,
-        grad_tokens,
-        grads_a[:, :, :3].transpose(1, 0, 2, 3).reshape(3, shard_rows, 192),
-        grads_a[:, :, 3].reshape(shard_rows, 192).T,
-        grads_f[:, :, :2].transpose(1, 2, 0, 3).reshape(shard_rows, 2, 768),
-        grads_f[:, :, 2].transpose(0, 2, 1).reshape(768, shard_rows),
-        mine[:2],
-        mine[2:],
-        jnp.sqrt(jnp.sum(small[4:], axis=1) / cells),
-    )
+        grads_a = grads[0].reshape(shard_rows, 3, 4, HEAD_DIM)
+        grads_f = grads[1:].reshape(3, shard_rows, 3, 256)
+        shard_start = lax.axis_index("fsdp") * shard_rows
+        mine = lax.dynamic_slice_in_dim(small[:4], shard_start, shard_rows, 1)
+        outs = (
+            layer_out,
+            grad_tokens,
+            grads_a[:, :, :3].transpose(1, 0, 2, 3).reshape(3, shard_rows, 192),
+            grads_a[:, :, 3].reshape(shard_rows, 192).T,
+            grads_f[:, :, :2].transpose(1, 2, 0, 3).reshape(shard_rows, 2, 768),
+            grads_f[:, :, 2].transpose(0, 2, 1).reshape(768, shard_rows),
+            mine[:2],
+            mine[2:],
+        )
+    return outs + (jnp.sqrt(jnp.sum(small[4:], axis=1) / cells),)
 
 
 def solution(mesh):

time: 278 us -> 270 us (0.971)
  local copies, waits for them, and re-layouts: 15.6 us -> 3.6 us
  Pallas kernels: 257 us -> 264 us
  other arithmetic: 4.86 us -> 1.17 us
    pallas_call x1 -> x2, Pallas kernels: 111 us -> 136 us  [the longest x1 132 us: forward(): pl.pallas_call(partial(forward_refs, span, len(raw)), out_shape=tuple((ja...]
    pallas_call x1, Pallas kernels: 145 us -> 127 us  [backward(): pl.pallas_call(partial(backward_kernel, span), out_shape=(jax.ShapeDtypeS...]
    reshape x8 -> x0, local copies, waits for them, and re-layouts: 3.98 us -> none  [the longest x1 1.02 us: local(): seg_col = segment.reshape(1024, 1)]
    slice x7 -> x0, local copies, waits for them, and re-layouts: 3.92 us -> none  [the longest x1 1.23 us: local(): grads_f = grads[1:].reshape(3, shard_rows, 3, 256)]
    unnamed x17 -> x4, local copies, waits for them, and re-layouts: 5.58 us -> 3.6 us
where the time goes in v3:
time: 270 us; the launch traced here: 269 us
  Pallas kernels  264 us (98%)
  local copies, waits for them, and re-layouts  3.6 us (1%)
    pallas_call x1, Pallas kernels, forward(): pl.pallas_call(partial(forward_refs, span, len(raw)), out_shape=tuple((ja...  132 us
    pallas_call x1, Pallas kernels, backward(): pl.pallas_call(partial(backward_kernel, span), out_shape=(jax.ShapeDtypeS...  127 us

profile of v3, /device:TPU:0, one launch (start us, length us, event | category | flops | bytes accessed | tf_op | source)
XLA Modules:
  0.0 269.2 jit_solution(9993099588250056178)
XLA Ops:
  0.6 0.5 multiply_exponential_fusion.refs_0_.slopes
  1.2 1.7 copy.18.refs_4_
  2.9 131.8 %forward.1 = (bf16[4,2,2,4,2,96,768]{6,5,4,3,2,1,0:T(8,128)(2,1)}, f32[8,768]{1,0:T(8,128)}, bf16[2,256,768]{2,1,0:T(8,128)(2,1)}, bf16[2,256,768]{2,1,0:T(8,128...) custom-call(f32[12]{0:T(128)} %multiply_exponential_fusion.refs_0_.s, ...), custom_call_target="tpu_custom_call" | custom-call | tf_op jit(solution)/shard_map/forward/pallas_call | solution.py:642
  134.7 127.3 %backward.1 = (bf16[2,256,768]{2,1,0:T(8,128)(2,1)}, bf16[2,256,768]{2,1,0:T(8,128)(2,1)}, f32[4,96,768]{2,1,0:T(8,128)}, f32[8,768]{1,0:T(8,128)}) custom-call(f32[12]{0:T(128)} %multiply_exponential_fusion.refs_0_.slopes, bf16[4,2,2,4,2,96,768]{6,5,4,3,2,1,0:T(8,128)(2,1)} %get-tuple-element.38.i_weights, f32[8,768]{1,0:T(8,128)} %get-tuple-element.39.norms, ...), custom_call_target="tpu_custom_call" | custom-call | tf_op jit(solution)/shard_map/backward/pallas_call | solution.py:1268
  262.0 0.0 copy-start
  262.1 4.7 %finish.1 = (bf16[2,256,768]{2,1,0:T(8,128)(2,1)}, bf16[2,256,768]{2,1,0:T(8,128)(2,1)}, f32[3,96,192]{2,1,0:T(8,128)}, f32[192,96]{1,0:T(8,128)}, f32[96,2,768]...) custom-call(s32[1]{0:T(128)} %bitcast.block, f32[4,96,768]{2,1,0:T(8,128)} %get-tuple-element.55.grads, ...), custom_call_target="tpu_custom_call" | custom-call | tf_op jit(solution)/shard_map/finish/pallas_call | solution.py:1383
  266.7 1.9 copy.19
  268.6 0.0 copy-done
  268.6 0.1 slice_reduce_fusion
  268.7 0.5 multiply_sqrt_fusion
Async XLA Ops:
  262.0 6.6 %copy-start = (f32[8,768]{1,0:T(8,128)S(1)}, f32[8,768]{1,0:T(8,128)}, u32[]{:S(2)}) copy-start(f32[8,768]{1,0:T(8,128)} %get-tuple-element.56.small) | copy-start | bytes 73732

commit v4 on v3

--- a/solution.py
+++ b/solution.py
@@ -259,14 +259,19 @@
     qkv, w_out = raw[0], raw[1]
     turned = w_out[...].astype(jnp.float32).T
     for c in range(3):
-        shard[0, :, c * 256 : c * 256 + 128] = qkv[c, :, 0:128]
-        shard[0, :, c * 256 + 128 : c * 256 + 256] = jnp.concatenate(
-            [
-                qkv[c, :, 128:192].astype(jnp.float32),
-                turned[:, c * HEAD_DIM : (c + 1) * HEAD_DIM],
-            ],
-            axis=1,
-        ).astype(jnp.bfloat16)
+        tiles = (
+            qkv[c, :, 0:128],
+            jnp.concatenate(
+                [
+                    qkv[c, :, 128:192].astype(jnp.float32),
+                    turned[:, c * HEAD_DIM : (c + 1) * HEAD_DIM],
+                ],
+                axis=1,
+            ).astype(jnp.bfloat16),
+        )
+        for i in range(2):
+            half, at = divmod(2 * c + i, 3)
+            shard[half, :, at * 128 : at * 128 + 128] = tiles[i]
 
 
 def pack_feed(raw, shard):
@@ -274,9 +279,12 @@
     turned = w_down[...].astype(jnp.float32).T.astype(jnp.bfloat16)
     for r in range(3):
         units = slice(r * 256, (r + 1) * 256)
-        shard[1 + r, :, 0:256] = w_in[:, 0, units]
-        shard[1 + r, :, 256:512] = w_in[:, 1, units]
-        shard[1 + r, :, 512:768] = turned[:, units]
+        first = slice(r * 256, r * 256 + 128)
+        second = slice(r * 256 + 128, r * 256 + 256)
+        shard[2 + 2 * r, :, 0:256] = w_in[:, 0, units]
+        shard[2 + 2 * r, :, 256:384] = w_in[:, 1, first]
+        shard[3 + 2 * r, :, 0:128] = w_in[:, 1, second]
+        shard[3 + 2 * r, :, 128:384] = turned[:, units]
 
 
 def out_weights(w):
@@ -287,8 +295,7 @@
 
 
 def whole(ref):
-    value = ref[...]
-    return value.reshape(768, value.shape[-1])
+    return jnp.concatenate([ref[i].reshape(768, 384) for i in range(2)], axis=1)
 
 
 HEAD_SPOTS = ((0, 0), (0, 1), (1, 0))
@@ -384,7 +391,7 @@
     x, y, z, k = place.shifted()
     rounds = [
         GatherRound(place, shard.at[r], weights.at[r], g_send.at[r], g_recv.at[r], g_keep.at[r])
-        for r in range(ROUNDS)
+        for r in range(2 * ROUNDS)
     ]
     norm_gather = NormGather(place, norm_rows, norms, n_send, n_recv, n_keep)
 
@@ -404,10 +411,10 @@
 
     def store(n):
         src, dst = (
-            (weights.at[0], o_weights.at[0]),
-            (weights.at[1], o_weights.at[1]),
-            (weights.at[2], o_weights.at[2]),
-            (weights.at[3], o_weights.at[3]),
+            (weights.at[0:2], o_weights.at[0:2]),
+            (weights.at[2:4], o_weights.at[2:4]),
+            (weights.at[4:6], o_weights.at[4:6]),
+            (weights.at[6:8], o_weights.at[6:8]),
             (xs, o_x),
             (keys, o_k),
             (values, o_v),
@@ -424,8 +431,8 @@
         shard[...] = raw[0][...]
     place.greet(ALL_PEERS)
     rounds[0].event(0)
+    swap(0).start()
     for n in range(2):
-        swap(n).start()
         stay(n).start()
     norm_rows[...] = jnp.zeros_like(norm_rows)
     norm_rows[0:2, 0:96] = gains[...].astype(f32)
@@ -440,18 +447,19 @@
     def step(r, n):
         def go():
             rounds[r].event(n)
-            if n == GatherRound.last:
-                store(r).start()
+            if n == GatherRound.last and r % 2:
+                store(r // 2).start()
 
         return go
 
-    order = [(0, 1), (0, 2), (1, 0), (1, 1), (0, 3), (0, 4), (1, 2), (2, 0), (2, 1)]
-    order += [(0, 5), (0, 6), (0, 7), (0, 8), (0, 9)]
-    begun = len(order)
-    order += [(1, 3), (1, 4), (2, 2), (3, 0), (3, 1), (1, 5), (1, 6), (1, 7), (1, 8), (2, 3), (2, 4), (3, 2), (1, 9)]
-    order += [(2, 5), (2, 6), (2, 7), (2, 8), (3, 3), (3, 4), (2, 9)]
-    order += [(3, 5), (3, 6), (3, 7), (3, 8), (3, 9)]
+    stages = {0: 0, 1: 1, 2: 1, 3: 2, 4: 2, 5: 3, 6: 3, 7: 3, 8: 3, 9: 4}
+    order = sorted((r + stages[n], r, n) for r in range(2 * ROUNDS) for n in range(10))
+    order = [(r, n) for _, r, n in order][1:]
+    begun = order.index((1, 9)) + 1
+    beside_heads = order.index((3, 9)) + 1 - begun
+    rest = len(order) - begun - beside_heads
     events = Events(step(*at) for at in order)
+    events.steps.insert(order.index((7, 4)) + 1, lambda: swap(1).start())
 
     events.run(1)
     fill_distance(dist, segments, place)
@@ -468,7 +476,7 @@
         return remote(ref, ref, kv_send.at[t, n], kv_recv.at[t, n], place.device(dk=1))
 
     def project(t, carry):
-        w = whole(weights.at[0, t // 2, t % 2])
+        w = whole(weights.at[0:2, t // 2, t % 2])
         for s in range(2):
             out = dot(xs[s], w).astype(bf16)
             for i in range(2):
@@ -482,7 +490,7 @@
 
     lax.fori_loop(0, 4, project, 0)
     out_t[1, pl.ds(HEAD_DIM, HEAD_DIM), :] = jnp.zeros((HEAD_DIM, 512), f32)
-    stop = events.spread(4, 7, 13)
+    stop = events.spread(4, 7, beside_heads)
 
     def attend(t, carry):
         share(t, 0).wait_recv()
@@ -506,7 +514,7 @@
                 point += 1
         for tile in range(2):
             ctx[2 * t + tile] = out_t[tile].T.astype(bf16)
-        left, right = out_weights(whole(weights.at[0, t // 2, t % 2]))
+        left, right = out_weights(whole(weights.at[0:2, t // 2, t % 2]))
         mixed = dot(ctx[2 * t], left, NT) + dot(ctx[2 * t + 1], right, NT)
 
         @pl.when(t == 0)
@@ -547,9 +555,19 @@
     store(9).start()
     store(10).start()
 
-    stop_f = events.place(
-        12, 2, {1: 1, 2: 1, 3: 1, 4: 1, 5: 1, 6: 1, 8: 1, 9: 1, 11: 1, 13: 1, 14: 1, 16: 1}
-    )
+    first_part = order.index((5, 9)) - begun - beside_heads
+    last_part = len(order) - order.index((6, 9))
+    counts = {}
+    for n in range(first_part):
+        at = n * 8 // first_part
+        counts[at] = counts.get(at, 0) + 1
+    counts[8] = 1
+    middle = rest + 1 - first_part - last_part - 1
+    for n in range(middle):
+        at = 9 + n * 6 // middle
+        counts[at] = counts.get(at, 0) + 1
+    counts[16] = last_part
+    stop_f = events.place(12, 2, counts)
     assert not events.steps
 
     def keep_copy(n):
@@ -563,7 +581,7 @@
         def _():
             keep_copy(n - 2).wait()
 
-        ref = weights.at[r, t // 2, t % 2]
+        ref = weights.at[pl.ds(2 * r, 2), t // 2, t % 2]
         for start in range(0, 512, CHUNK):
             rows = pl.ds(start, CHUNK)
             w = whole(ref)
@@ -619,7 +637,7 @@
     any_space = pl.BlockSpec(memory_space=pl.ANY)
     vmem = pl.BlockSpec(memory_space=pltpu.VMEM)
     outs = (
-        ((ROUNDS, 2, 2, 4, 2, 96, 768), bf16, any_space),
+        ((2 * ROUNDS, 2, 2, 4, 2, 96, 384), bf16, any_space),
         ((8, 768), f32, vmem),
         ((2, 256, 768), bf16, any_space),
         ((2, 256, 768), bf16, any_space),
@@ -645,9 +663,9 @@
         in_specs=[pl.BlockSpec(memory_space=pltpu.SMEM)] + [vmem] * (len(raw) + 5),
         out_specs=tuple(spec for _, _, spec in outs),
         scratch_shapes=[
-            pltpu.VMEM((ROUNDS, 96, 768), bf16),
+            pltpu.VMEM((2 * ROUNDS, 96, 384), bf16),
             pltpu.VMEM((8, 768), f32),
-            pltpu.VMEM((ROUNDS, 2, 2, 4, 2, 96, 768), bf16),
+            pltpu.VMEM((2 * ROUNDS, 2, 2, 4, 2, 96, 384), bf16),
             pltpu.VMEM((4, 2, 8, 768), f32),
             pltpu.VMEM((2, 256, 768), bf16),
             pltpu.VMEM((8, 512, 128), bf16),
@@ -661,9 +679,9 @@
             pltpu.VMEM((512, 768), f32),
             pltpu.VMEM((512, 768), f32),
             pltpu.VMEM((2, 3, 512, 256), bf16),
-            dma((ROUNDS, copies)),
-            dma((ROUNDS, copies)),
-            dma((ROUNDS,)),
+            dma((2 * ROUNDS, copies)),
+            dma((2 * ROUNDS, copies)),
+            dma((2 * ROUNDS,)),
             dma((4,)),
             dma((4,)),
             dma,
@@ -905,7 +923,7 @@
         r = 3 - n // 4
         wx, wk = where(n % 4)
         if part == 0:
-            return pltpu.make_async_copy(i_weights.at[r, wx, wk], w_buf.at[n % 2], step_sems.at[n % 2, 0])
+            return pltpu.make_async_copy(i_weights.at[pl.ds(2 * r, 2), wx, wk], w_buf.at[n % 2], step_sems.at[n % 2, 0])
         return pltpu.make_async_copy(
             i_kept.at[(r - 1) * 4 + wx * 2 + wk], kept.at[n % 2], step_sems.at[n % 2, 1]
         )
@@ -1097,7 +1115,7 @@
 
     def fetch_heads(n):
         wx, wk = where_heads(n)
-        return pltpu.make_async_copy(i_weights.at[0, wx, wk], w_buf.at[n % 2], step_sems.at[n % 2, 0])
+        return pltpu.make_async_copy(i_weights.at[0:2, wx, wk], w_buf.at[n % 2], step_sems.at[n % 2, 0])
 
     fetch_heads(0).start()
     dq_t[1, pl.ds(HEAD_DIM, HEAD_DIM), :] = jnp.zeros((HEAD_DIM, 512), f32)
@@ -1276,7 +1294,7 @@
         in_specs=in_specs,
         out_specs=(any_space, any_space, vmem, vmem),
         scratch_shapes=[
-            pltpu.VMEM((2, 4, 2, 96, 768), bf16),
+            pltpu.VMEM((2, 2, 4, 2, 96, 384), bf16),
             pltpu.VMEM((2, 3, 512, 256), bf16),
             pltpu.VMEM((768, 512), bf16),
             pltpu.VMEM((768, 512), bf16),
@@ -1428,7 +1446,7 @@
         gate_up = input_weight.reshape(shard_rows, 2, 3, 256).transpose(0, 2, 1, 3)
         down = w_down.T.reshape(shard_rows, 3, 1, 256)
         wf = jnp.concatenate([gate_up, down], axis=2).reshape(shard_rows, 3, 768)
-        shard = jnp.concatenate([wa, wf], axis=1).transpose(1, 0, 2)
+        shard = jnp.concatenate([wa, wf], axis=1).reshape(shard_rows, 8, 384).transpose(1, 0, 2)
         raw = (lax.all_gather(shard, "fsdp", axis=1, tiled=True, axis_index_groups=groups),)
         gains, biases = (
             lax.all_gather(rows, "fsdp", axis=1, tiled=True, axis_index_groups=groups)

time: 270 us -> 252 us (0.933)
  Pallas kernels: 264 us -> 246 us
    pallas_call x1, Pallas kernels: 132 us -> 113 us  [forward(): pl.pallas_call(partial(forward_refs, span, len(raw)), out_shape=tuple((ja...]
where the time goes in v4:
time: 252 us
  Pallas kernels  246 us (98%)
  local copies, waits for them, and re-layouts  3.6 us (1%)
    pallas_call x1, Pallas kernels, backward(): pl.pallas_call(partial(backward_kernel, span), out_shape=(jax.ShapeDtypeS...  129 us
    pallas_call x1, Pallas kernels, forward(): pl.pallas_call(partial(forward_refs, span, len(raw)), out_shape=tuple((ja...  113 us

profile of v4, /device:TPU:0, one launch (start us, length us, event | category | flops | bytes accessed | tf_op | source)
XLA Modules:
  0.0 251.8 jit_solution(191360754718635052)
XLA Ops:
  0.6 0.5 multiply_exponential_fusion.refs_0_.slopes
  1.2 1.7 copy.18.refs_4_
  2.9 112.9 %forward.1 = (bf16[8,2,2,4,2,96,384]{6,5,4,3,2,1,0:T(8,128)(2,1)}, f32[8,768]{1,0:T(8,128)}, bf16[2,256,768]{2,1,0:T(8,128)(2,1)}, bf16[2,256,768]{2,1,0:T(8,128...) custom-call(f32[12]{0:T(128)} %multiply_exponential_fusion.refs_0_.s, ...), custom_call_target="tpu_custom_call" | custom-call | tf_op jit(solution)/shard_map/forward/pallas_call | solution.py:660
  115.8 128.8 %backward.1 = (bf16[2,256,768]{2,1,0:T(8,128)(2,1)}, bf16[2,256,768]{2,1,0:T(8,128)(2,1)}, f32[4,96,768]{2,1,0:T(8,128)}, f32[8,768]{1,0:T(8,128)}) custom-call(f32[12]{0:T(128)} %multiply_exponential_fusion.refs_0_.slopes, bf16[8,2,2,4,2,96,384]{6,5,4,3,2,1,0:T(8,128)(2,1)} %get-tuple-element.38.i_weights, f32[8,768]{1,0:T(8,128)} %get-tuple-element.39.norms, ...), custom_call_target="tpu_custom_call" | custom-call | tf_op jit(solution)/shard_map/backward/pallas_call | solution.py:1286
  244.6 0.0 copy-start
  244.6 4.7 %finish.1 = (bf16[2,256,768]{2,1,0:T(8,128)(2,1)}, bf16[2,256,768]{2,1,0:T(8,128)(2,1)}, f32[3,96,192]{2,1,0:T(8,128)}, f32[192,96]{1,0:T(8,128)}, f32[96,2,768]...) custom-call(s32[1]{0:T(128)} %bitcast.block, f32[4,96,768]{2,1,0:T(8,128)} %get-tuple-element.55.grads, ...), custom_call_target="tpu_custom_call" | custom-call | tf_op jit(solution)/shard_map/finish/pallas_call | solution.py:1401
  249.3 1.9 copy.19
  251.2 0.0 copy-done
  251.2 0.1 slice_reduce_fusion
  251.3 0.5 multiply_sqrt_fusion
Async XLA Ops:
  244.6 6.6 %copy-start = (f32[8,768]{1,0:T(8,128)S(1)}, f32[8,768]{1,0:T(8,128)}, u32[]{:S(2)}) copy-start(f32[8,768]{1,0:T(8,128)} %get-tuple-element.56.small) | copy-start | bytes 73732

commit v5 on v4

--- a/solution.py
+++ b/solution.py
@@ -118,7 +118,7 @@
         7: (("ay1",), ("d5",)),
         8: (("bx1",), ("d6",)),
     }
-    last = 9
+    last = 10
 
     def __init__(self, place, own, out, send, recv, keep):
         self.place, self.own, self.out = place, own, out
@@ -170,7 +170,9 @@
             self.wait("z1", "z2", "z3")
             self.start("ax", "by", "ay0", "bx0", "d0")
         elif n == 9:
-            self.wait(*["d%d" % i for i in range(7)])
+            self.wait("d0", "d2", "d3")
+        elif n == 10:
+            self.wait("d1", "d4", "d5", "d6")
         else:
             self.wait(*self.steps[n][0])
             self.start(*self.steps[n][1])
@@ -275,7 +277,7 @@
 
 
 def pack_feed(raw, shard):
-    w_in, w_down = raw[2], raw[3]
+    w_in, w_down = raw[2:]
     turned = w_down[...].astype(jnp.float32).T.astype(jnp.bfloat16)
     for r in range(3):
         units = slice(r * 256, (r + 1) * 256)
@@ -351,13 +353,16 @@
     o_ctx,
     o_lse,
     o_kept,
-    o_h1b,
     o_n1,
     o_i1,
     o_n2,
     o_i2,
     o_out,
     o_squares,
+    o_h1_t,
+    o_x_t,
+    o_dist,
+    o_wo,
     shard,
     norm_rows,
     weights,
@@ -369,6 +374,9 @@
     ctx,
     h1b,
     n1,
+    h1_t,
+    x_t,
+    wo,
     dist,
     out_t,
     acc,
@@ -420,8 +428,11 @@
             (values, o_v),
             (q, o_q),
             (ctx, o_ctx),
-            (h1b, o_h1b),
             (n1, o_n1),
+            (h1_t, o_h1_t),
+            (x_t, o_x_t),
+            (dist, o_dist),
+            (wo, o_wo),
         )[n]
         return pltpu.make_async_copy(src, dst, store_sems.at[n])
 
@@ -452,12 +463,13 @@
 
         return go
 
-    stages = {0: 0, 1: 1, 2: 1, 3: 2, 4: 2, 5: 3, 6: 3, 7: 3, 8: 3, 9: 4}
-    order = sorted((r + stages[n], r, n) for r in range(2 * ROUNDS) for n in range(10))
+    stages = {0: 0, 1: 1, 2: 1, 3: 2, 4: 2, 5: 3, 6: 3, 7: 3, 8: 3, 9: 4, 10: 4}
+    order = sorted((r + stages[n], r, n) for r in range(2 * ROUNDS) for n in range(11))
     order = [(r, n) for _, r, n in order][1:]
-    begun = order.index((1, 9)) + 1
-    beside_heads = order.index((3, 9)) + 1 - begun
-    rest = len(order) - begun - beside_heads
+    order = order[: order.index((7, 4)) + 1]
+    order += [(7, 5), (6, 9), (7, 9), (7, 6), (7, 7), (7, 8), (6, 10), (7, 10)]
+    begun = order.index((1, 10)) + 1
+    beside_heads = order.index((3, 10)) + 1 - begun
     events = Events(step(*at) for at in order)
     events.steps.insert(order.index((7, 4)) + 1, lambda: swap(1).start())
 
@@ -470,6 +482,11 @@
     swap(0).wait_recv()
     stay(0).wait()
     store(4).start()
+    for i in range(512 // ROWS):
+        rows = pl.ds((i % 2) * ROWS, ROWS)
+        x_t[:, i * ROWS : (i + 1) * ROWS] = xs[i // 2, rows, :].astype(f32).T.astype(bf16)
+    store(11).start()
+    store(12).start()
 
     def share(t, n):
         ref = (keys, values)[n].at[pl.ds(2 * t, 2), :, place.k]
@@ -515,6 +532,8 @@
         for tile in range(2):
             ctx[2 * t + tile] = out_t[tile].T.astype(bf16)
         left, right = out_weights(whole(weights.at[0:2, t // 2, t % 2]))
+        wo[t, 0] = left
+        wo[t, 1] = right
         mixed = dot(ctx[2 * t], left, NT) + dot(ctx[2 * t + 1], right, NT)
 
         @pl.when(t == 0)
@@ -529,7 +548,7 @@
         return carry
 
     lax.fori_loop(0, 4, attend, 0)
-    for n in range(5, 9):
+    for n in (5, 6, 7, 8, 13):
         store(n).start()
     norm_gather.wait("y")
     norm_sum = jnp.sum(norms[...].reshape(8, 8, 768), axis=0)
@@ -543,6 +562,7 @@
         value = normed * norm_sum[0:1] + norm_sum[2:3]
         h1[rows, :] = value
         h1b[rows, :] = value.astype(bf16)
+        h1_t[:, rows] = value.T.astype(bf16)
         n1[rows, :] = normed
         o_i1[rows, :] = inv
         acc[rows, :] = jnp.zeros_like(attn)
@@ -555,33 +575,36 @@
     store(9).start()
     store(10).start()
 
-    first_part = order.index((5, 9)) - begun - beside_heads
-    last_part = len(order) - order.index((6, 9))
+    first_part = order.index((5, 10)) - begun - beside_heads
+    middle = len(order) - 7 - order.index((5, 10)) - 1
     counts = {}
     for n in range(first_part):
         at = n * 8 // first_part
         counts[at] = counts.get(at, 0) + 1
     counts[8] = 1
-    middle = rest + 1 - first_part - last_part - 1
     for n in range(middle):
         at = 9 + n * 6 // middle
         counts[at] = counts.get(at, 0) + 1
-    counts[16] = last_part
+    counts[16] = 1
+    counts[18] = counts[22] = 2
+    counts[20] = 3
     stop_f = events.place(12, 2, counts)
     assert not events.steps
 
     def keep_copy(n):
-        return pltpu.make_async_copy(kept.at[n % 2], o_kept.at[n], kept_sems.at[n % 2])
+        at = n // 4 * 4 + (x ^ (n % 4 // 2)) * 2 + (k ^ (n % 2))
+        return pltpu.make_async_copy(kept.at[n % 2], o_kept.at[at], kept_sems.at[n % 2])
 
     def feed(n, carry):
-        r, t = 1 + n // 4, n % 4
+        r = 1 + n // 4
+        wx, wk = x ^ (n % 4 // 2), k ^ (n % 2)
         stop_f(n, 0)
 
         @pl.when(n >= 2)
         def _():
             keep_copy(n - 2).wait()
 
-        ref = weights.at[pl.ds(2 * r, 2), t // 2, t % 2]
+        ref = weights.at[pl.ds(2 * r, 2), wx, wk]
         for start in range(0, 512, CHUNK):
             rows = pl.ds(start, CHUNK)
             w = whole(ref)
@@ -624,7 +647,7 @@
     for t in range(4):
         for n in range(2):
             share(t, n).wait_send()
-    for n in range(11):
+    for n in range(14):
         store(n).wait()
 
 
@@ -647,20 +670,25 @@
         ((8, 512, 128), bf16, any_space),
         ((4, 8, 512), f32, vmem),
         ((12, 3, 512, 256), bf16, any_space),
-        ((512, 768), bf16, any_space),
         ((512, 768), f32, any_space),
         ((512, 1), f32, vmem),
         ((512, 768), f32, vmem),
         ((512, 1), f32, vmem),
         ((512, 768), bf16, vmem),
         ((4, 8, 768), f32, vmem),
+        ((768, 512), bf16, any_space),
+        ((768, 512), bf16, any_space),
+        ((1024, 512), f32, any_space),
+        ((4, 2, 768, 128), bf16, any_space),
     )
     dma = pltpu.SemaphoreType.DMA
     copies = len(GatherRound.names)
     return pl.pallas_call(
         partial(forward_refs, span, len(raw)),
         out_shape=tuple(jax.ShapeDtypeStruct(s, d) for s, d, _ in outs),
-        in_specs=[pl.BlockSpec(memory_space=pltpu.SMEM)] + [vmem] * (len(raw) + 5),
+        in_specs=[pl.BlockSpec(memory_space=pltpu.SMEM)]
+        + [vmem] * (len(raw) + 2)
+        + [any_space, any_space, vmem],
         out_specs=tuple(spec for _, _, spec in outs),
         scratch_shapes=[
             pltpu.VMEM((2 * ROUNDS, 96, 384), bf16),
@@ -674,6 +702,9 @@
             pltpu.VMEM((8, 512, 128), bf16),
             pltpu.VMEM((512, 768), bf16),
             pltpu.VMEM((512, 768), f32),
+            pltpu.VMEM((768, 512), bf16),
+            pltpu.VMEM((768, 512), bf16),
+            pltpu.VMEM((4, 2, 768, 128), bf16),
             pltpu.VMEM((1024, 512), f32),
             pltpu.VMEM((2, 128, 512), f32),
             pltpu.VMEM((512, 768), f32),
@@ -688,7 +719,7 @@
             dma((6,)),
             dma((4, 2)),
             dma((4, 2)),
-            dma((11,)),
+            dma((14,)),
             dma((2,)),
         ],
         compiler_params=pltpu.CompilerParams(
@@ -815,7 +846,6 @@
     slopes,
     i_weights,
     norms,
-    i_x,
     i_cot,
     i_q,
     i_k,
@@ -823,19 +853,22 @@
     i_ctx,
     i_lse,
     i_kept,
-    i_h1b,
     i_n1,
     i_i1,
     i_n2,
     i_i2,
     i_out,
     squares,
-    segments,
+    i_h1_t,
+    i_x_t,
+    i_dist,
+    i_wo,
     o_out,
     o_tokens,
     o_grads,
     o_small,
     w_buf,
+    wo,
     kept,
     h1_t,
     f_t,
@@ -885,8 +918,8 @@
         ScatterRound(
             place,
             held.at[n],
-            twin.at[n % 3],
-            stage,
+            twin.at[n % 6],
+            stage.at[n % 2],
             [
                 ref.at[n]
                 for ref in (land_ay, land_bx, land_ax, land_by, land_z, land_cz, land_dz, land_last)
@@ -895,21 +928,22 @@
             r_recv.at[n],
             r_pair.at[n],
         )
-        for n in range(ROUNDS)
+        for n in range(2 * ROUNDS)
     ]
 
     def load(n):
         src, dst = (
-            (i_cot, d_rows.at[2]),
+            (i_cot, d_rows.at[1]),
             (i_n2, n_buf),
-            (i_h1b, d_rows.at[1]),
-            (i_x, d_rows.at[2]),
+            (i_h1_t, h1_t),
+            (i_x_t, h1_t),
             (i_q, q),
             (i_k, keys),
             (i_v, values),
             (i_ctx, ctx),
             (i_lse, lse),
             (i_n1, n_buf),
+            (i_dist, dist),
         )[n]
         return pltpu.make_async_copy(src, dst, load_sems.at[n])
 
@@ -928,10 +962,12 @@
             i_kept.at[(r - 1) * 4 + wx * 2 + wk], kept.at[n % 2], step_sems.at[n % 2, 1]
         )
 
-    for n in (0, 1, 2, 4, 5, 6, 7, 8):
+    for n in (0, 1):
         load(n).start()
     fetch(0, 0).start()
     fetch(0, 1).start()
+    for n in (2, 4, 5, 6, 7, 8, 10):
+        load(n).start()
     place.greet(ALL_PEERS)
 
     def swap(n):
@@ -960,7 +996,7 @@
     sums = [jnp.zeros((8, 768), f32)] * 2
     for i in range(512 // ROWS):
         rows = pl.ds(i * ROWS, ROWS)
-        grad = halves(d_rows.at[2], i)[...].astype(f32)
+        grad = halves(d_rows.at[1], i)[...].astype(f32)
         normed = n_buf[rows, :]
         out = norm_backward(grad, normed, i_i2[rows, :], norms[1:2])
         d_h1[rows, :] = out
@@ -971,44 +1007,65 @@
     small[1] = sums[0]
     small[3] = sums[1]
     load(9).start()
-    load(3).start()
     load(2).wait()
-    for i in range(512 // ROWS):
-        rows = pl.ds(i * ROWS, ROWS)
-        h1_t[:, rows] = halves(d_rows.at[1], i)[...].astype(f32).T.astype(bf16)
-    fill_distance(dist, segments, place)
 
     def pair(n, dx):
         return lambda: rounds[n].pair_sum(dx)
 
     def step(n, at):
-        return lambda: rounds[n].event(at, o_grads.at[3 - n])
-
-    def put(n, dx, theirs, value, cols):
+        chunk = 3 - n // 2
+        return lambda: rounds[n].event(at, o_grads.at[2 * chunk + n % 2])
+
+    def put(n, dx, theirs, value, start):
         block = value.astype(bf16).reshape(4, 2, 96, value.shape[-1])
+        stop_at = start + value.shape[-1]
+
+        def store(ref_of):
+            for half in range(2):
+                low, high = max(start, 384 * half), min(stop_at, 384 * half + 384)
+                if low < high:
+                    ref_of(half)[:, :, :, low - 384 * half : high - 384 * half] = block[
+                        :, :, :, low - start : high - start
+                    ]
 
         @pl.when(theirs)
         def _():
-            stage[dx, :, :, :, cols] = block
+            store(lambda half: stage.at[half, dx])
 
         @pl.when(jnp.logical_not(theirs))
         def _():
-            held[n, dx, :, :, :, cols] = block
+            store(lambda half: held.at[2 * n + half, dx])
+
+    def pushes(n, dx):
+        return [
+            remote(
+                stage.at[half, dx],
+                twin.at[(2 * n + half) % 6, dx],
+                r_pair.at[2 * n + half, 0, dx],
+                r_pair.at[2 * n + half, 1, dx],
+                place.device(dk=1),
+            )
+            for half in range(2)
+        ]
 
     def push(n, dx):
-        return remote(
-            stage.at[dx], twin.at[n % 3, dx], r_pair.at[n, 0, dx], r_pair.at[n, 1, dx], place.device(dk=1)
-        )
+        for copy in pushes(n, dx):
+            copy.start()
+
+    def pushed(n, dx):
+        for copy in pushes(n, dx):
+            copy.wait_send()
 
     plan = {
-        1: [pair(0, 1)],
-        3: [pair(0, 0)],
-        5: [step(0, 0), pair(1, 1)],
-        7: [step(0, 2), pair(1, 0)],
-        8: [step(0, 1)],
-        9: [step(1, 0), pair(2, 1)],
-        10: [step(0, 3)],
-        11: [step(0, 4), step(1, 2), pair(2, 0)],
+        1: [pair(0, 1), pair(1, 1)],
+        3: [pair(0, 0), pair(1, 0)],
+        5: [step(0, 0), step(1, 0), pair(2, 1), pair(3, 1)],
+        6: [step(0, 1), step(0, 2), step(1, 2)],
+        7: [pair(2, 0), pair(3, 0), step(1, 1)],
+        8: [step(0, 3), step(1, 3)],
+        9: [step(0, 5), step(2, 0), step(3, 0), pair(4, 1), pair(5, 1)],
+        10: [step(0, 4), step(2, 2), step(3, 2), step(2, 1)],
+        11: [step(1, 4), step(1, 5), pair(4, 0), pair(5, 0)],
     }
 
     def feed(n, carry):
@@ -1022,23 +1079,23 @@
 
         @pl.when(jnp.logical_and(theirs, n >= 4))
         def _():
-            push(n // 4 - 1, dx).wait_send()
+            pushed(n // 4 - 1, dx)
 
         fetch(n, 0).wait()
         fetch(n, 1).wait()
         w = whole(w_buf.at[n % 2])
         hold = kept.at[n % 2]
         d_ffn = d_rows[0].reshape(512, 768)
-        put(n // 4, dx, theirs, dot(f_t[...], hold[0]), slice(512, 768))
+        put(n // 4, dx, theirs, dot(f_t[...], hold[0]), 512)
         d_hidden = dot(d_ffn, w[:, 512:])
         d_gate = (d_hidden * hold[2].astype(f32)).astype(bf16)
         d_up = (d_hidden * hold[1].astype(f32)).astype(bf16)
-        put(n // 4, dx, theirs, dot(h1_t[...], d_gate), slice(0, 256))
-        put(n // 4, dx, theirs, dot(h1_t[...], d_up), slice(256, 512))
+        put(n // 4, dx, theirs, dot(h1_t[...], d_gate), 0)
+        put(n // 4, dx, theirs, dot(h1_t[...], d_up), 256)
 
         @pl.when(theirs)
         def _():
-            push(n // 4, dx).start()
+            push(n // 4, dx)
 
         d_h1[...] += dot(d_gate, w[:, :256], NT) + dot(d_up, w[:, 256:512], NT)
         for at, todo in plan.items():
@@ -1052,10 +1109,7 @@
 
     lax.fori_loop(0, 12, feed, 0)
     load(9).wait()
-    load(3).wait()
-    for i in range(512 // ROWS):
-        rows = pl.ds(i * ROWS, ROWS)
-        h1_t[:, rows] = halves(d_rows.at[2], i)[...].astype(f32).T.astype(bf16)
+    load(3).start()
     sums = [jnp.zeros((8, 768), f32)] * 2
     for i in range(512 // ROWS):
         rows = pl.ds(i * ROWS, ROWS)
@@ -1069,7 +1123,7 @@
         sums[1] = sums[1] + columns(grad)
     small[0] = sums[0]
     small[2] = sums[1]
-    for n in range(4, 9):
+    for n in (3, 4, 5, 6, 7, 8, 10):
         load(n).wait()
 
     small[0] = jnp.concatenate(
@@ -1117,7 +1171,12 @@
         wx, wk = where_heads(n)
         return pltpu.make_async_copy(i_weights.at[0:2, wx, wk], w_buf.at[n % 2], step_sems.at[n % 2, 0])
 
+    def fetch_wo(n):
+        wx, wk = where_heads(n)
+        return pltpu.make_async_copy(i_wo.at[wx * 2 + wk], wo.at[n % 2], step_sems.at[n % 2, 1])
+
     fetch_heads(0).start()
+    fetch_wo(0).start()
     dq_t[1, pl.ds(HEAD_DIM, HEAD_DIM), :] = jnp.zeros((HEAD_DIM, 512), f32)
 
     def share(t):
@@ -1126,19 +1185,25 @@
         )
 
     beside = {
-        (0, 0): [small_step(0), step(0, 5)],
-        (0, 2): [small_step(1), step(2, 0)],
-        (0, 4): [small_step(2), step(1, 1)],
-        (1, 0): [small_step(3), step(0, 6)],
-        (1, 2): [step(1, 3)],
-        (1, 4): [small_step(4), step(2, 2)],
-        (2, 0): [step(1, 4)],
-        (2, 2): [step(1, 5)],
-        (2, 5): [step(2, 1)],
-        (3, 0): [pair(3, 1)],
-        (3, 1): [step(1, 6)],
-        (3, 3): [step(2, 3)],
-        (3, 5): [step(2, 4)],
+        (0, 0): [small_step(0), step(0, 6)],
+        (0, 1): [step(3, 1)],
+        (0, 2): [small_step(1), step(2, 3)],
+        (0, 3): [step(3, 3)],
+        (0, 4): [small_step(2), step(4, 0), step(5, 0)],
+        (1, 0): [small_step(3), step(1, 6)],
+        (1, 1): [step(2, 5)],
+        (1, 2): [step(2, 4)],
+        (1, 3): [small_step(4), step(4, 2), step(5, 2)],
+        (1, 5): [step(4, 1)],
+        (2, 0): [step(3, 4), step(3, 5)],
+        (2, 1): [step(2, 6)],
+        (2, 2): [step(5, 1)],
+        (2, 4): [step(4, 3), step(5, 3)],
+        (3, 0): [pair(6, 1), pair(7, 1)],
+        (3, 1): [step(3, 6)],
+        (3, 3): [step(4, 4), step(4, 5)],
+        (3, 5): [step(6, 0), step(7, 0)],
+        (4, 6): [step(5, 4), step(5, 5)],
     }
     first = lax.broadcasted_iota(jnp.int32, (768, 128), 1) < HEAD_DIM
 
@@ -1155,7 +1220,8 @@
         wx, wk = where_heads(n)
         t = wx * 2 + wk
         fetch_heads(n).wait()
-        left, right = out_weights(whole(w_buf.at[n % 2]))
+        fetch_wo(n).wait()
+        left, right = wo[n % 2, 0], wo[n % 2, 1]
         d_attn = d_rows[1].reshape(512, 768)
         d_ctx[0] = dot(d_attn, left).astype(bf16)
         d_ctx[1] = dot(d_attn, right).astype(bf16)
@@ -1202,7 +1268,7 @@
 
         @pl.when(theirs)
         def _():
-            push(2, dx).wait_send()
+            pushed(2, dx)
 
         share(t).wait_recv()
         parts = [q[2 * t], q[2 * t + 1]]
@@ -1223,11 +1289,11 @@
             d_w[:, 512:640],
             jnp.where(first, d_w[:, 640:768], right),
         ]
-        put(3, dx, theirs, jnp.concatenate(tiles, axis=1), slice(0, 768))
+        put(3, dx, theirs, jnp.concatenate(tiles, axis=1), 0)
 
         @pl.when(theirs)
         def _():
-            push(3, dx).start()
+            push(3, dx)
 
         d_h1[...] += dot(d_qkv, whole(w_buf.at[n % 2]), NT)
 
@@ -1240,9 +1306,12 @@
         def _():
             project(n - 1)
 
+        stop(n, 6)
+
         @pl.when(n < 3)
         def _():
             fetch_heads(n + 1).start()
+            fetch_wo(n + 1).start()
 
         return carry
 
@@ -1250,21 +1319,24 @@
     for i in range(512 // ROWS):
         rows = pl.ds(i * ROWS, ROWS)
         halves(d_rows.at[0], i)[...] = d_h1[rows, :].astype(bf16)
-    rounds[3].pair_sum(0)
-    swap(1).start()
-    stay(1).start()
-    step(2, 5)()
-    for at in (0, 1, 2):
-        step(3, at)()
-    step(2, 6)()
-    for at in (3, 4, 5, 6):
-        step(3, at)()
+    for n, at in (
+        [(6, -1), (7, -1)]
+        + [(4, 6), (6, 2), (7, 2), (5, 6), (6, 1), (7, 1), (6, 3), (7, 3)]
+        + [(6, 5), (6, 4), (7, 5), (7, 4), (6, 6), (7, 6)]
+    ):
+        if at < 0:
+            rounds[n].pair_sum(0)
+        else:
+            step(n, at)()
+        if (n, at) == (7, -1):
+            swap(1).start()
+            stay(1).start()
     for n in range(6):
         spread(n).wait_send()
     for r in rounds:
         r.finish()
     for dx in range(2):
-        push(3, dx).wait_send()
+        pushed(3, dx)
     for t in range(4):
         share(t).wait_send()
     for n in range(2):
@@ -1272,33 +1344,34 @@
         stay(n).wait()
 
 
-def backward(span, slopes, saved, segments):
+def backward(span, slopes, saved):
     f32, bf16 = jnp.float32, jnp.bfloat16
     any_space = pl.BlockSpec(memory_space=pl.ANY)
     vmem = pl.BlockSpec(memory_space=pltpu.VMEM)
     dma = pltpu.SemaphoreType.DMA
-    (weights, norms, xs, cot, q, keys, values, ctx, lse, kept, h1b, n1, i1, n2, i2, out, squares) = saved
-    h1b = h1b.reshape(2, 256, 768)
+    (weights, norms, xs, cot, q, keys, values, ctx, lse, kept, n1, i1, n2, i2, out, squares) = saved[:16]
+    h1_t, x_t, dist, wo = saved[16:]
     out = out.reshape(2, 256, 768)
-    in_specs = [pl.BlockSpec(memory_space=pltpu.SMEM), any_space, vmem] + [any_space] * 10
-    in_specs += [vmem, any_space, vmem, any_space, vmem, vmem]
+    in_specs = [pl.BlockSpec(memory_space=pltpu.SMEM), any_space, vmem] + [any_space] * 8
+    in_specs += [vmem, any_space, vmem, any_space, vmem] + [any_space] * 4
     copies = len(ScatterRound.names)
     return pl.pallas_call(
         partial(backward_kernel, span),
         out_shape=(
             jax.ShapeDtypeStruct((2, 256, 768), bf16),
             jax.ShapeDtypeStruct((2, 256, 768), bf16),
-            jax.ShapeDtypeStruct((ROUNDS, 96, 768), f32),
+            jax.ShapeDtypeStruct((2 * ROUNDS, 96, 384), f32),
             jax.ShapeDtypeStruct((8, 768), f32),
         ),
         in_specs=in_specs,
         out_specs=(any_space, any_space, vmem, vmem),
         scratch_shapes=[
             pltpu.VMEM((2, 2, 4, 2, 96, 384), bf16),
+            pltpu.VMEM((2, 2, 768, 128), bf16),
             pltpu.VMEM((2, 3, 512, 256), bf16),
             pltpu.VMEM((768, 512), bf16),
             pltpu.VMEM((768, 512), bf16),
-            pltpu.VMEM((3, 2, 256, 768), bf16),
+            pltpu.VMEM((2, 2, 256, 768), bf16),
             pltpu.VMEM((512, 768), f32),
             pltpu.VMEM((512, 768), f32),
             pltpu.VMEM((8, 512, 128), bf16),
@@ -1313,24 +1386,24 @@
             pltpu.VMEM((2, 128, 512), f32),
             pltpu.VMEM((1024, 128), f32),
             pltpu.VMEM((1024, 128), f32),
-            pltpu.VMEM((ROUNDS, 2, 4, 2, 96, 768), bf16),
-            pltpu.VMEM((3, 2, 4, 2, 96, 768), bf16),
-            pltpu.VMEM((2, 4, 2, 96, 768), bf16),
-            pltpu.VMEM((ROUNDS, 2, 4, 48, 768), bf16),
-            pltpu.VMEM((ROUNDS, 4, 2, 48, 768), bf16),
-            pltpu.VMEM((ROUNDS, 4, 32, 768), bf16),
-            pltpu.VMEM((ROUNDS, 4, 32, 768), bf16),
-            pltpu.VMEM((ROUNDS, 3, 64, 768), bf16),
-            pltpu.VMEM((ROUNDS, 3, 2, 16, 768), bf16),
-            pltpu.VMEM((ROUNDS, 3, 2, 16, 768), bf16),
-            pltpu.VMEM((ROUNDS, 2, 16, 768), bf16),
+            pltpu.VMEM((2 * ROUNDS, 2, 4, 2, 96, 384), bf16),
+            pltpu.VMEM((6, 2, 4, 2, 96, 384), bf16),
+            pltpu.VMEM((2, 2, 4, 2, 96, 384), bf16),
+            pltpu.VMEM((2 * ROUNDS, 2, 4, 48, 384), bf16),
+            pltpu.VMEM((2 * ROUNDS, 4, 2, 48, 384), bf16),
+            pltpu.VMEM((2 * ROUNDS, 4, 32, 384), bf16),
+            pltpu.VMEM((2 * ROUNDS, 4, 32, 384), bf16),
+            pltpu.VMEM((2 * ROUNDS, 3, 64, 384), bf16),
+            pltpu.VMEM((2 * ROUNDS, 3, 2, 16, 384), bf16),
+            pltpu.VMEM((2 * ROUNDS, 3, 2, 16, 384), bf16),
+            pltpu.VMEM((2 * ROUNDS, 2, 16, 384), bf16),
             pltpu.VMEM((4, 8, 768), f32),
             pltpu.VMEM((6, 8, 768), f32),
-            dma((10,)),
+            dma((11,)),
             dma((2, 2)),
-            dma((ROUNDS, copies)),
-            dma((ROUNDS, copies)),
-            dma((ROUNDS, 2, 2)),
+            dma((2 * ROUNDS, copies)),
+            dma((2 * ROUNDS, copies)),
+            dma((2 * ROUNDS, 2, 2)),
             dma((6,)),
             dma((4,)),
             dma((4,)),
@@ -1345,7 +1418,6 @@
         slopes,
         weights,
         norms,
-        xs,
         cot,
         q,
         keys,
@@ -1353,14 +1425,16 @@
         ctx,
         lse,
         kept,
-        h1b,
         n1,
         i1,
         n2,
         i2,
         out,
         squares,
-        segments,
+        h1_t,
+        x_t,
+        dist,
+        wo,
     )
 
 
@@ -1373,9 +1447,14 @@
     move(0, lo, rows.at[0]).start()
     move(1, gt, rows.at[1]).start()
     turned = []
+
+    def tile(i):
+        return grads[i // 3, :, i % 3 * 128 : i % 3 * 128 + 128]
+
     for c in range(3):
-        o_qkv[c] = grads[0, :, c * 256 : c * 256 + 192]
-        turned.append(grads[0, :, c * 256 + 128 : c * 256 + 256].T[HEAD_DIM:])
+        o_qkv[c, :, 0:128] = tile(2 * c)
+        o_qkv[c, :, 128:192] = tile(2 * c + 1)[:, :HEAD_DIM]
+        turned.append(tile(2 * c + 1).T[HEAD_DIM:])
     o_wout[...] = jnp.concatenate(turned, axis=0)
     move(0, lo, rows.at[0]).wait()
     move(2, rows.at[0], o_lo).start()
@@ -1383,9 +1462,10 @@
     move(3, rows.at[1], o_gt).start()
     for r in range(3):
         units = slice(r * 256, (r + 1) * 256)
-        o_win[:, 0, units] = grads[1 + r, :, 0:256]
-        o_win[:, 1, units] = grads[1 + r, :, 256:512]
-        o_down[units, :] = grads[1 + r, :, 512:768].T
+        o_win[:, 0, units] = grads[2 + 2 * r, :, 0:256]
+        o_win[:, 1, r * 256 : r * 256 + 128] = grads[2 + 2 * r, :, 256:384]
+        o_win[:, 1, r * 256 + 128 : r * 256 + 256] = grads[3 + 2 * r, :, 0:128]
+        o_down[units, :] = grads[3 + 2 * r, :, 128:384].T
     mine = pltpu.roll(small[...], 768 - block[0] * 96, 1)
     o_gains[...] = mine[0:2, 0:96]
     o_biases[...] = mine[2:4, 0:96]
@@ -1432,7 +1512,7 @@
     f32 = jnp.float32
     shard_rows = query_key_value_weight.shape[1]
     span = 96 // shard_rows
-    slopes = jnp.exp2(-8.0 * (jnp.arange(HEADS).astype(f32) + 1.0) / HEADS)
+    slopes = jnp.asarray([2.0 ** (-8.0 * (h + 1) / HEADS) for h in range(HEADS)], f32)
     cells = float(lax.axis_size("fsdp") * 2 * 1024 * 768)
     if span == 1:
         raw = (query_key_value_weight, w_out, input_weight, w_down)
@@ -1454,7 +1534,7 @@
         )
 
     saved = forward(span, slopes, raw, gains, biases, tokens, cotangent, segment_ids)
-    layer_out, grad_tokens, grads, small = backward(span, slopes, saved, segment_ids)
+    layer_out, grad_tokens, grads, small = backward(span, slopes, saved)
 
     if span == 1:
         block = lax.axis_index("fsdp").astype(jnp.int32).reshape(1)
@@ -1464,6 +1544,7 @@
             grads, "fsdp", scatter_dimension=1, tiled=True, axis_index_groups=groups
         )
         small = lax.psum(small, "fsdp", axis_index_groups=groups)
+        grads = grads.reshape(4, 2, shard_rows, 384).transpose(0, 2, 1, 3)
         grads_a = grads[0].reshape(shard_rows, 3, 4, HEAD_DIM)
         grads_f = grads[1:].reshape(3, shard_rows, 3, 256)
         shard_start = lax.axis_index("fsdp") * shard_rows

time: 252 us -> 253 us (level)
  no operation moved by 1% of the time
where the time goes in v5:
time: 253 us
  Pallas kernels  248 us (98%)
  local copies, waits for them, and re-layouts  3.6 us (1%)
    pallas_call x1, Pallas kernels, backward(): pl.pallas_call(partial(backward_kernel, span), out_shape=(jax.ShapeDtypeS...  131 us
    pallas_call x1, Pallas kernels, forward(): pl.pallas_call(partial(forward_refs, span, len(raw)), out_shape=tuple((ja...  113 us

profile of v5, /device:TPU:0, one launch (start us, length us, event | category | flops | bytes accessed | tf_op | source)
XLA Modules:
  0.0 252.9 jit_solution(11399230769329433125)
XLA Ops:
  0.6 1.7 copy.19.refs_4_
  2.4 112.7 %forward.1 = (bf16[8,2,2,4,2,96,384]{6,5,4,3,2,1,0:T(8,128)(2,1)}, f32[8,768]{1,0:T(8,128)}, bf16[2,256,768]{2,1,0:T(8,128)(2,1)}, bf16[2,256,768]{2,1,0:T(8,128...) custom-call(f32[12]{0:T(128)} %constant.13.clone.refs_0_.slopes, ...), custom_call_target="tpu_custom_call" | custom-call | tf_op jit(solution)/shard_map/forward/pallas_call | solution.py:686
  115.0 130.7 %backward.1 = (bf16[2,256,768]{2,1,0:T(8,128)(2,1)}, bf16[2,256,768]{2,1,0:T(8,128)(2,1)}, f32[8,96,384]{2,1,0:T(8,128)}, f32[8,768]{1,0:T(8,128)}) custom-call(f32[12]{0:T(128)} %constant.13.clone.refs_0_.slopes, bf16[8,2,2,4,2,96,384]{6,5,4,3,2,1,0:T(8,128)(2,1)} %get-tuple-element.40.i_weights, f32[8,768]{1,0:T(8,128)} %get-tuple-element.41.norms, ...), custom_call_target="tpu_custom_call" | custom-call | tf_op jit(solution)/shard_map/backward/pallas_call | solution.py:1358
  245.7 0.0 copy-start
  245.7 4.7 %finish.1 = (bf16[2,256,768]{2,1,0:T(8,128)(2,1)}, bf16[2,256,768]{2,1,0:T(8,128)(2,1)}, f32[3,96,192]{2,1,0:T(8,128)}, f32[192,96]{1,0:T(8,128)}, f32[96,2,768]...) custom-call(s32[1]{0:T(128)} %bitcast.block, f32[8,96,384]{2,1,0:T(8,128)} %get-tuple-element.59.grads, ...), custom_call_target="tpu_custom_call" | custom-call | tf_op jit(solution)/shard_map/finish/pallas_call | solution.py:1481
  250.4 1.9 copy.20
  252.3 0.0 copy-done
  252.3 0.1 slice_reduce_fusion
  252.4 0.5 multiply_sqrt_fusion
Async XLA Ops:
  245.7 6.6 %copy-start = (f32[8,768]{1,0:T(8,128)S(1)}, f32[8,768]{1,0:T(8,128)}, u32[]{:S(2)}) copy-start(f32[8,768]{1,0:T(8,128)} %get-tuple-element.60.small) | copy-start | bytes 73732

commit v6 on v5

--- a/solution.py
+++ b/solution.py
@@ -889,7 +889,6 @@
     acc_v,
     held,
     twin,
-    stage,
     land_ay,
     land_bx,
     land_ax,
@@ -919,7 +918,7 @@
             place,
             held.at[n],
             twin.at[n % 6],
-            stage.at[n % 2],
+            held.at[2 * ROUNDS + n % 2],
             [
                 ref.at[n]
                 for ref in (land_ay, land_bx, land_ax, land_by, land_z, land_cz, land_dz, land_last)
@@ -1019,27 +1018,18 @@
     def put(n, dx, theirs, value, start):
         block = value.astype(bf16).reshape(4, 2, 96, value.shape[-1])
         stop_at = start + value.shape[-1]
-
-        def store(ref_of):
-            for half in range(2):
-                low, high = max(start, 384 * half), min(stop_at, 384 * half + 384)
-                if low < high:
-                    ref_of(half)[:, :, :, low - 384 * half : high - 384 * half] = block[
-                        :, :, :, low - start : high - start
-                    ]
-
-        @pl.when(theirs)
-        def _():
-            store(lambda half: stage.at[half, dx])
-
-        @pl.when(jnp.logical_not(theirs))
-        def _():
-            store(lambda half: held.at[2 * n + half, dx])
+        for half in range(2):
+            low, high = max(start, 384 * half), min(stop_at, 384 * half + 384)
+            if low < high:
+                slot = theirs * (2 * ROUNDS + half) + (1 - theirs) * (2 * n + half)
+                held[slot, dx, :, :, :, low - 384 * half : high - 384 * half] = block[
+                    :, :, :, low - start : high - start
+                ]
 
     def pushes(n, dx):
         return [
             remote(
-                stage.at[half, dx],
+                held.at[2 * ROUNDS + half, dx],
                 twin.at[(2 * n + half) % 6, dx],
                 r_pair.at[2 * n + half, 0, dx],
                 r_pair.at[2 * n + half, 1, dx],
@@ -1056,28 +1046,40 @@
         for copy in pushes(n, dx):
             copy.wait_send()
 
-    plan = {
+    between = {
+        5: [step(0, 0), step(1, 0)],
+        6: [step(0, 1)],
+        8: [step(0, 2), step(1, 1)],
+        9: [step(1, 2)],
+        10: [step(0, 3), step(1, 3)],
+        11: [step(0, 5), step(2, 0), step(3, 0)],
+    }
+    after = {
         1: [pair(0, 1), pair(1, 1)],
         3: [pair(0, 0), pair(1, 0)],
-        5: [step(0, 0), step(1, 0), pair(2, 1), pair(3, 1)],
-        6: [step(0, 1), step(0, 2), step(1, 2)],
-        7: [pair(2, 0), pair(3, 0), step(1, 1)],
-        8: [step(0, 3), step(1, 3)],
-        9: [step(0, 5), step(2, 0), step(3, 0), pair(4, 1), pair(5, 1)],
-        10: [step(0, 4), step(2, 2), step(3, 2), step(2, 1)],
-        11: [step(1, 4), step(1, 5), pair(4, 0), pair(5, 0)],
+        5: [pair(2, 1), pair(3, 1)],
+        7: [pair(2, 0), pair(3, 0)],
+        11: [pair(4, 1), pair(5, 1), pair(4, 0), pair(5, 0)],
     }
+
+    def go(n, plan):
+        for at, todo in plan.items():
+
+            @pl.when(n == at)
+            def _():
+                for item in todo:
+                    item()
 
     def feed(n, carry):
         dx = 1 - n % 4 // 2
-        theirs = n % 2 == 0
+        theirs = 1 - n % 2
 
         @pl.when(n < 11)
         def _():
             fetch(n + 1, 0).start()
             fetch(n + 1, 1).start()
 
-        @pl.when(jnp.logical_and(theirs, n >= 4))
+        @pl.when(jnp.logical_and(theirs == 1, n >= 4))
         def _():
             pushed(n // 4 - 1, dx)
 
@@ -1086,25 +1088,20 @@
         w = whole(w_buf.at[n % 2])
         hold = kept.at[n % 2]
         d_ffn = d_rows[0].reshape(512, 768)
-        put(n // 4, dx, theirs, dot(f_t[...], hold[0]), 512)
         d_hidden = dot(d_ffn, w[:, 512:])
         d_gate = (d_hidden * hold[2].astype(f32)).astype(bf16)
         d_up = (d_hidden * hold[1].astype(f32)).astype(bf16)
-        put(n // 4, dx, theirs, dot(h1_t[...], d_gate), 0)
-        put(n // 4, dx, theirs, dot(h1_t[...], d_up), 256)
-
-        @pl.when(theirs)
+        d_projected = jnp.concatenate([d_gate, d_up], axis=1)
+        put(n // 4, dx, theirs, dot(f_t[...], hold[0]), 512)
+        go(n, between)
+        put(n // 4, dx, theirs, dot(h1_t[...], d_projected), 0)
+
+        @pl.when(theirs == 1)
         def _():
             push(n // 4, dx)
 
-        d_h1[...] += dot(d_gate, w[:, :256], NT) + dot(d_up, w[:, 256:512], NT)
-        for at, todo in plan.items():
-
-            @pl.when(n == at)
-            def _():
-                for item in todo:
-                    item()
-
+        go(n, after)
+        d_h1[...] += dot(d_projected, w[:, :512], NT)
         return carry
 
     lax.fori_loop(0, 12, feed, 0)
@@ -1185,25 +1182,25 @@
         )
 
     beside = {
-        (0, 0): [small_step(0), step(0, 6)],
-        (0, 1): [step(3, 1)],
-        (0, 2): [small_step(1), step(2, 3)],
-        (0, 3): [step(3, 3)],
-        (0, 4): [small_step(2), step(4, 0), step(5, 0)],
-        (1, 0): [small_step(3), step(1, 6)],
-        (1, 1): [step(2, 5)],
-        (1, 2): [step(2, 4)],
-        (1, 3): [small_step(4), step(4, 2), step(5, 2)],
-        (1, 5): [step(4, 1)],
-        (2, 0): [step(3, 4), step(3, 5)],
-        (2, 1): [step(2, 6)],
-        (2, 2): [step(5, 1)],
-        (2, 4): [step(4, 3), step(5, 3)],
+        (0, 0): [small_step(0), step(0, 4)],
+        (0, 1): [step(2, 1)],
+        (0, 2): [small_step(1), step(1, 5)],
+        (0, 3): [step(2, 2)],
+        (0, 4): [small_step(2)],
+        (0, 5): [step(3, 2)],
+        (1, 0): [small_step(3), step(1, 4), step(3, 1), step(0, 6)],
+        (1, 2): [step(2, 3), step(3, 3)],
+        (1, 3): [small_step(4), step(2, 5)],
+        (1, 5): [step(2, 4), step(1, 6)],
+        (2, 0): [step(3, 5), step(3, 4), step(4, 0), step(5, 0)],
+        (2, 2): [step(4, 1), step(4, 2), step(5, 2)],
+        (2, 4): [step(2, 6)],
+        (2, 5): [step(3, 6)],
         (3, 0): [pair(6, 1), pair(7, 1)],
-        (3, 1): [step(3, 6)],
-        (3, 3): [step(4, 4), step(4, 5)],
-        (3, 5): [step(6, 0), step(7, 0)],
-        (4, 6): [step(5, 4), step(5, 5)],
+        (3, 1): [step(5, 1)],
+        (3, 3): [step(4, 3), step(5, 3)],
+        (3, 5): [step(4, 5), step(4, 4)],
+        (4, 6): [step(6, 0), step(7, 0), step(5, 5), step(5, 4)],
     }
     first = lax.broadcasted_iota(jnp.int32, (768, 128), 1) < HEAD_DIM
 
@@ -1264,9 +1261,9 @@
         wx, wk = where_heads(n)
         t = wx * 2 + wk
         dx = 1 - n // 2
-        theirs = wk != k
-
-        @pl.when(theirs)
+        theirs = wk ^ k
+
+        @pl.when(theirs == 1)
         def _():
             pushed(2, dx)
 
@@ -1278,20 +1275,14 @@
                 mine = mine + d_kv_in[t, kind, tile].reshape(512, 128).astype(f32)
                 parts.append(mine.astype(bf16))
         d_qkv = jnp.concatenate(parts, axis=1)
-        d_w = dot(h1_t[...], d_qkv)
-        left = dot(f_t[...], ctx[2 * t])
-        right = swap_halves(dot(f_t[...], ctx[2 * t + 1]))
-        tiles = [
-            d_w[:, 0:128],
-            jnp.where(first, d_w[:, 128:256], pltpu.roll(left, HEAD_DIM, 1)),
-            d_w[:, 256:384],
-            jnp.where(first, d_w[:, 384:512], left),
-            d_w[:, 512:640],
-            jnp.where(first, d_w[:, 640:768], right),
-        ]
-        put(3, dx, theirs, jnp.concatenate(tiles, axis=1), 0)
-
-        @pl.when(theirs)
+        d_wo = dot(f_t[...], jnp.concatenate([ctx[2 * t], ctx[2 * t + 1]], axis=1))
+        turned = (swap_halves(d_wo[:, :128]), d_wo[:, :128], swap_halves(d_wo[:, 128:]))
+        for kind in range(3):
+            d_w = dot(h1_t[...], d_qkv[:, 256 * kind : 256 * kind + 256])
+            put(3, dx, theirs, d_w[:, :128], 256 * kind)
+            put(3, dx, theirs, jnp.where(first, d_w[:, 128:], turned[kind]), 256 * kind + 128)
+
+        @pl.when(theirs == 1)
         def _():
             push(3, dx)
 
@@ -1321,7 +1312,7 @@
         halves(d_rows.at[0], i)[...] = d_h1[rows, :].astype(bf16)
     for n, at in (
         [(6, -1), (7, -1)]
-        + [(4, 6), (6, 2), (7, 2), (5, 6), (6, 1), (7, 1), (6, 3), (7, 3)]
+        + [(6, 1), (4, 6), (7, 1), (6, 2), (7, 2), (5, 6), (6, 3), (7, 3)]
         + [(6, 5), (6, 4), (7, 5), (7, 4), (6, 6), (7, 6)]
     ):
         if at < 0:
@@ -1386,9 +1377,8 @@
             pltpu.VMEM((2, 128, 512), f32),
             pltpu.VMEM((1024, 128), f32),
             pltpu.VMEM((1024, 128), f32),
-            pltpu.VMEM((2 * ROUNDS, 2, 4, 2, 96, 384), bf16),
+            pltpu.VMEM((2 * ROUNDS + 2, 2, 4, 2, 96, 384), bf16),
             pltpu.VMEM((6, 2, 4, 2, 96, 384), bf16),
-            pltpu.VMEM((2, 2, 4, 2, 96, 384), bf16),
             pltpu.VMEM((2 * ROUNDS, 2, 4, 48, 384), bf16),
             pltpu.VMEM((2 * ROUNDS, 4, 2, 48, 384), bf16),
             pltpu.VMEM((2 * ROUNDS, 4, 32, 384), bf16),

time: 253 us -> 247 us (0.976)
  Pallas kernels: 248 us -> 242 us
    pallas_call x1, Pallas kernels: 131 us -> 124 us  [backward(): pl.pallas_call(partial(backward_kernel, span), out_shape=(jax.ShapeDtypeS...]
where the time goes in v6:
time: 247 us
  Pallas kernels  242 us (98%)
  local copies, waits for them, and re-layouts  3.6 us (1%)
    pallas_call x1, Pallas kernels, backward(): pl.pallas_call(partial(backward_kernel, span), out_shape=(jax.ShapeDtypeS...  124 us
    pallas_call x1, Pallas kernels, forward(): pl.pallas_call(partial(forward_refs, span, len(raw)), out_shape=tuple((ja...  113 us

profile of v6, /device:TPU:0, one launch (start us, length us, event | category | flops | bytes accessed | tf_op | source)
XLA Modules:
  0.0 246.7 jit_solution(1752210305357137579)
XLA Ops:
  0.6 1.7 copy.19.refs_4_
  2.4 112.7 %forward.1 = (bf16[8,2,2,4,2,96,384]{6,5,4,3,2,1,0:T(8,128)(2,1)}, f32[8,768]{1,0:T(8,128)}, bf16[2,256,768]{2,1,0:T(8,128)(2,1)}, bf16[2,256,768]{2,1,0:T(8,128...) custom-call(f32[12]{0:T(128)} %constant.13.clone.refs_0_.slopes, ...), custom_call_target="tpu_custom_call" | custom-call | tf_op jit(solution)/shard_map/forward/pallas_call | solution.py:686
  115.0 124.5 %backward.1 = (bf16[2,256,768]{2,1,0:T(8,128)(2,1)}, bf16[2,256,768]{2,1,0:T(8,128)(2,1)}, f32[8,96,384]{2,1,0:T(8,128)}, f32[8,768]{1,0:T(8,128)}) custom-call(f32[12]{0:T(128)} %constant.13.clone.refs_0_.slopes, bf16[8,2,2,4,2,96,384]{6,5,4,3,2,1,0:T(8,128)(2,1)} %get-tuple-element.40.i_weights, f32[8,768]{1,0:T(8,128)} %get-tuple-element.41.norms, ...), custom_call_target="tpu_custom_call" | custom-call | tf_op jit(solution)/shard_map/backward/pallas_call | solution.py:1349
  239.5 0.0 copy-start
  239.5 4.7 %finish.1 = (bf16[2,256,768]{2,1,0:T(8,128)(2,1)}, bf16[2,256,768]{2,1,0:T(8,128)(2,1)}, f32[3,96,192]{2,1,0:T(8,128)}, f32[192,96]{1,0:T(8,128)}, f32[96,2,768]...) custom-call(s32[1]{0:T(128)} %bitcast.block, f32[8,96,384]{2,1,0:T(8,128)} %get-tuple-element.59.grads, ...), custom_call_target="tpu_custom_call" | custom-call | tf_op jit(solution)/shard_map/finish/pallas_call | solution.py:1471
  244.2 1.9 copy.20
  246.0 0.0 copy-done
  246.1 0.1 slice_reduce_fusion
  246.2 0.5 multiply_sqrt_fusion
Async XLA Ops:
  239.5 6.6 %copy-start = (f32[8,768]{1,0:T(8,128)S(1)}, f32[8,768]{1,0:T(8,128)}, u32[]{:S(2)}) copy-start(f32[8,768]{1,0:T(8,128)} %get-tuple-element.60.small) | copy-start | bytes 73732

commit v7 on v6

--- a/solution.py
+++ b/solution.py
@@ -468,6 +468,9 @@
     order = [(r, n) for _, r, n in order][1:]
     order = order[: order.index((7, 4)) + 1]
     order += [(7, 5), (6, 9), (7, 9), (7, 6), (7, 7), (7, 8), (6, 10), (7, 10)]
+    head_part = order[: order.index((1, 10)) + 1]
+    later = [at for at in head_part if at[0] >= 2 and at not in ((2, 0), (2, 1), (2, 2), (3, 0))]
+    order = [at for at in head_part if at not in later] + later + order[len(head_part) :]
     begun = order.index((1, 10)) + 1
     beside_heads = order.index((3, 10)) + 1 - begun
     events = Events(step(*at) for at in order)
@@ -1182,24 +1185,24 @@
         )
 
     beside = {
-        (0, 0): [small_step(0), step(0, 4)],
-        (0, 1): [step(2, 1)],
-        (0, 2): [small_step(1), step(1, 5)],
-        (0, 3): [step(2, 2)],
-        (0, 4): [small_step(2)],
-        (0, 5): [step(3, 2)],
-        (1, 0): [small_step(3), step(1, 4), step(3, 1), step(0, 6)],
-        (1, 2): [step(2, 3), step(3, 3)],
-        (1, 3): [small_step(4), step(2, 5)],
-        (1, 5): [step(2, 4), step(1, 6)],
-        (2, 0): [step(3, 5), step(3, 4), step(4, 0), step(5, 0)],
-        (2, 2): [step(4, 1), step(4, 2), step(5, 2)],
-        (2, 4): [step(2, 6)],
-        (2, 5): [step(3, 6)],
-        (3, 0): [pair(6, 1), pair(7, 1)],
-        (3, 1): [step(5, 1)],
-        (3, 3): [step(4, 3), step(5, 3)],
-        (3, 5): [step(4, 5), step(4, 4)],
+        (1, 6): [small_step(0), step(0, 4)],
+        (2, 0): [step(2, 1)],
+        (2, 1): [small_step(1), step(1, 5)],
+        (2, 2): [step(2, 2)],
+        (2, 3): [small_step(2)],
+        (2, 4): [step(3, 2)],
+        (2, 6): [
+            small_step(3), step(1, 4), step(3, 1), step(0, 6), pair(6, 1),
+            pair(7, 1),
+        ],
+        (3, 1): [step(2, 3), step(3, 3)],
+        (3, 2): [small_step(4), step(2, 5)],
+        (3, 4): [step(2, 4), step(1, 6)],
+        (3, 6): [
+            step(3, 5), step(3, 4), step(4, 0), step(5, 0), step(4, 1),
+            step(4, 2), step(5, 2), step(2, 6), step(3, 6), step(5, 1),
+            step(4, 3), step(5, 3), step(4, 5), step(4, 4),
+        ],
         (4, 6): [step(6, 0), step(7, 0), step(5, 5), step(5, 4)],
     }
     first = lax.broadcasted_iota(jnp.int32, (768, 128), 1) < HEAD_DIM

time: 247 us -> 240 us (0.972)
  Pallas kernels: 242 us -> 234 us
    pallas_call x1, Pallas kernels: 124 us -> 119 us  [backward(): pl.pallas_call(partial(backward_kernel, span), out_shape=(jax.ShapeDtypeS...]
where the time goes in v7:
time: 240 us; the launch traced here: 239 us
  Pallas kernels  234 us (98%)
  local copies, waits for them, and re-layouts  3.6 us (2%)
    pallas_call x1, Pallas kernels, backward(): pl.pallas_call(partial(backward_kernel, span), out_shape=(jax.ShapeDtypeS...  119 us
    pallas_call x1, Pallas kernels, forward(): pl.pallas_call(partial(forward_refs, span, len(raw)), out_shape=tuple((ja...  111 us

profile of v7, /device:TPU:0, one launch (start us, length us, event | category | flops | bytes accessed | tf_op | source)
XLA Modules:
  0.0 239.4 jit_solution(1537562722798699354)
XLA Ops:
  0.6 1.7 copy.19.refs_4_
  2.4 111.2 %forward.1 = (bf16[8,2,2,4,2,96,384]{6,5,4,3,2,1,0:T(8,128)(2,1)}, f32[8,768]{1,0:T(8,128)}, bf16[2,256,768]{2,1,0:T(8,128)(2,1)}, bf16[2,256,768]{2,1,0:T(8,128...) custom-call(f32[12]{0:T(128)} %constant.13.clone.refs_0_.slopes, ...), custom_call_target="tpu_custom_call" | custom-call | tf_op jit(solution)/shard_map/forward/pallas_call | solution.py:689
  113.6 118.6 %backward.1 = (bf16[2,256,768]{2,1,0:T(8,128)(2,1)}, bf16[2,256,768]{2,1,0:T(8,128)(2,1)}, f32[8,96,384]{2,1,0:T(8,128)}, f32[8,768]{1,0:T(8,128)}) custom-call(f32[12]{0:T(128)} %constant.13.clone.refs_0_.slopes, bf16[8,2,2,4,2,96,384]{6,5,4,3,2,1,0:T(8,128)(2,1)} %get-tuple-element.40.i_weights, f32[8,768]{1,0:T(8,128)} %get-tuple-element.41.norms, ...), custom_call_target="tpu_custom_call" | custom-call | tf_op jit(solution)/shard_map/backward/pallas_call | solution.py:1352
  232.2 0.0 copy-start
  232.2 4.7 %finish.1 = (bf16[2,256,768]{2,1,0:T(8,128)(2,1)}, bf16[2,256,768]{2,1,0:T(8,128)(2,1)}, f32[3,96,192]{2,1,0:T(8,128)}, f32[192,96]{1,0:T(8,128)}, f32[96,2,768]...) custom-call(s32[1]{0:T(128)} %bitcast.block, f32[8,96,384]{2,1,0:T(8,128)} %get-tuple-element.59.grads, ...), custom_call_target="tpu_custom_call" | custom-call | tf_op jit(solution)/shard_map/finish/pallas_call | solution.py:1474
  236.9 1.9 copy.20
  238.7 0.0 copy-done
  238.8 0.1 slice_reduce_fusion
  238.9 0.5 multiply_sqrt_fusion
Async XLA Ops:
  232.2 6.6 %copy-start = (f32[8,768]{1,0:T(8,128)S(1)}, f32[8,768]{1,0:T(8,128)}, u32[]{:S(2)}) copy-start(f32[8,768]{1,0:T(8,128)} %get-tuple-element.60.small) | copy-start | bytes 73732

commit v8 on v7

--- a/solution.py
+++ b/solution.py
@@ -277,8 +277,7 @@
 
 
 def pack_feed(raw, shard):
-    w_in, w_down = raw[2:]
-    turned = w_down[...].astype(jnp.float32).T.astype(jnp.bfloat16)
+    w_in, w_down_t = raw[2:]
     for r in range(3):
         units = slice(r * 256, (r + 1) * 256)
         first = slice(r * 256, r * 256 + 128)
@@ -286,7 +285,7 @@
         shard[2 + 2 * r, :, 0:256] = w_in[:, 0, units]
         shard[2 + 2 * r, :, 256:384] = w_in[:, 1, first]
         shard[3 + 2 * r, :, 0:128] = w_in[:, 1, second]
-        shard[3 + 2 * r, :, 128:384] = turned[:, units]
+        shard[3 + 2 * r, :, 128:384] = w_down_t[:, units]
 
 
 def out_weights(w):
@@ -1432,7 +1431,7 @@
 
 
 def finish_kernel(
-    block, grads, small, lo, gt, o_lo, o_gt, o_qkv, o_wout, o_win, o_down, o_gains, o_biases, rows, sems
+    block, grads, small, lo, gt, o_lo, o_gt, o_qkv, o_wout, o_win, o_down_t, o_gains, o_biases, rows, sems
 ):
     def move(n, src, dst):
         return pltpu.make_async_copy(src, dst, sems.at[n])
@@ -1458,7 +1457,7 @@
         o_win[:, 0, units] = grads[2 + 2 * r, :, 0:256]
         o_win[:, 1, r * 256 : r * 256 + 128] = grads[2 + 2 * r, :, 256:384]
         o_win[:, 1, r * 256 + 128 : r * 256 + 256] = grads[3 + 2 * r, :, 0:128]
-        o_down[units, :] = grads[3 + 2 * r, :, 128:384].T
+        o_down_t[:, units] = grads[3 + 2 * r, :, 128:384]
     mine = pltpu.roll(small[...], 768 - block[0] * 96, 1)
     o_gains[...] = mine[0:2, 0:96]
     o_biases[...] = mine[2:4, 0:96]
@@ -1479,7 +1478,7 @@
             shape((3, 96, 192), f32),
             shape((192, 96), f32),
             shape((96, 2, 768), f32),
-            shape((768, 96), f32),
+            shape((96, 768), f32),
             shape((2, 96), f32),
             shape((2, 96), f32),
         ),
@@ -1508,7 +1507,7 @@
     slopes = jnp.asarray([2.0 ** (-8.0 * (h + 1) / HEADS) for h in range(HEADS)], f32)
     cells = float(lax.axis_size("fsdp") * 2 * 1024 * 768)
     if span == 1:
-        raw = (query_key_value_weight, w_out, input_weight, w_down)
+        raw = (query_key_value_weight, w_out, input_weight, w_down.T)
         gains, biases = norm_gains, norm_biases
     else:
         count = lax.axis_size("fsdp")
@@ -1532,6 +1531,7 @@
     if span == 1:
         block = lax.axis_index("fsdp").astype(jnp.int32).reshape(1)
         outs = finish(block, grads, small, layer_out, grad_tokens)
+        outs = outs[:5] + (outs[5].T,) + outs[6:]
     else:
         grads = lax.psum_scatter(
             grads, "fsdp", scatter_dimension=1, tiled=True, axis_index_groups=groups

time: 240 us -> 236 us (0.983)
  local copies, waits for them, and re-layouts: 3.6 us -> 0.01 us
    unnamed x4 -> x2, local copies, waits for them, and re-layouts: 3.6 us -> 0.01 us
where the time goes in v8:
time: 236 us
  Pallas kernels  234 us (99%)
    pallas_call x1, Pallas kernels, backward(): pl.pallas_call(partial(backward_kernel, span), out_shape=(jax.ShapeDtypeS...  119 us
    pallas_call x1, Pallas kernels, forward(): pl.pallas_call(partial(forward_refs, span, len(raw)), out_shape=tuple((ja...  111 us

profile of v8, /device:TPU:0, one launch (start us, length us, event | category | flops | bytes accessed | tf_op | source)
XLA Modules:
  0.0 235.8 jit_solution(9010146510408484173)
XLA Ops:
  0.6 111.3 %forward.1 = (bf16[8,2,2,4,2,96,384]{6,5,4,3,2,1,0:T(8,128)(2,1)}, f32[8,768]{1,0:T(8,128)}, bf16[2,256,768]{2,1,0:T(8,128)(2,1)}, bf16[2,256,768]{2,1,0:T(8,128...) custom-call(f32[12]{0:T(128)} %constant.13.clone.refs_0_.slopes, ...), custom_call_target="tpu_custom_call" | custom-call | tf_op jit(solution)/shard_map/forward/pallas_call | solution.py:688
  111.9 118.6 %backward.1 = (bf16[2,256,768]{2,1,0:T(8,128)(2,1)}, bf16[2,256,768]{2,1,0:T(8,128)(2,1)}, f32[8,96,384]{2,1,0:T(8,128)}, f32[8,768]{1,0:T(8,128)}) custom-call(f32[12]{0:T(128)} %constant.13.clone.refs_0_.slopes, bf16[8,2,2,4,2,96,384]{6,5,4,3,2,1,0:T(8,128)(2,1)} %get-tuple-element.40.i_weights, f32[8,768]{1,0:T(8,128)} %get-tuple-element.41.norms, ...), custom_call_target="tpu_custom_call" | custom-call | tf_op jit(solution)/shard_map/backward/pallas_call | solution.py:1351
  230.5 0.0 copy-start
  230.5 4.6 %finish.1 = (bf16[2,256,768]{2,1,0:T(8,128)(2,1)}, bf16[2,256,768]{2,1,0:T(8,128)(2,1)}, f32[3,96,192]{2,1,0:T(8,128)}, f32[192,96]{1,0:T(8,128)}, f32[96,2,768]...) custom-call(s32[1]{0:T(128)} %bitcast.block, f32[8,96,384]{2,1,0:T(8,128)} %get-tuple-element.59.grads, ...), custom_call_target="tpu_custom_call" | custom-call | tf_op jit(solution)/shard_map/finish/pallas_call | solution.py:1473
  235.2 0.0 copy-done
  235.2 0.1 slice_reduce_fusion
  235.3 0.5 multiply_sqrt_fusion
Async XLA Ops:
  230.5 4.7 %copy-start = (f32[8,768]{1,0:T(8,128)S(1)}, f32[8,768]{1,0:T(8,128)}, u32[]{:S(2)}) copy-start(f32[8,768]{1,0:T(8,128)} %get-tuple-element.60.small) | copy-start | bytes 73732

commit v9 on v8

--- a/solution.py
+++ b/solution.py
@@ -607,8 +607,8 @@
             keep_copy(n - 2).wait()
 
         ref = weights.at[pl.ds(2 * r, 2), wx, wk]
-        for start in range(0, 512, CHUNK):
-            rows = pl.ds(start, CHUNK)
+        for start in range(0, 512, 512):
+            rows = pl.ds(start, 512)
             w = whole(ref)
             projected = dot(h1b[rows, :], w[:, :512])
             gate, up = projected[:, :256], projected[:, 256:]
@@ -1191,15 +1191,15 @@
         (2, 3): [small_step(2)],
         (2, 4): [step(3, 2)],
         (2, 6): [
-            small_step(3), step(1, 4), step(3, 1), step(0, 6), pair(6, 1),
+            small_step(3), step(1, 4), step(3, 1), pair(6, 1),
             pair(7, 1),
         ],
         (3, 1): [step(2, 3), step(3, 3)],
         (3, 2): [small_step(4), step(2, 5)],
-        (3, 4): [step(2, 4), step(1, 6)],
+        (3, 4): [step(2, 4)],
         (3, 6): [
             step(3, 5), step(3, 4), step(4, 0), step(5, 0), step(4, 1),
-            step(4, 2), step(5, 2), step(2, 6), step(3, 6), step(5, 1),
+            step(4, 2), step(5, 2), step(5, 1),
             step(4, 3), step(5, 3), step(4, 5), step(4, 4),
         ],
         (4, 6): [step(6, 0), step(7, 0), step(5, 5), step(5, 4)],
@@ -1313,9 +1313,9 @@
         rows = pl.ds(i * ROWS, ROWS)
         halves(d_rows.at[0], i)[...] = d_h1[rows, :].astype(bf16)
     for n, at in (
-        [(6, -1), (7, -1)]
-        + [(6, 1), (4, 6), (7, 1), (6, 2), (7, 2), (5, 6), (6, 3), (7, 3)]
-        + [(6, 5), (6, 4), (7, 5), (7, 4), (6, 6), (7, 6)]
+        (6, -1), (7, -1), (6, 1), (7, 1), (6, 2), (7, 2), (6, 3), (7, 3),
+        (6, 5), (6, 4), (7, 5), (7, 4), (0, 6), (1, 6), (2, 6), (3, 6),
+        (4, 6), (5, 6), (6, 6), (7, 6),
     ):
         if at < 0:
             rounds[n].pair_sum(0)
@@ -1431,38 +1431,74 @@
 
 
 def finish_kernel(
-    block, grads, small, lo, gt, o_lo, o_gt, o_qkv, o_wout, o_win, o_down_t, o_gains, o_biases, rows, sems
+    block,
+    i_grads,
+    small,
+    lo,
+    gt,
+    o_lo,
+    o_gt,
+    o_qkv,
+    o_wout,
+    o_win,
+    o_down_t,
+    o_gains,
+    o_biases,
+    rows,
+    grads,
+    qkv,
+    wout,
+    win,
+    down_t,
+    sems,
 ):
-    def move(n, src, dst):
-        return pltpu.make_async_copy(src, dst, sems.at[n])
-
-    move(0, lo, rows.at[0]).start()
-    move(1, gt, rows.at[1]).start()
-    turned = []
+    moves = (
+        (i_grads.at[0:2], grads.at[0:2]),
+        (lo, rows.at[0]),
+        (gt, rows.at[1]),
+        (i_grads.at[2:8], grads.at[2:8]),
+        (rows.at[0], o_lo),
+        (rows.at[1], o_gt),
+        (qkv, o_qkv),
+        (wout, o_wout),
+        (win, o_win),
+        (down_t, o_down_t),
+    )
+
+    def move(n):
+        return pltpu.make_async_copy(*moves[n], sems.at[n])
 
     def tile(i):
         return grads[i // 3, :, i % 3 * 128 : i % 3 * 128 + 128]
 
-    for c in range(3):
-        o_qkv[c, :, 0:128] = tile(2 * c)
-        o_qkv[c, :, 128:192] = tile(2 * c + 1)[:, :HEAD_DIM]
-        turned.append(tile(2 * c + 1).T[HEAD_DIM:])
-    o_wout[...] = jnp.concatenate(turned, axis=0)
-    move(0, lo, rows.at[0]).wait()
-    move(2, rows.at[0], o_lo).start()
-    move(1, gt, rows.at[1]).wait()
-    move(3, rows.at[1], o_gt).start()
-    for r in range(3):
-        units = slice(r * 256, (r + 1) * 256)
-        o_win[:, 0, units] = grads[2 + 2 * r, :, 0:256]
-        o_win[:, 1, r * 256 : r * 256 + 128] = grads[2 + 2 * r, :, 256:384]
-        o_win[:, 1, r * 256 + 128 : r * 256 + 256] = grads[3 + 2 * r, :, 0:128]
-        o_down_t[:, units] = grads[3 + 2 * r, :, 128:384]
+    for n in range(4):
+        move(n).start()
     mine = pltpu.roll(small[...], 768 - block[0] * 96, 1)
     o_gains[...] = mine[0:2, 0:96]
     o_biases[...] = mine[2:4, 0:96]
-    move(2, rows.at[0], o_lo).wait()
-    move(3, rows.at[1], o_gt).wait()
+    move(0).wait()
+    turned = []
+    for c in range(3):
+        qkv[c, :, 0:128] = tile(2 * c)
+        qkv[c, :, 128:192] = tile(2 * c + 1)[:, :HEAD_DIM]
+        turned.append(tile(2 * c + 1).T[HEAD_DIM:])
+    wout[...] = jnp.concatenate(turned, axis=0)
+    move(6).start()
+    move(7).start()
+    for n in (1, 2):
+        move(n).wait()
+        move(n + 3).start()
+    move(3).wait()
+    for r in range(3):
+        units = slice(r * 256, (r + 1) * 256)
+        win[:, 0, units] = grads[2 + 2 * r, :, 0:256]
+        win[:, 1, r * 256 : r * 256 + 128] = grads[2 + 2 * r, :, 256:384]
+        win[:, 1, r * 256 + 128 : r * 256 + 256] = grads[3 + 2 * r, :, 0:128]
+        down_t[:, units] = grads[3 + 2 * r, :, 128:384]
+    move(8).start()
+    move(9).start()
+    for n in range(4, 10):
+        move(n).wait()
 
 
 def finish(block, grads, small, lo, gt):
@@ -1482,9 +1518,17 @@
             shape((2, 96), f32),
             shape((2, 96), f32),
         ),
-        in_specs=[pl.BlockSpec(memory_space=pltpu.SMEM), vmem, vmem, any_space, any_space],
-        out_specs=(any_space, any_space) + (vmem,) * 6,
-        scratch_shapes=[pltpu.VMEM((2,) + lo.shape, lo.dtype), pltpu.SemaphoreType.DMA((4,))],
+        in_specs=[pl.BlockSpec(memory_space=pltpu.SMEM), any_space, vmem, any_space, any_space],
+        out_specs=(any_space,) * 6 + (vmem,) * 2,
+        scratch_shapes=[
+            pltpu.VMEM((2,) + lo.shape, lo.dtype),
+            pltpu.VMEM(grads.shape, f32),
+            pltpu.VMEM((3, 96, 192), f32),
+            pltpu.VMEM((192, 96), f32),
+            pltpu.VMEM((96, 2, 768), f32),
+            pltpu.VMEM((96, 768), f32),
+            pltpu.SemaphoreType.DMA((10,)),
+        ],
         compiler_params=pltpu.CompilerParams(vmem_limit_bytes=VMEM_LIMIT),
         name="finish",
     )(block, grads, small, lo, gt)

time: 236 us -> 236 us (level)
  no operation moved by 1% of the time
where the time goes in v9:
time: 236 us
  Pallas kernels  234 us (99%)
    pallas_call x1, Pallas kernels, backward(): pl.pallas_call(partial(backward_kernel, span), out_shape=(jax.ShapeDtypeS...  119 us
    pallas_call x1, Pallas kernels, forward(): pl.pallas_call(partial(forward_refs, span, len(raw)), out_shape=tuple((ja...  111 us

profile of v9, /device:TPU:0, one launch (start us, length us, event | category | flops | bytes accessed | tf_op | source)
XLA Modules:
  0.0 235.6 jit_solution(1096370833069689796)
XLA Ops:
  0.6 111.1 %forward.1 = (bf16[8,2,2,4,2,96,384]{6,5,4,3,2,1,0:T(8,128)(2,1)}, f32[8,768]{1,0:T(8,128)}, bf16[2,256,768]{2,1,0:T(8,128)(2,1)}, bf16[2,256,768]{2,1,0:T(8,128...) custom-call(f32[12]{0:T(128)} %constant.13.clone.refs_0_.slopes, ...), custom_call_target="tpu_custom_call" | custom-call | tf_op jit(solution)/shard_map/forward/pallas_call | solution.py:688
  111.7 118.8 %backward.1 = (bf16[2,256,768]{2,1,0:T(8,128)(2,1)}, bf16[2,256,768]{2,1,0:T(8,128)(2,1)}, f32[8,96,384]{2,1,0:T(8,128)}, f32[8,768]{1,0:T(8,128)}) custom-call(f32[12]{0:T(128)} %constant.13.clone.refs_0_.slopes, bf16[8,2,2,4,2,96,384]{6,5,4,3,2,1,0:T(8,128)(2,1)} %get-tuple-element.40.i_weights, f32[8,768]{1,0:T(8,128)} %get-tuple-element.41.norms, ...), custom_call_target="tpu_custom_call" | custom-call | tf_op jit(solution)/shard_map/backward/pallas_call | solution.py:1351
  230.5 0.0 copy-start
  230.5 4.4 %finish.1 = (bf16[2,256,768]{2,1,0:T(8,128)(2,1)}, bf16[2,256,768]{2,1,0:T(8,128)(2,1)}, f32[3,96,192]{2,1,0:T(8,128)}, f32[192,96]{1,0:T(8,128)}, f32[96,2,768]...) custom-call(s32[1]{0:T(128)} %bitcast.block, f32[8,96,384]{2,1,0:T(8,128)} %get-tuple-element.59.i_grads, ...), custom_call_target="tpu_custom_call" | custom-call | tf_op jit(solution)/shard_map/finish/pallas_call | solution.py:1509
  234.9 0.0 copy-done
  234.9 0.1 slice_reduce_fusion
  235.0 0.5 multiply_sqrt_fusion
Async XLA Ops:
  230.5 4.4 %copy-start = (f32[8,768]{1,0:T(8,128)S(1)}, f32[8,768]{1,0:T(8,128)}, u32[]{:S(2)}) copy-start(f32[8,768]{1,0:T(8,128)} %get-tuple-element.60.small) | copy-start | bytes 73732

commit v10 on v9

--- a/solution.py
+++ b/solution.py
@@ -1191,18 +1191,18 @@
         (2, 3): [small_step(2)],
         (2, 4): [step(3, 2)],
         (2, 6): [
-            small_step(3), step(1, 4), step(3, 1), pair(6, 1),
-            pair(7, 1),
+            small_step(3), step(1, 4), step(3, 1), step(4, 0), step(5, 0),
+            pair(6, 1), pair(7, 1),
         ],
         (3, 1): [step(2, 3), step(3, 3)],
         (3, 2): [small_step(4), step(2, 5)],
-        (3, 4): [step(2, 4)],
+        (3, 4): [step(2, 4), step(4, 2)],
+        (3, 5): [step(4, 1)],
         (3, 6): [
-            step(3, 5), step(3, 4), step(4, 0), step(5, 0), step(4, 1),
-            step(4, 2), step(5, 2), step(5, 1),
-            step(4, 3), step(5, 3), step(4, 5), step(4, 4),
+            step(3, 4), step(5, 2), step(5, 1), step(3, 5), step(4, 3),
+            step(5, 3), step(4, 4), step(4, 5),
         ],
-        (4, 6): [step(6, 0), step(7, 0), step(5, 5), step(5, 4)],
+        (4, 6): [step(6, 0), step(7, 0), step(5, 4), step(5, 5)],
     }
     first = lax.broadcasted_iota(jnp.int32, (768, 128), 1) < HEAD_DIM
 

time: 236 us -> 237 us (level)
  no operation moved by 1% of the time
where the time goes in v10:
time: 237 us; the launch traced here: 236 us
  Pallas kernels  235 us (99%)
    pallas_call x1, Pallas kernels, backward(): pl.pallas_call(partial(backward_kernel, span), out_shape=(jax.ShapeDtypeS...  119 us
    pallas_call x1, Pallas kernels, forward(): pl.pallas_call(partial(forward_refs, span, len(raw)), out_shape=tuple((ja...  111 us

profile of v10, /device:TPU:0, one launch (start us, length us, event | category | flops | bytes accessed | tf_op | source)
XLA Modules:
  0.0 236.2 jit_solution(9991566584987754322)
XLA Ops:
  0.6 111.1 %forward.1 = (bf16[8,2,2,4,2,96,384]{6,5,4,3,2,1,0:T(8,128)(2,1)}, f32[8,768]{1,0:T(8,128)}, bf16[2,256,768]{2,1,0:T(8,128)(2,1)}, bf16[2,256,768]{2,1,0:T(8,128...) custom-call(f32[12]{0:T(128)} %constant.13.clone.refs_0_.slopes, ...), custom_call_target="tpu_custom_call" | custom-call | tf_op jit(solution)/shard_map/forward/pallas_call | solution.py:688
  111.7 119.4 %backward.1 = (bf16[2,256,768]{2,1,0:T(8,128)(2,1)}, bf16[2,256,768]{2,1,0:T(8,128)(2,1)}, f32[8,96,384]{2,1,0:T(8,128)}, f32[8,768]{1,0:T(8,128)}) custom-call(f32[12]{0:T(128)} %constant.13.clone.refs_0_.slopes, bf16[8,2,2,4,2,96,384]{6,5,4,3,2,1,0:T(8,128)(2,1)} %get-tuple-element.40.i_weights, f32[8,768]{1,0:T(8,128)} %get-tuple-element.41.norms, ...), custom_call_target="tpu_custom_call" | custom-call | tf_op jit(solution)/shard_map/backward/pallas_call | solution.py:1351
  231.1 0.0 copy-start
  231.2 4.4 %finish.1 = (bf16[2,256,768]{2,1,0:T(8,128)(2,1)}, bf16[2,256,768]{2,1,0:T(8,128)(2,1)}, f32[3,96,192]{2,1,0:T(8,128)}, f32[192,96]{1,0:T(8,128)}, f32[96,2,768]...) custom-call(s32[1]{0:T(128)} %bitcast.block, f32[8,96,384]{2,1,0:T(8,128)} %get-tuple-element.59.i_grads, ...), custom_call_target="tpu_custom_call" | custom-call | tf_op jit(solution)/shard_map/finish/pallas_call | solution.py:1509
  235.5 0.0 copy-done
  235.5 0.1 slice_reduce_fusion
  235.7 0.5 multiply_sqrt_fusion
Async XLA Ops:
  231.1 4.4 %copy-start = (f32[8,768]{1,0:T(8,128)S(1)}, f32[8,768]{1,0:T(8,128)}, u32[]{:S(2)}) copy-start(f32[8,768]{1,0:T(8,128)} %get-tuple-element.60.small) | copy-start | bytes 73732
